TPU v7x, 512 devices: a whole 4x4x16 slice. The times are simulated.
512 devices in a mesh: grp: 64 (over y, z_hi, x, core), node: 8 (over z_lo).
Axes of the slice: x: 4, y: 4, z: 16 (z_hi: 2, z_lo: 8; z = z_hi * 8 + z_lo), core: 2. Of those that a mesh axis runs over, the one named last changes fastest.
Arguments:
- grad_out: bfloat16 [24576, 2048], P('grp', 'node'), may hold values from -32 to 32
- gate_prob: float32 [24576], P('grp'), may hold values from 0.05 to 1
- hidden: bfloat16 [24576, 7168], P('grp', 'node'), may hold values from -0.19921875 to 0.19921875
- w_down: bfloat16 [2048, 7168], P(None, 'node'), may hold values from -0.0625 to 0.0625
- slot_counts: int32 [64], P('grp'), may hold values from 0 to 384, as said below
Outputs:
- grad_hidden: bfloat16 [24576, 7168], P('grp', 'node')
- grad_weight: bfloat16 [2048, 7168], P('grp', 'node')
Inputs may be any that keep to these rules, and one draw needn't show every extreme that they name: `slot_counts`: each count is a multiple of 128; in every draw some group's count is 384.
All inputs are finite; a program needn't handle non-finite values.
Results may differ from a plain program's by a relative error of at most 0.0057.
Values may be sent and summed in bfloat16 or wider, within the bound.
No kernel may reach another device: no remote copies, remote signals or barrier semaphores. Data moves between devices by JAX's collectives and lax.ppermute only.
A program may use at most 64 MiB of HBM per device.

v0:
```python
import jax
import jax.numpy as jnp
from jax import lax
from jax.sharding import PartitionSpec as P

TILE_ROWS = 128


def hidden_grads(features, w_down, tile_rows, first_tile, tile_count):
    buffer_rows = features.shape[0]
    zeros_out = jnp.zeros((buffer_rows, w_down.shape[1]), jnp.bfloat16)

    def hidden_one_tile(tile_index, result):
        tile_block = lax.dynamic_slice_in_dim(features, tile_index * tile_rows, tile_rows, 0)
        product = jnp.dot(tile_block, w_down, preferred_element_type=jnp.float32).astype(
            jnp.bfloat16
        )
        return lax.dynamic_update_slice_in_dim(result, product, tile_index * tile_rows, 0)

    return lax.fori_loop(first_tile, first_tile + tile_count, hidden_one_tile, zeros_out)


def weight_term(features, hidden_part, tile_rows, tile_count):

    def weight_one_tile(tile_index, running):
        slot_block = lax.dynamic_slice_in_dim(features, tile_index * tile_rows, tile_rows, 0)
        unit_block = lax.dynamic_slice_in_dim(hidden_part, tile_index * tile_rows, tile_rows, 0)
        return running + lax.dot_general(
            slot_block, unit_block, (((0,), (0,)), ((), ())), preferred_element_type=jnp.float32
        )

    start_sum = jnp.zeros((features.shape[1], hidden_part.shape[1]), jnp.float32)
    return lax.fori_loop(0, tile_count, weight_one_tile, start_sum)


def owner_rows(received):
    return jnp.sum(received.astype(jnp.float32), axis=0)


def body(grad_out, gate_prob, hidden, w_down, slot_counts):
    tile_rows = TILE_ROWS
    own_tiles = slot_counts[0] // tile_rows
    scaled = (gate_prob[:, None] * grad_out.astype(jnp.float32)).astype(jnp.bfloat16)
    gathered = lax.all_gather(scaled, "node", axis=1, tiled=True)
    grad_hidden = hidden_grads(gathered, w_down, tile_rows, 0, own_tiles)
    group_count = lax.axis_size("grp")
    model_rows = gathered.shape[1]
    rows_here = model_rows // group_count
    whole_term = weight_term(gathered, hidden, tile_rows, own_tiles).astype(jnp.bfloat16)
    blocks = whole_term.reshape(group_count, rows_here, hidden.shape[1])
    received = lax.all_to_all(blocks, "grp", split_axis=0, concat_axis=0, tiled=True)
    summed = owner_rows(received)
    return (grad_hidden, summed.astype(jnp.bfloat16))


def solution(mesh):
    return jax.shard_map(
        body,
        mesh=mesh,
        in_specs=(P("grp", "node"), P("grp"), P("grp", "node"), P(None, "node"), P("grp")),
        out_specs=(P("grp", "node"), P("grp", "node")),
        check_vma=False,
    )
```

profile of v0, /device:TPU:97, one launch (start us, length us, event | category | flops | bytes accessed | tf_op | source)
XLA Modules:
  0.0 307.5 jit_solution(12469548475492476656)
XLA Ops:
  7.2 0.0 all-gather.2.cloned.1.call-start
  7.2 1.7 multiply_convert_fusion
  8.9 0.0 all-gather.2.cloned.1.call-update
  9.6 61.6 %all-gather.2.cloned.1.call-done = bf16[384,2048]{1,0:T(8,128)(2,1)} async-done(((bf16[384,256]{1,0:T(8,128)(2,1)}), bf16[384,2048]{1,0:T(8,128)(2,1)}) %all-gather.2.cloned.1.call-update) | async-done | bytes 1572880 | tf_op jit(solution)/shard_map/all_gather | solution.py:44
  71.2 0.0 copy-start
  71.2 3.4 %broadcast_in_dim.8 = f32[2048,896]{1,0:T(8,128)} broadcast(f32[]{:T(128)} %constant.38.clone.1), dimensions={} | broadcast | bytes 7340036 | tf_op jit(solution)/shard_map/broadcast_in_dim | solution.py:32
  74.6 0.0 copy-done
  74.6 22.0 %while.21 = (s32[]{:T(128)}, f32[2048,896]{1,0:T(8,128)}, s32[]{:T(128)}, bf16[384,2048]{1,0:T(8,128)(2,1)S(1)}, bf16[384,896]{1,0:T(8,128)(2,1)}, /*index=5*/s32[]{:T(128)}, s32[]{:T(128)}, s32[]{:T(128)}, s32[]{:T(128)}) while((s32[]{:T(128)}, f32[2048,896]{1,0:T(8,128)}, s32[]{:T(128)}, bf16[384,2048]{1,0:T(8,128)(2,1)S(1)}, ...), condition=%wide.region_3.4_spmd, body=%wide.region_2.3_spmd.sunk | while | flops 471597056 | bytes 15434891 | solution.py:33
  74.7 7.3 %convolution_add_fusion.2 = f32[2048,896]{1,0:T(8,128)} fusion(f32[2048,896]{1,0:T(8,128)} %get-tuple-element.181, bf16[384,2048]{1,0:T(8,128)(2,1)S(1)} %get-tuple-element.192, s32[]{:T(128)S(6)} %select_n.17, bf16[384,896]{1,0:T(8,128)(2,1)} %get-tuple-element.193), kind=kOutput, calls=%fused_computation.4.clone.1 | convolution fusion | flops 471597056 | bytes 15434752 | tf_op jit(solution)/shard_map/while/body/dot_general | solution.py:28
  82.0 7.3 %convolution_add_fusion.2 = f32[2048,896]{1,0:T(8,128)} fusion(f32[2048,896]{1,0:T(8,128)} %get-tuple-element.181, bf16[384,2048]{1,0:T(8,128)(2,1)S(1)} %get-tuple-element.192, s32[]{:T(128)S(6)} %select_n.17, bf16[384,896]{1,0:T(8,128)(2,1)} %get-tuple-element.193), kind=kOutput, calls=%fused_computation.4.clone.1 | convolution fusion | flops 471597056 | bytes 15434752 | tf_op jit(solution)/shard_map/while/body/dot_general | solution.py:28
  89.3 7.3 %convolution_add_fusion.2 = f32[2048,896]{1,0:T(8,128)} fusion(f32[2048,896]{1,0:T(8,128)} %get-tuple-element.181, bf16[384,2048]{1,0:T(8,128)(2,1)S(1)} %get-tuple-element.192, s32[]{:T(128)S(6)} %select_n.17, bf16[384,896]{1,0:T(8,128)(2,1)} %get-tuple-element.193), kind=kOutput, calls=%fused_computation.4.clone.1 | convolution fusion | flops 471597056 | bytes 15434752 | tf_op jit(solution)/shard_map/while/body/dot_general | solution.py:28
  96.6 5.4 %convert_element_type.16 = bf16[2048,896]{1,0:T(8,128)(2,1)} convert(f32[2048,896]{1,0:T(8,128)} %get-tuple-element.59) | non-fusion elementwise | flops 1835008 | bytes 11010048 | tf_op jit(solution)/shard_map/convert_element_type | solution.py:49
  102.0 15.4 %all-to-all-start = ((bf16[64,32,896]{2,1,0:T(8,128)(2,1)}), bf16[64,32,896]{2,1,0:T(8,128)(2,1)}, u32[]{:S(2)}, u32[]{:S(2)}) async-start(bf16[64,32,896]{2,1,0:T(8,128)(2,1)} %bitcast.9), calls=%async_computation | async-start | bytes 7340032 | tf_op jit(solution)/shard_map/all_to_all | solution.py:51
  117.4 0.1 broadcast_in_dim.7
  117.5 8.4 %while.20 = (s32[]{:T(128)}, bf16[384,896]{1,0:T(8,128)(2,1)S(1)}, s32[]{:T(128)}, bf16[384,2048]{1,0:T(8,128)(2,1)S(1)}, bf16[2048,896]{1,0:T(8,128)(2,1)}, /*index=5*/s32[]{:T(128)}, s32[]{:T(128)}, s32[]{:T(128)}, s32[]{:T(128)}) while((s32[]{:T(128)}, bf16[384,896]{1,0:T(8,128)(2,1)S(1)}, s32[]{:T(128)}, bf16[384,2048]{1,0:T(8,128)(2,1)S(1)}, ...), condition=%wide.region_1.2_spmd, body=%wide.region_0.1_spmd.sunk | while | flops 469876736 | bytes 4424843 | solution.py:20
  117.5 2.8 fusion.14
  120.3 2.8 fusion.14
  123.1 2.8 fusion.14
  125.9 0.0 copy-start.1
  125.9 171.5 %all-to-all-done = bf16[64,32,896]{2,1,0:T(8,128)(2,1)} async-done(((bf16[64,32,896]{2,1,0:T(8,128)(2,1)}), bf16[64,32,896]{2,1,0:T(8,128)(2,1)}, u32[]{:S(2)}, u32[]{:S(2)}) %all-to-all-start) | async-done | bytes 3670048 | tf_op jit(solution)/shard_map/all_to_all | solution.py:51
  297.4 3.2 %reduce_sum.12 = bf16[32,896]{1,0:T(8,128)(2,1)} reduce(bf16[64,32,896]{2,1,0:T(8,128)(2,1)} %all-to-all-done, bf16[]{:T(256)} %constant.33.clone.1), dimensions={0}, to_apply=%region_4.5 | reduce | flops 1806336 | bytes 3727362 | tf_op jit(solution)/shard_map/reduce_sum | solution.py:37
  300.6 0.0 copy-done.1
Async XLA Ops:
  7.2 64.1 %all-gather.2.cloned.1.call-start = ((), (), s32[]{:S(2)}) async-start(), calls=%async_computation.1 | async-start | bytes 1769472 | tf_op jit(solution)/shard_map/all_gather | solution.py:44
  71.2 3.4 %copy-start = (bf16[384,2048]{1,0:T(8,128)(2,1)S(1)}, bf16[384,2048]{1,0:T(8,128)(2,1)}, u32[]{:S(2)}) copy-start(bf16[384,2048]{1,0:T(8,128)(2,1)} %all-gather.2.cloned.1.call-done) | copy-start | bytes 4718596
  102.0 195.4 %all-to-all-start = ((bf16[64,32,896]{2,1,0:T(8,128)(2,1)}), bf16[64,32,896]{2,1,0:T(8,128)(2,1)}, u32[]{:S(2)}, u32[]{:S(2)}) async-start(bf16[64,32,896]{2,1,0:T(8,128)(2,1)} %bitcast.9), calls=%async_computation | async-start | bytes 7340032 | tf_op jit(solution)/shard_map/all_to_all | solution.py:51
  125.9 174.8 %copy-start.1 = (bf16[384,896]{1,0:T(8,128)(2,1)}, bf16[384,896]{1,0:T(8,128)(2,1)S(1)}, u32[]{:S(2)}) copy-start(bf16[384,896]{1,0:T(8,128)(2,1)S(1)} %get-tuple-element.56) | copy-start | bytes 2064388
Sparse Core Ops, SparseCore 0:
  10.6 60.6 all-gather.1
where the time goes:
time: 307 us
  waiting for transfers between devices  233 us (76%)
  matrix products  30.3 us (10%)
  starting transfers between devices  15.4 us (5%)
  between operations  14.7 us (5%)
  other arithmetic  10.3 us (3%)
  local copies, waits for them, and re-layouts  3.49 us (1%)
    all_to_all x1, waiting for transfers between devices, body(): lax.all_to_all(blocks, 'grp', split_axis=0, concat_axis=0, tiled=True)  172 us
    all_gather x1, waiting for transfers between devices, body(): gathered = lax.all_gather(scaled, 'node', axis=1, tiled=True)  61.6 us
    dot_general x3, matrix products, weight_one_tile(): lax.dot_general(slot_block, unit_block, (((0,), (0,)), ((), ())), preferr...  22 us
    all_to_all x1, starting transfers between devices, body(): lax.all_to_all(blocks, 'grp', split_axis=0, concat_axis=0, tiled=True)  15.4 us
    dot_general x3, matrix products, hidden_one_tile(): jnp.dot(tile_block, w_down, preferred_element_type=jnp.float32)  8.32 us
  transfers between devices with their start and end apart: 2, of which 2 were waited for; matrix products, arithmetic and copies ran while one was open for 3% of the time, Pallas kernels for 0%

commit v1 on v0

v1 whole, which is shorter than its diff:
```python
import jax
import jax.numpy as jnp
from jax import lax
from jax.sharding import Mesh, PartitionSpec as P

GRP = ("y", "zh", "x", "core")
RING = (0, 2, 4, 6, 7, 5, 3, 1)
CW = [(RING[i], RING[(i + 1) % 8]) for i in range(8)]
CCW = [(b, a) for a, b in CW]


def gather_features(shard):
    rows, width = shard.shape
    table = jnp.array(RING, jnp.int32)
    place = jnp.argsort(table)[lax.axis_index("node")]
    pieces = [(shard, 0)]
    forward = backward = shard
    for step in range(1, 4):
        forward = lax.ppermute(forward, "node", CW)
        backward = lax.ppermute(backward, "node", CCW)
        pieces += [(forward, -step), (backward, step)]
    half = rows // 2
    last = jnp.concatenate(
        [lax.ppermute(forward[:half], "node", CW), lax.ppermute(backward[half:], "node", CCW)], 0
    )
    pieces.append((last, 4))
    full = jnp.zeros((rows, 8 * width), shard.dtype)
    for piece, shift in pieces:
        owner = table[(place + shift + 8) % 8]
        full = lax.dynamic_update_slice(full, piece, (0, owner * width))
    return full


def body(grad_out, gate_prob, hidden, w_down, slot_counts):
    rows = grad_out.shape[0]
    live = jnp.arange(rows, dtype=jnp.int32) < slot_counts[0]
    scaled = gate_prob[:, None] * grad_out.astype(jnp.float32)
    scaled = jnp.where(live[:, None], scaled, 0.0).astype(jnp.bfloat16)
    full = gather_features(scaled)
    term = lax.dot_general(
        full, hidden, (((0,), (0,)), ((), ())), preferred_element_type=jnp.float32
    ).astype(jnp.bfloat16)
    grad_hidden = jnp.dot(full, w_down, preferred_element_type=jnp.float32).astype(jnp.bfloat16)

    units = hidden.shape[1]
    core, zh = lax.axis_index("core"), lax.axis_index("zh")
    blocks = term.reshape(4, 2, 4, 2, 32, units)
    mine = lax.dynamic_index_in_dim(blocks, core, 3, keepdims=False)
    other = lax.dynamic_index_in_dim(blocks, 1 - core, 3, keepdims=False)
    got = lax.ppermute(other, "core", [(0, 1), (1, 0)])
    pair = (mine.astype(jnp.float32) + got.astype(jnp.float32)).astype(jnp.bfloat16)
    pair = pair.transpose(0, 2, 1, 3, 4).reshape(16, 64, units)
    swapped = lax.all_to_all(pair, ("y", "x"), 0, 0, tiled=True)
    total = jnp.sum(swapped.astype(jnp.float32), axis=0).reshape(2, 32, units)
    keep = lax.dynamic_index_in_dim(total, zh, 0, keepdims=False)
    send = lax.dynamic_index_in_dim(total, 1 - zh, 0, keepdims=False).astype(jnp.bfloat16)
    far = lax.ppermute(send, "zh", [(0, 1), (1, 0)])
    return grad_hidden, (keep + far.astype(jnp.float32)).astype(jnp.bfloat16)


def solution(mesh):
    fine = Mesh(mesh.devices.reshape(4, 2, 4, 2, 8), GRP + ("node",))
    return jax.shard_map(
        body,
        mesh=fine,
        in_specs=(P(GRP, "node"), P(GRP), P(GRP, "node"), P(None, "node"), P(GRP)),
        out_specs=(P(GRP, "node"), P(GRP, "node")),
        check_vma=False,
    )
```

time: 307 us -> 131 us (0.43)
  the two profiles are of different devices: /device:TPU:97 before, /device:TPU:32 now
where the time goes in v1:
time: 131 us; the launch traced here: 130 us
  waiting for transfers between devices  53 us (40%)
  starting transfers between devices  51.6 us (39%)
  between operations  12 us (9%)
  matrix products  6.96 us (5%)
  local copies, waits for them, and re-layouts  4.08 us (3%)
  other arithmetic  2.86 us (2%)
    all_to_all x1, waiting for transfers between devices, body(): swapped = lax.all_to_all(pair, ('y', 'x'), 0, 0, tiled=True)  28.9 us
    ppermute x3, starting transfers between devices, gather_features(): forward = lax.ppermute(forward, 'node', CW)  15.2 us
    ppermute x1, starting transfers between devices, body(): far = lax.ppermute(send, 'zh', [(0, 1), (1, 0)])  12 us
    ppermute x3, starting transfers between devices, gather_features(): backward = lax.ppermute(backward, 'node', CCW)  9.95 us
    ppermute x3, waiting for transfers between devices, gather_features(): backward = lax.ppermute(backward, 'node', CCW)  9.52 us
    all_to_all x1, starting transfers between devices, body(): swapped = lax.all_to_all(pair, ('y', 'x'), 0, 0, tiled=True)  6.42 us
    ppermute x1, waiting for transfers between devices, gather_features(): lax.ppermute(forward[:half], 'node', CW)  4.79 us
    dot_general x1, matrix products, body(): jnp.dot(full, w_down, preferred_element_type=jnp.float32)  4.7 us
  transfers between devices with their start and end apart: 11, of which 9 were waited for; matrix products, arithmetic and copies ran while one was open for 4% of the time, Pallas kernels for 0%

profile of v1, /device:TPU:32, one launch (start us, length us, event | category | flops | bytes accessed | tf_op | source)
XLA Modules:
  0.0 130.5 jit_solution(12523798492049470437)
XLA Ops:
  0.6 0.0 copy-start
  0.6 0.0 copy-start.3
  0.7 0.0 copy-start.4
  0.7 1.3 %dynamic_slice.41 = s32[1]{0:T(128)} dynamic-slice(s32[8]{0:T(128)} %constant.123, s32[]{:T(128)S(6)} %select_n.105), dynamic_slice_sizes={1} | dynamic-slice | bytes 12 | tf_op jit(solution)/shard_map/dynamic_slice | solution.py:15
  7.3 1.7 %fusion.3 = (s32[1]{0:T(128)}, s32[1]{0:T(128)}, s32[1]{0:T(128)}, s32[1]{0:T(128)}, s32[1]{0:T(128)}, /*index=5*/s32[1]{0:T(128)}, s32[1]{0:T(128)}, s32[1]{0:T(128)}) fusion(s32[8]{0:T(128)} %constant.120.clone, s32[]{:T(128)S(6)} %select_n.128, s32[]{:T(128)S(6)} %select_n.119, s32[]{:T(128)S(6)} %select_n.116, s32[]{:T(128)S(6)} %select_n.113, ...), kind=kLoop, calls=%fused_computation.23 | loop fusion | bytes 96 | tf_op jit(solution)/shard_map/dynamic_slice | solution.py:29
  10.3 0.2 broadcast_in_dim.17
  10.4 0.0 copy-done.3
  10.5 0.0 copy-done.4
  10.5 0.2 constant_dynamic-update-slice_fusion.6
  10.6 7.4 %collective-permute-start = (bf16[384,256]{1,0:T(8,128)(2,1)S(1)}, bf16[384,256]{1,0:T(8,128)(2,1)S(1)}, u32[]{:S(2)}, u32[]{:S(2)}) collective-permute-start(bf16[384,256]{1,0:T(8,128)(2,1)S(1)} %get-tuple-element.5), channel_id=1, source_target_pairs={{0,2},{2,4},{4,6},{6,7},{7,5},{5,3},{3,1},{1,0},{8,10},{10,12},{12... | collective-permute-start | bytes 589832 | tf_op jit(solution)/shard_map/ppermute | solution.py:19
  18.0 1.9 %collective-permute-start.1 = (bf16[384,256]{1,0:T(8,128)(2,1)S(1)}, bf16[384,256]{1,0:T(8,128)(2,1)S(1)}, u32[]{:S(2)}, u32[]{:S(2)}) collective-permute-start(bf16[384,256]{1,0:T(8,128)(2,1)S(1)} %get-tuple-element.5), channel_id=1, source_target_pairs={{2,0},{4,2},{6,4},{7,6},{5,7},{3,5},{1,3},{0,1},{10,8},{12,10},{14... | collective-permute-start | bytes 589832 | tf_op jit(solution)/shard_map/ppermute | solution.py:20
  24.4 1.8 %collective-permute-done = bf16[384,256]{1,0:T(8,128)(2,1)S(1)} collective-permute-done((bf16[384,256]{1,0:T(8,128)(2,1)S(1)}, bf16[384,256]{1,0:T(8,128)(2,1)S(1)}, u32[]{:S(2)}, u32[]{:S(2)}) %collective-permute-start) | collective-permute-done | bytes 196640 | tf_op jit(solution)/shard_map/ppermute | solution.py:19
  26.2 4.4 %collective-permute-start.2 = (bf16[384,256]{1,0:T(8,128)(2,1)S(1)}, bf16[384,256]{1,0:T(8,128)(2,1)S(1)}, u32[]{:S(2)}, u32[]{:S(2)}) collective-permute-start(bf16[384,256]{1,0:T(8,128)(2,1)S(1)} %collective-permute-done), channel_id=1, source_target_pairs={{0,2},{2,4},{4,6},{6,7},{7,5},{5,3},{3,1},{1,0},{8,10},{10,12},{12... | collective-permute-start | bytes 589832 | tf_op jit(solution)/shard_map/ppermute | solution.py:19
  30.6 0.0 collective-permute-done.1
  30.6 2.4 %collective-permute-start.3 = (bf16[384,256]{1,0:T(8,128)(2,1)S(1)}, bf16[384,256]{1,0:T(8,128)(2,1)S(1)}, u32[]{:S(2)}, u32[]{:S(2)}) collective-permute-start(bf16[384,256]{1,0:T(8,128)(2,1)S(1)} %collective-permute-done.1), channel_id=1, source_target_pairs={{2,0},{4,2},{6,4},{7,6},{5,7},{3,5},{1,3},{0,1},{10,8},{12,10},{14... | collective-permute-start | bytes 589832 | tf_op jit(solution)/shard_map/ppermute | solution.py:20
  33.0 1.6 %collective-permute-done.2 = bf16[384,256]{1,0:T(8,128)(2,1)S(1)} collective-permute-done((bf16[384,256]{1,0:T(8,128)(2,1)S(1)}, bf16[384,256]{1,0:T(8,128)(2,1)S(1)}, u32[]{:S(2)}, u32[]{:S(2)}) %collective-permute-start.2) | collective-permute-done | bytes 196640 | tf_op jit(solution)/shard_map/ppermute | solution.py:19
  34.7 3.5 %collective-permute-start.4 = (bf16[384,256]{1,0:T(8,128)(2,1)S(1)}, bf16[384,256]{1,0:T(8,128)(2,1)S(1)}, u32[]{:S(2)}, u32[]{:S(2)}) collective-permute-start(bf16[384,256]{1,0:T(8,128)(2,1)S(1)} %collective-permute-done.2), channel_id=1, source_target_pairs={{0,2},{2,4},{4,6},{6,7},{7,5},{5,3},{3,1},{1,0},{8,10},{10,12},{12... | collective-permute-start | bytes 589832 | tf_op jit(solution)/shard_map/ppermute | solution.py:19
  38.2 1.3 %collective-permute-done.3 = bf16[384,256]{1,0:T(8,128)(2,1)S(1)} collective-permute-done((bf16[384,256]{1,0:T(8,128)(2,1)S(1)}, bf16[384,256]{1,0:T(8,128)(2,1)S(1)}, u32[]{:S(2)}, u32[]{:S(2)}) %collective-permute-start.3) | collective-permute-done | bytes 196640 | tf_op jit(solution)/shard_map/ppermute | solution.py:20
  39.5 5.7 %collective-permute-start.5 = (bf16[384,256]{1,0:T(8,128)(2,1)S(1)}, bf16[384,256]{1,0:T(8,128)(2,1)S(1)}, u32[]{:S(2)}, u32[]{:S(2)}) collective-permute-start(bf16[384,256]{1,0:T(8,128)(2,1)S(1)} %collective-permute-done.3), channel_id=1, source_target_pairs={{2,0},{4,2},{6,4},{7,6},{5,7},{3,5},{1,3},{0,1},{10,8},{12,10},{14... | collective-permute-start | bytes 589832 | tf_op jit(solution)/shard_map/ppermute | solution.py:20
  45.2 8.2 %collective-permute-done.5 = bf16[384,256]{1,0:T(8,128)(2,1)S(1)} collective-permute-done((bf16[384,256]{1,0:T(8,128)(2,1)S(1)}, bf16[384,256]{1,0:T(8,128)(2,1)S(1)}, u32[]{:S(2)}, u32[]{:S(2)}) %collective-permute-start.5) | collective-permute-done | bytes 196640 | tf_op jit(solution)/shard_map/ppermute | solution.py:20
  53.4 3.8 %collective-permute-start.7 = (bf16[192,256]{1,0:T(8,128)(2,1)S(1)}, bf16[192,256]{1,0:T(8,128)(2,1)S(1)}, u32[]{:S(2)}, u32[]{:S(2)}) collective-permute-start(bf16[192,256]{1,0:T(8,128)(2,1)S(1)} %slice.9), channel_id=1, source_target_pairs={{2,0},{4,2},{6,4},{7,6},{5,7},{3,5},{1,3},{0,1},{10,8},{12,10},{14... | collective-permute-start | bytes 294920 | tf_op jit(solution)/shard_map/ppermute | solution.py:24
  57.3 0.0 collective-permute-done.4
  57.3 2.3 %collective-permute-start.6 = (bf16[192,256]{1,0:T(8,128)(2,1)S(1)}, bf16[192,256]{1,0:T(8,128)(2,1)S(1)}, u32[]{:S(2)}, u32[]{:S(2)}) collective-permute-start(bf16[192,256]{1,0:T(8,128)(2,1)S(1)} %slice.8), channel_id=1, source_target_pairs={{0,2},{2,4},{4,6},{6,7},{7,5},{5,3},{3,1},{1,0},{8,10},{10,12},{12... | collective-permute-start | bytes 294920 | tf_op jit(solution)/shard_map/ppermute | solution.py:24
  59.6 0.6 collective-permute-done.7
  60.2 4.8 %collective-permute-done.6 = bf16[192,256]{1,0:T(8,128)(2,1)S(1)} collective-permute-done((bf16[192,256]{1,0:T(8,128)(2,1)S(1)}, bf16[192,256]{1,0:T(8,128)(2,1)S(1)}, u32[]{:S(2)}, u32[]{:S(2)}) %collective-permute-start.6) | collective-permute-done | bytes 98336 | tf_op jit(solution)/shard_map/ppermute | solution.py:24
  65.0 0.0 copy-done
  65.0 0.0 copy-start.1
  65.0 2.3 %convolution_convert_fusion = bf16[2048,896]{1,0:T(8,128)(2,1)S(1)} fusion(bf16[384,2048]{1,0:T(8,128)(2,1)S(1)} %maximum_dynamic-update-slice_fusion, bf16[384,896]{1,0:T(8,128)(2,1)S(1)} %copy-done), kind=kOutput, calls=%fused_computation.3 | convolution fusion | flops 1411121152 | bytes 5931008 | tf_op jit(solution)/shard_map/dot_general | solution.py:40
  67.3 0.0 copy-done.1
  67.3 0.5 constant_dynamic-slice_fusion.1
  67.8 0.2 copy.15
  68.1 1.9 %collective-permute-start.8 = (bf16[4,2,4,32,896]{4,3,1,2,0:T(8,128)(2,1)S(1)}, bf16[4,2,4,32,896]{4,3,1,2,0:T(8,128)(2,1)S(1)}, u32[]{:S(2)}, u32[]{:S(2)}) collective-permute-start(bf16[4,2,4,32,896]{4,3,1,2,0:T(8,128)(2,1)S(1)} %bitcast.43), channel_id=1, source_target_pairs={{0,8},{8,0},{1,9},{9,1},{2,10},{10,2},{3,11},{11,3},{4,12},{12,4},... | collective-permute-start | bytes 5505032 | tf_op jit(solution)/shard_map/ppermute | solution.py:50
  70.0 3.8 %collective-permute-done.8 = bf16[4,2,4,32,896]{4,3,1,2,0:T(8,128)(2,1)S(1)} collective-permute-done((bf16[4,2,4,32,896]{4,3,1,2,0:T(8,128)(2,1)S(1)}, bf16[4,2,4,32,896]{4,3,1,2,0:T(8,128)(2,1)S(1)}, u32[]{:S(2)}, u32[]{:S(2)}) %collective-permute-start.8) | collective-permute-done | bytes 1835040 | tf_op jit(solution)/shard_map/ppermute | solution.py:50
  73.8 1.8 %fusion = bf16[4,2,4,32,896]{4,3,1,2,0:T(8,128)(2,1)} fusion(bf16[4,2,4,32,896]{4,3,1,2,0:T(8,128)(2,1)S(1)} %collective-permute-done.8, bf16[4,2,4,1,32,896]{5,4,3,2,1,0:T(8,128)(2,1)S(1)} %get-tuple-element.6), kind=kLoop, calls=%fused_computation.1 | loop fusion | flops 3670016 | bytes 5505024 | tf_op jit(solution)/shard_map/convert_element_type | solution.py:51
  75.5 6.4 %all-to-all-start = ((bf16[16,64,896]{2,1,0:T(8,128)(2,1)}), bf16[16,64,896]{2,1,0:T(8,128)(2,1)S(1)}, u32[]{:S(2)}, u32[]{:S(2)}) async-start(bf16[16,64,896]{2,1,0:T(8,128)(2,1)} %bitcast.41), calls=%async_computation | async-start | bytes 3670016 | tf_op jit(solution)/shard_map/all_to_all | solution.py:53
  82.0 28.9 %all-to-all-done = bf16[16,64,896]{2,1,0:T(8,128)(2,1)S(1)} async-done(((bf16[16,64,896]{2,1,0:T(8,128)(2,1)}), bf16[16,64,896]{2,1,0:T(8,128)(2,1)S(1)}, u32[]{:S(2)}, u32[]{:S(2)}) %all-to-all-start) | async-done | bytes 1835040 | tf_op jit(solution)/shard_map/all_to_all | solution.py:53
  110.9 0.0 copy-start.2
  110.9 0.2 convert_reduce_fusion
  111.1 12.0 %collective-permute-start.9 = (bf16[32,896]{1,0:T(8,128)(2,1)S(1)}, bf16[32,896]{1,0:T(8,128)(2,1)S(1)}, u32[]{:S(2)}, u32[]{:S(2)}) collective-permute-start(bf16[32,896]{1,0:T(8,128)(2,1)S(1)} %fusion.2), channel_id=1, source_target_pairs={{0,64},{64,0},{1,65},{65,1},{2,66},{66,2},{3,67},{67,3},{4,68},{68... | collective-permute-start | bytes 172040 | tf_op jit(solution)/shard_map/ppermute | solution.py:57
  123.1 0.0 copy-done.2
  123.2 4.7 %convolution_convert_fusion.1 = bf16[384,896]{1,0:T(8,128)(2,1)} fusion(bf16[384,2048]{1,0:T(8,128)(2,1)S(1)} %copy-done.2, bf16[2048,896]{1,0:T(8,128)(2,1)} %param.9), kind=kOutput, calls=%fused_computation.6 | convolution fusion | flops 1409630208 | bytes 5931008 | tf_op jit(solution)/shard_map/dot_general | solution.py:43
  127.9 2.0 %collective-permute-done.9 = bf16[32,896]{1,0:T(8,128)(2,1)S(1)} collective-permute-done((bf16[32,896]{1,0:T(8,128)(2,1)S(1)}, bf16[32,896]{1,0:T(8,128)(2,1)S(1)}, u32[]{:S(2)}, u32[]{:S(2)}) %collective-permute-start.9) | collective-permute-done | bytes 57376 | tf_op jit(solution)/shard_map/ppermute | solution.py:57
  129.8 0.6 fusion.1
  (11 shorter events, 0.2 us)
Async XLA Ops:
  0.6 64.4 %copy-start = (bf16[384,896]{1,0:T(8,128)(2,1)S(1)}, bf16[384,896]{1,0:T(8,128)(2,1)}, u32[]{:S(2)}) copy-start(bf16[384,896]{1,0:T(8,128)(2,1)} %param.8) | copy-start | bytes 2064388
  0.6 9.8 %copy-start.3 = (bf16[384,256]{1,0:T(8,128)(2,1)S(1)}, bf16[384,256]{1,0:T(8,128)(2,1)}, u32[]{:S(2)}) copy-start(bf16[384,256]{1,0:T(8,128)(2,1)} %param.6) | copy-start | bytes 589828
  0.7 9.8 %copy-start.4 = (f32[384]{0:T(512)S(1)}, f32[384]{0:T(512)}, u32[]{:S(2)}) copy-start(f32[384]{0:T(512)} %param.7) | copy-start | bytes 4612
  10.6 15.6 %collective-permute-start = (bf16[384,256]{1,0:T(8,128)(2,1)S(1)}, bf16[384,256]{1,0:T(8,128)(2,1)S(1)}, u32[]{:S(2)}, u32[]{:S(2)}) collective-permute-start(bf16[384,256]{1,0:T(8,128)(2,1)S(1)} %get-tuple-element.5), channel_id=1, source_target_pairs={{0,2},{2,4},{4,6},{6,7},{7,5},{5,3},{3,1},{1,0},{8,10},{10,12},{12... | collective-permute-start | bytes 589832 | tf_op jit(solution)/shard_map/ppermute | solution.py:19
  18.0 12.6 %collective-permute-start.1 = (bf16[384,256]{1,0:T(8,128)(2,1)S(1)}, bf16[384,256]{1,0:T(8,128)(2,1)S(1)}, u32[]{:S(2)}, u32[]{:S(2)}) collective-permute-start(bf16[384,256]{1,0:T(8,128)(2,1)S(1)} %get-tuple-element.5), channel_id=1, source_target_pairs={{2,0},{4,2},{6,4},{7,6},{5,7},{3,5},{1,3},{0,1},{10,8},{12,10},{14... | collective-permute-start | bytes 589832 | tf_op jit(solution)/shard_map/ppermute | solution.py:20
  26.2 8.5 %collective-permute-start.2 = (bf16[384,256]{1,0:T(8,128)(2,1)S(1)}, bf16[384,256]{1,0:T(8,128)(2,1)S(1)}, u32[]{:S(2)}, u32[]{:S(2)}) collective-permute-start(bf16[384,256]{1,0:T(8,128)(2,1)S(1)} %collective-permute-done), channel_id=1, source_target_pairs={{0,2},{2,4},{4,6},{6,7},{7,5},{5,3},{3,1},{1,0},{8,10},{10,12},{12... | collective-permute-start | bytes 589832 | tf_op jit(solution)/shard_map/ppermute | solution.py:19
  30.6 8.9 %collective-permute-start.3 = (bf16[384,256]{1,0:T(8,128)(2,1)S(1)}, bf16[384,256]{1,0:T(8,128)(2,1)S(1)}, u32[]{:S(2)}, u32[]{:S(2)}) collective-permute-start(bf16[384,256]{1,0:T(8,128)(2,1)S(1)} %collective-permute-done.1), channel_id=1, source_target_pairs={{2,0},{4,2},{6,4},{7,6},{5,7},{3,5},{1,3},{0,1},{10,8},{12,10},{14... | collective-permute-start | bytes 589832 | tf_op jit(solution)/shard_map/ppermute | solution.py:20
  34.7 22.6 %collective-permute-start.4 = (bf16[384,256]{1,0:T(8,128)(2,1)S(1)}, bf16[384,256]{1,0:T(8,128)(2,1)S(1)}, u32[]{:S(2)}, u32[]{:S(2)}) collective-permute-start(bf16[384,256]{1,0:T(8,128)(2,1)S(1)} %collective-permute-done.2), channel_id=1, source_target_pairs={{0,2},{2,4},{4,6},{6,7},{7,5},{5,3},{3,1},{1,0},{8,10},{10,12},{12... | collective-permute-start | bytes 589832 | tf_op jit(solution)/shard_map/ppermute | solution.py:19
  39.5 13.9 %collective-permute-start.5 = (bf16[384,256]{1,0:T(8,128)(2,1)S(1)}, bf16[384,256]{1,0:T(8,128)(2,1)S(1)}, u32[]{:S(2)}, u32[]{:S(2)}) collective-permute-start(bf16[384,256]{1,0:T(8,128)(2,1)S(1)} %collective-permute-done.3), channel_id=1, source_target_pairs={{2,0},{4,2},{6,4},{7,6},{5,7},{3,5},{1,3},{0,1},{10,8},{12,10},{14... | collective-permute-start | bytes 589832 | tf_op jit(solution)/shard_map/ppermute | solution.py:20
  53.4 6.8 %collective-permute-start.7 = (bf16[192,256]{1,0:T(8,128)(2,1)S(1)}, bf16[192,256]{1,0:T(8,128)(2,1)S(1)}, u32[]{:S(2)}, u32[]{:S(2)}) collective-permute-start(bf16[192,256]{1,0:T(8,128)(2,1)S(1)} %slice.9), channel_id=1, source_target_pairs={{2,0},{4,2},{6,4},{7,6},{5,7},{3,5},{1,3},{0,1},{10,8},{12,10},{14... | collective-permute-start | bytes 294920 | tf_op jit(solution)/shard_map/ppermute | solution.py:24
  57.3 7.7 %collective-permute-start.6 = (bf16[192,256]{1,0:T(8,128)(2,1)S(1)}, bf16[192,256]{1,0:T(8,128)(2,1)S(1)}, u32[]{:S(2)}, u32[]{:S(2)}) collective-permute-start(bf16[192,256]{1,0:T(8,128)(2,1)S(1)} %slice.8), channel_id=1, source_target_pairs={{0,2},{2,4},{4,6},{6,7},{7,5},{5,3},{3,1},{1,0},{8,10},{10,12},{12... | collective-permute-start | bytes 294920 | tf_op jit(solution)/shard_map/ppermute | solution.py:24
  65.0 2.3 %copy-start.1 = (bf16[384,2048]{1,0:T(8,128)(2,1)}, bf16[384,2048]{1,0:T(8,128)(2,1)S(1)}, u32[]{:S(2)}) copy-start(bf16[384,2048]{1,0:T(8,128)(2,1)S(1)} %maximum_dynamic-update-slice_fusion) | copy-start | bytes 4718596
  68.1 5.7 %collective-permute-start.8 = (bf16[4,2,4,32,896]{4,3,1,2,0:T(8,128)(2,1)S(1)}, bf16[4,2,4,32,896]{4,3,1,2,0:T(8,128)(2,1)S(1)}, u32[]{:S(2)}, u32[]{:S(2)}) collective-permute-start(bf16[4,2,4,32,896]{4,3,1,2,0:T(8,128)(2,1)S(1)} %bitcast.43), channel_id=1, source_target_pairs={{0,8},{8,0},{1,9},{9,1},{2,10},{10,2},{3,11},{11,3},{4,12},{12,4},... | collective-permute-start | bytes 5505032 | tf_op jit(solution)/shard_map/ppermute | solution.py:50
  75.5 35.3 %all-to-all-start = ((bf16[16,64,896]{2,1,0:T(8,128)(2,1)}), bf16[16,64,896]{2,1,0:T(8,128)(2,1)S(1)}, u32[]{:S(2)}, u32[]{:S(2)}) async-start(bf16[16,64,896]{2,1,0:T(8,128)(2,1)} %bitcast.41), calls=%async_computation | async-start | bytes 3670016 | tf_op jit(solution)/shard_map/all_to_all | solution.py:53
  110.9 12.3 %copy-start.2 = (bf16[384,2048]{1,0:T(8,128)(2,1)S(1)}, bf16[384,2048]{1,0:T(8,128)(2,1)}, u32[]{:S(2)}) copy-start(bf16[384,2048]{1,0:T(8,128)(2,1)} %copy-done.1) | copy-start | bytes 4718596
  111.1 18.7 %collective-permute-start.9 = (bf16[32,896]{1,0:T(8,128)(2,1)S(1)}, bf16[32,896]{1,0:T(8,128)(2,1)S(1)}, u32[]{:S(2)}, u32[]{:S(2)}) collective-permute-start(bf16[32,896]{1,0:T(8,128)(2,1)S(1)} %fusion.2), channel_id=1, source_target_pairs={{0,64},{64,0},{1,65},{65,1},{2,66},{66,2},{3,67},{67,3},{4,68},{68... | collective-permute-start | bytes 172040 | tf_op jit(solution)/shard_map/ppermute | solution.py:57

commit v2 on v1

v2 whole, which is shorter than its diff:
```python
import functools

import jax
import jax.numpy as jnp
import numpy as np
from jax import lax
from jax.experimental import pallas as pl
from jax.experimental.pallas import tpu as pltpu
from jax.sharding import Mesh, PartitionSpec as P


GRP = ("y", "zh", "x", "core")
RING = (0, 2, 4, 6, 7, 5, 3, 1)
CW = [(RING[i], RING[(i + 1) % 8]) for i in range(8)]
CCW = [(b, a) for a, b in CW]
SHIFTS = (0, -1, 1, -2, 2, -3, 3, 4)
ORDER = np.array(
    [[RING[(RING.index(n) + s) % 8] for s in SHIFTS] for n in range(8)], np.int32
)
FIRST = 5


def hidden_kernel(order_ref, pieces_ref, w_ref, out_ref, total_ref):
    step = pl.program_id(0)
    part = jnp.dot(pieces_ref[...], w_ref[...], preferred_element_type=jnp.float32)

    @pl.when(step == 0)
    def _():
        total_ref[...] = part

    @pl.when(step > 0)
    def _():
        total_ref[...] += part

    @pl.when(step == pl.num_programs(0) - 1)
    def _():
        out_ref[...] = total_ref[...].astype(out_ref.dtype)


def hidden_grads(order, pieces, w_down):
    rows, model = pieces.shape
    width, units = model // 8, w_down.shape[1]
    return pl.pallas_call(
        hidden_kernel,
        grid_spec=pltpu.PrefetchScalarGridSpec(
            num_scalar_prefetch=1,
            grid=(8,),
            in_specs=[
                pl.BlockSpec((rows, width), lambda k, order_ref: (0, k)),
                pl.BlockSpec((width, units), lambda k, order_ref: (order_ref[k], 0)),
            ],
            out_specs=pl.BlockSpec((rows, units), lambda k, order_ref: (0, 0)),
            scratch_shapes=[pltpu.VMEM((rows, units), jnp.float32)],
        ),
        out_shape=jax.ShapeDtypeStruct((rows, units), jnp.bfloat16),
        cost_estimate=pl.CostEstimate(
            flops=2 * rows * model * units, bytes_accessed=8_000_000, transcendentals=0
        ),
        compiler_params=pltpu.CompilerParams(vmem_limit_bytes=20 << 20),
        name="hidden_grads",
    )(order, pieces, w_down)


def term_kernel(count, core_ref, mine_ref, theirs_ref, hid_ref, hid_theirs_ref, out_ref, left_ref):
    rows = mine_ref.shape[0]
    line = lax.broadcasted_iota(jnp.int32, (128, 256), 0)
    column = lax.broadcasted_iota(jnp.int32, (128, 256), 1)
    wanted = (
        lax.rem(lax.div(line, 8), 4) * 64
        + core_ref[0] * 32
        + lax.div(line, 32) * 8
        + lax.rem(line, 8)
    )
    pick = jnp.where(column == wanted, 1.0, 0.0).astype(jnp.bfloat16)
    for k in range(count):
        for side, ref in ((0, mine_ref), (1, theirs_ref)):
            turned = lax.dot_general(
                pick,
                ref[:, k * 256 : (k + 1) * 256],
                (((1,), (1,)), ((), ())),
                preferred_element_type=jnp.float32,
            )
            for d in range(16):
                left_ref[
                    d * count * 8 + k * 8 : d * count * 8 + k * 8 + 8,
                    side * rows : (side + 1) * rows,
                ] = turned[d * 8 : d * 8 + 8]
    left = left_ref[...].astype(jnp.bfloat16)
    units = out_ref.shape[1]
    for low in range(0, units, 256):
        high = min(low + 256, units)
        product = jnp.dot(
            left[:, :rows], hid_ref[:, low:high], preferred_element_type=jnp.float32
        ) + jnp.dot(
            left[:, rows:], hid_theirs_ref[:, low:high], preferred_element_type=jnp.float32
        )
        out_ref[:, low:high] = product.astype(out_ref.dtype)


def weight_term(core, mine, theirs, hidden, hidden_theirs):
    rows, units = hidden.shape
    count = mine.shape[1] // 256
    vmem = pl.BlockSpec(memory_space=pltpu.VMEM)
    return pl.pallas_call(
        functools.partial(term_kernel, count),
        in_specs=[pl.BlockSpec(memory_space=pltpu.SMEM)] + [vmem] * 4,
        out_specs=vmem,
        out_shape=jax.ShapeDtypeStruct((count * 128, units), jnp.bfloat16),
        scratch_shapes=[pltpu.VMEM((count * 128, 2 * rows), jnp.float32)],
        cost_estimate=pl.CostEstimate(
            flops=count * 128 * 4 * rows * units,
            bytes_accessed=2 * (2 * rows * (count * 256 + units) + count * 128 * units),
            transcendentals=0,
        ),
        compiler_params=pltpu.CompilerParams(vmem_limit_bytes=20 << 20),
        name="weight_term",
    )(core, mine, theirs, hidden, hidden_theirs)


def sum_kernel(order_ref, first_ref, second_ref, out_ref):
    at = 0
    for ref in (first_ref, second_ref):
        total = ref[0].astype(jnp.float32)
        for d in range(1, 16):
            total += ref[d].astype(jnp.float32)
        for k in range(ref.shape[1] // 8):
            out_ref[order_ref[at]] = total[k * 8 : k * 8 + 8].astype(out_ref.dtype)
            at += 1


def plane_sums(order, first, second):
    units = first.shape[2]
    vmem = pl.BlockSpec(memory_space=pltpu.VMEM)
    return pl.pallas_call(
        sum_kernel,
        in_specs=[pl.BlockSpec(memory_space=pltpu.SMEM), vmem, vmem],
        out_specs=vmem,
        out_shape=jax.ShapeDtypeStruct((8, 8, units), jnp.bfloat16),
        cost_estimate=pl.CostEstimate(
            flops=16 * 64 * units, bytes_accessed=2 * 17 * 64 * units, transcendentals=0
        ),
        compiler_params=pltpu.CompilerParams(vmem_limit_bytes=20 << 20),
        name="plane_sums",
    )(order, first, second)


def body(grad_out, gate_prob, hidden, w_down, slot_counts):
    rows, units = hidden.shape
    order = lax.dynamic_index_in_dim(
        jnp.asarray(ORDER), lax.axis_index("node"), 0, keepdims=False
    )
    core = lax.axis_index("core").reshape(1)
    live = jnp.arange(rows, dtype=jnp.int32) < slot_counts[0]
    scaled = gate_prob[:, None] * grad_out.astype(jnp.float32)
    scaled = jnp.where(live[:, None], scaled, 0.0).astype(jnp.bfloat16)

    def swap(value):
        return lax.ppermute(value, "core", [(0, 1), (1, 0)])

    def scatter(term):
        pieces = term.reshape(16, term.shape[0] // 16, units)
        return lax.all_to_all(pieces, ("y", "x"), 0, 0, tiled=True)

    pieces = [scaled]
    forward = backward = scaled
    for _ in range(1, 4):
        forward = lax.ppermute(forward, "node", CW)
        backward = lax.ppermute(backward, "node", CCW)
        pieces += [forward, backward]
    pieces.append(lax.ppermute(forward, "node", CW))

    hidden_theirs = swap(hidden)
    one = jnp.concatenate(pieces[:FIRST], axis=1)
    one_theirs = swap(one)
    term_one = weight_term(core, one, one_theirs, hidden, hidden_theirs)
    first = scatter(term_one)
    two = jnp.concatenate(pieces[FIRST:], axis=1)
    two_theirs = swap(two)
    term_two = weight_term(core, two, two_theirs, hidden, hidden_theirs)
    second = scatter(term_two)
    sums = plane_sums(order, first, second)
    grad_hidden = hidden_grads(order, jnp.concatenate([one, two], axis=1), w_down)
    halves = lax.all_to_all(sums, ("y", "zh"), 0, 0, tiled=True)
    halves = halves.reshape(4, 2, 8, units)
    grad_weight = halves[:, 0].astype(jnp.float32) + halves[:, 1].astype(jnp.float32)
    return grad_hidden, grad_weight.reshape(32, units).astype(jnp.bfloat16)


def solution(mesh):
    fine = Mesh(mesh.devices.reshape(4, 2, 4, 2, 8), GRP + ("node",))
    return jax.shard_map(
        body,
        mesh=fine,
        in_specs=(P(GRP, "node"), P(GRP), P(GRP, "node"), P(None, "node"), P(GRP)),
        out_specs=(P(GRP, "node"), P(GRP, "node")),
        check_vma=False,
    )
```

time: 131 us -> 134 us (1.023)
  Pallas kernels: 0 us -> 14.7 us
  starting transfers between devices: 51.6 us -> 62.3 us
  between operations: 12 us -> 1.53 us
  matrix products: 6.96 us -> 0 us
  waiting for transfers between devices: 53 us -> 47.7 us
  local copies, waits for them, and re-layouts: 4.08 us -> 5.54 us
    all_to_all x1 -> x3, starting transfers between devices: 6.42 us -> 24.4 us  [the longest x2 12.3 us: scatter(): return lax.all_to_all(pieces, ('y', 'x'), 0, 0, tiled=True)]
    pallas_call x0 -> x4, Pallas kernels: none -> 14.7 us  [the longest x2 7.53 us: weight_term(): pl.pallas_call(functools.partial(term_kernel, count), in_specs=[pl.BlockS...]
    ppermute x10, waiting for transfers between devices: 24.1 us -> 14.1 us  [the longest x3 6.5 us: body(): forward = lax.ppermute(forward, 'node', CW)]
    ppermute x10, starting transfers between devices: 45.2 us -> 38 us  [the longest x3 15.8 us: body(): forward = lax.ppermute(forward, 'node', CW)]
    dot_general x2 -> x0, matrix products: 6.96 us -> none  [the longest x1 4.7 us: body(): jnp.dot(full, w_down, preferred_element_type=jnp.float32)]
    unnamed x10 -> x14, local copies, waits for them, and re-layouts: 0.03 us -> 4.78 us
    all_to_all x1 -> x3, waiting for transfers between devices: 28.9 us -> 33.6 us  [the longest x2 26.1 us: scatter(): return lax.all_to_all(pieces, ('y', 'x'), 0, 0, tiled=True)]
    dynamic_slice x4 -> x0, local copies, waits for them, and re-layouts: 3.73 us -> none  [the longest x1 1.65 us: gather_features(): owner = table[(place + shift + 8) % 8]]
  transfers between devices with their start and end apart: 11 -> 13, of which waited for: 9 -> 9; matrix products, arithmetic and copies ran while one was open for 4% -> 1% of each run, Pallas kernels for 0% -> 10%
where the time goes in v2:
time: 134 us
  starting transfers between devices  62.3 us (46%)
  waiting for transfers between devices  47.7 us (36%)
  Pallas kernels  14.7 us (11%)
  local copies, waits for them, and re-layouts  5.54 us (4%)
  other arithmetic  1.74 us (1%)
  between operations  1.53 us (1%)
    all_to_all x2, waiting for transfers between devices, scatter(): return lax.all_to_all(pieces, ('y', 'x'), 0, 0, tiled=True)  26.1 us
    ppermute x3, starting transfers between devices, body(): forward = lax.ppermute(forward, 'node', CW)  15.8 us
    all_to_all x2, starting transfers between devices, scatter(): return lax.all_to_all(pieces, ('y', 'x'), 0, 0, tiled=True)  12.3 us
    all_to_all x1, starting transfers between devices, body(): halves = lax.all_to_all(sums, ('y', 'zh'), 0, 0, tiled=True)  12.1 us
    ppermute x3, starting transfers between devices, body(): backward = lax.ppermute(backward, 'node', CCW)  9.95 us
    pallas_call x2, Pallas kernels, weight_term(): pl.pallas_call(functools.partial(term_kernel, count), in_specs=[pl.BlockS...  7.53 us
    all_to_all x1, waiting for transfers between devices, body(): halves = lax.all_to_all(sums, ('y', 'zh'), 0, 0, tiled=True)  7.53 us
    ppermute x3, waiting for transfers between devices, body(): forward = lax.ppermute(forward, 'node', CW)  6.5 us
  transfers between devices with their start and end apart: 13, of which 9 were waited for; matrix products, arithmetic and copies ran while one was open for 1% of the time, Pallas kernels for 10%

profile of v2, /device:TPU:32, one launch (start us, length us, event | category | flops | bytes accessed | tf_op | source)
XLA Modules:
  0.0 133.6 jit_solution(3755258465665252539)
XLA Ops:
  1.3 1.1 constant_dynamic-update-slice_fusion.12
  2.4 7.4 %collective-permute-start = (bf16[384,256]{1,0:T(8,128)(2,1)S(1)}, bf16[384,256]{1,0:T(8,128)(2,1)S(1)}, u32[]{:S(2)}, u32[]{:S(2)}) collective-permute-start(bf16[384,256]{1,0:T(8,128)(2,1)S(1)} %get-tuple-element.3), channel_id=1, source_target_pairs={{0,2},{2,4},{4,6},{6,7},{7,5},{5,3},{3,1},{1,0},{8,10},{10,12},{12... | collective-permute-start | bytes 589832 | tf_op jit(solution)/shard_map/ppermute | solution.py:167
  9.8 1.9 %collective-permute-start.1 = (bf16[384,256]{1,0:T(8,128)(2,1)S(1)}, bf16[384,256]{1,0:T(8,128)(2,1)S(1)}, u32[]{:S(2)}, u32[]{:S(2)}) collective-permute-start(bf16[384,256]{1,0:T(8,128)(2,1)S(1)} %get-tuple-element.3), channel_id=1, source_target_pairs={{2,0},{4,2},{6,4},{7,6},{5,7},{3,5},{1,3},{0,1},{10,8},{12,10},{14... | collective-permute-start | bytes 589832 | tf_op jit(solution)/shard_map/ppermute | solution.py:168
  11.7 1.9 %collective-permute-start.8 = (bf16[384,896]{1,0:T(8,128)(2,1)}, bf16[384,896]{1,0:T(8,128)(2,1)S(1)}, u32[]{:S(2)}, u32[]{:S(2)}) collective-permute-start(bf16[384,896]{1,0:T(8,128)(2,1)} %hid_ref.3), channel_id=1, source_target_pairs={{0,8},{8,0},{1,9},{9,1},{2,10},{10,2},{3,11},{11,3},{4,12},{12,4},... | collective-permute-start | bytes 2064392 | tf_op jit(solution)/shard_map/ppermute | solution.py:158
  13.6 3.5 %collective-permute-done = bf16[384,256]{1,0:T(8,128)(2,1)S(1)} collective-permute-done((bf16[384,256]{1,0:T(8,128)(2,1)S(1)}, bf16[384,256]{1,0:T(8,128)(2,1)S(1)}, u32[]{:S(2)}, u32[]{:S(2)}) %collective-permute-start) | collective-permute-done | bytes 196640 | tf_op jit(solution)/shard_map/ppermute | solution.py:167
  17.1 4.4 %collective-permute-start.2 = (bf16[384,256]{1,0:T(8,128)(2,1)S(1)}, bf16[384,256]{1,0:T(8,128)(2,1)S(1)}, u32[]{:S(2)}, u32[]{:S(2)}) collective-permute-start(bf16[384,256]{1,0:T(8,128)(2,1)S(1)} %collective-permute-done), channel_id=1, source_target_pairs={{0,2},{2,4},{4,6},{6,7},{7,5},{5,3},{3,1},{1,0},{8,10},{10,12},{12... | collective-permute-start | bytes 589832 | tf_op jit(solution)/shard_map/ppermute | solution.py:167
  21.5 0.0 collective-permute-done.1
  21.5 2.4 %collective-permute-start.3 = (bf16[384,256]{1,0:T(8,128)(2,1)S(1)}, bf16[384,256]{1,0:T(8,128)(2,1)S(1)}, u32[]{:S(2)}, u32[]{:S(2)}) collective-permute-start(bf16[384,256]{1,0:T(8,128)(2,1)S(1)} %collective-permute-done.1), channel_id=1, source_target_pairs={{2,0},{4,2},{6,4},{7,6},{5,7},{3,5},{1,3},{0,1},{10,8},{12,10},{14... | collective-permute-start | bytes 589832 | tf_op jit(solution)/shard_map/ppermute | solution.py:168
  24.0 0.0 copy-start.1
  24.0 1.6 %collective-permute-done.2 = bf16[384,256]{1,0:T(8,128)(2,1)S(1)} collective-permute-done((bf16[384,256]{1,0:T(8,128)(2,1)S(1)}, bf16[384,256]{1,0:T(8,128)(2,1)S(1)}, u32[]{:S(2)}, u32[]{:S(2)}) %collective-permute-start.2) | collective-permute-done | bytes 196640 | tf_op jit(solution)/shard_map/ppermute | solution.py:167
  25.6 4.1 %collective-permute-start.4 = (bf16[384,256]{1,0:T(8,128)(2,1)S(1)}, bf16[384,256]{1,0:T(8,128)(2,1)S(1)}, u32[]{:S(2)}, u32[]{:S(2)}) collective-permute-start(bf16[384,256]{1,0:T(8,128)(2,1)S(1)} %collective-permute-done.2), channel_id=1, source_target_pairs={{0,2},{2,4},{4,6},{6,7},{7,5},{5,3},{3,1},{1,0},{8,10},{10,12},{12... | collective-permute-start | bytes 589832 | tf_op jit(solution)/shard_map/ppermute | solution.py:167
  29.7 1.6 %collective-permute-done.3 = bf16[384,256]{1,0:T(8,128)(2,1)S(1)} collective-permute-done((bf16[384,256]{1,0:T(8,128)(2,1)S(1)}, bf16[384,256]{1,0:T(8,128)(2,1)S(1)}, u32[]{:S(2)}, u32[]{:S(2)}) %collective-permute-start.3) | collective-permute-done | bytes 196640 | tf_op jit(solution)/shard_map/ppermute | solution.py:168
  31.2 5.7 %collective-permute-start.5 = (bf16[384,256]{1,0:T(8,128)(2,1)S(1)}, bf16[384,256]{1,0:T(8,128)(2,1)S(1)}, u32[]{:S(2)}, u32[]{:S(2)}) collective-permute-start(bf16[384,256]{1,0:T(8,128)(2,1)S(1)} %collective-permute-done.3), channel_id=1, source_target_pairs={{2,0},{4,2},{6,4},{7,6},{5,7},{3,5},{1,3},{0,1},{10,8},{12,10},{14... | collective-permute-start | bytes 589832 | tf_op jit(solution)/shard_map/ppermute | solution.py:168
  37.0 1.4 %collective-permute-done.4 = bf16[384,256]{1,0:T(8,128)(2,1)S(1)} collective-permute-done((bf16[384,256]{1,0:T(8,128)(2,1)S(1)}, bf16[384,256]{1,0:T(8,128)(2,1)S(1)}, u32[]{:S(2)}, u32[]{:S(2)}) %collective-permute-start.4) | collective-permute-done | bytes 196640 | tf_op jit(solution)/shard_map/ppermute | solution.py:167
  38.4 6.0 %collective-permute-start.6 = (bf16[384,256]{1,0:T(8,128)(2,1)S(1)}, bf16[384,256]{1,0:T(8,128)(2,1)S(1)}, u32[]{:S(2)}, u32[]{:S(2)}) collective-permute-start(bf16[384,256]{1,0:T(8,128)(2,1)S(1)} %collective-permute-done.4), channel_id=1, source_target_pairs={{0,2},{2,4},{4,6},{6,7},{7,5},{5,3},{3,1},{1,0},{8,10},{10,12},{12... | collective-permute-start | bytes 589832 | tf_op jit(solution)/shard_map/ppermute | solution.py:170
  44.4 0.8 collective-permute-done.5
  45.2 5.3 %collective-permute-done.6 = bf16[384,256]{1,0:T(8,128)(2,1)S(1)} collective-permute-done((bf16[384,256]{1,0:T(8,128)(2,1)S(1)}, bf16[384,256]{1,0:T(8,128)(2,1)S(1)}, u32[]{:S(2)}, u32[]{:S(2)}) %collective-permute-start.6) | collective-permute-done | bytes 196640 | tf_op jit(solution)/shard_map/ppermute | solution.py:170
  50.5 0.0 copy-start.2
  50.5 1.2 copy-done.2
  51.7 1.9 %collective-permute-start.9 = (bf16[384,768]{1,0:T(8,128)(2,1)S(1)}, bf16[384,768]{1,0:T(8,128)(2,1)}, u32[]{:S(2)}, u32[]{:S(2)}) collective-permute-start(bf16[384,768]{1,0:T(8,128)(2,1)S(1)} %get-tuple-element.4.mine_ref), channel_id=1, source_target_pairs={{0,8},{8,0},{1,9},{9,1},{2,10},{10,2},{3,11},{11,3},{4,12},{12,4},... | collective-permute-start | bytes 1769480 | tf_op jit(solution)/shard_map/ppermute | solution.py:158
  53.6 2.4 %collective-permute-start.7 = (bf16[384,1280]{1,0:T(8,128)(2,1)S(1)}, bf16[384,1280]{1,0:T(8,128)(2,1)}, u32[]{:S(2)}, u32[]{:S(2)}) collective-permute-start(bf16[384,1280]{1,0:T(8,128)(2,1)S(1)} %get-tuple-element.10.mine_ref), channel_id=1, source_target_pairs={{0,8},{8,0},{1,9},{9,1},{2,10},{10,2},{3,11},{11,3},{4,12},{12,4},... | collective-permute-start | bytes 2949128 | tf_op jit(solution)/shard_map/ppermute | solution.py:158
  56.1 0.0 collective-permute-done.8.hid_theirs_ref
  56.1 0.0 collective-permute-done.9.theirs_ref
  56.1 0.0 copy-done.1
  56.1 3.3 %weight_term.3 = bf16[384,896]{1,0:T(8,128)(2,1)} custom-call(s32[1]{0:T(128)} %bitcast.2.core_ref, bf16[384,768]{1,0:T(8,128)(2,1)S(1)} %get-tuple-element.4.mine_ref, bf16[384,768]{1,0:T(8,128)(2,1)} %collective-permute-done.9.theirs_ref, bf16[384,896]{1,0:T(8,128)(2,1)S(1)} %copy-done.1, bf16[384,896]{1,0:T(8,128)(2,1)S(1)} %collective-permute-done.8.hid_theirs_ref), custom_call_target="tpu_custom_call" | custom-call | flops 528482304 | bytes 3244032 | tf_op jit(solution)/shard_map/weight_term/pallas_call | solution.py:104
  59.3 8.6 %all-to-all-start.1 = ((bf16[16,24,896]{2,1,0:T(8,128)(2,1)}), bf16[16,24,896]{2,1,0:T(8,128)(2,1)S(1)}, u32[]{:S(2)}, u32[]{:S(2)}) async-start(bf16[16,24,896]{2,1,0:T(8,128)(2,1)} %bitcast.4), calls=%async_computation.1 | async-start | bytes 1376256 | tf_op jit(solution)/shard_map/all_to_all | solution.py:162
  67.9 0.0 collective-permute-done.7.theirs_ref
  67.9 4.3 %weight_term.2 = bf16[640,896]{1,0:T(8,128)(2,1)} custom-call(s32[1]{0:T(128)} %bitcast.2.core_ref, bf16[384,1280]{1,0:T(8,128)(2,1)S(1)} %get-tuple-element.10.mine_ref, bf16[384,1280]{1,0:T(8,128)(2,1)} %collective-permute-done.7.theirs_ref, bf16[384,896]{1,0:T(8,128)(2,1)S(1)} %copy-done.1, bf16[384,896]{1,0:T(8,128)(2,1)S(1)} %collective-permute-done.8.hid_theirs_ref), custom_call_target="tpu_custom_call" | custom-call | flops 880803840 | bytes 4489216 | tf_op jit(solution)/shard_map/weight_term/pallas_call | solution.py:104
  72.2 9.2 %all-to-all-done.1.second_ref = bf16[16,24,896]{2,1,0:T(8,128)(2,1)S(1)} async-done(((bf16[16,24,896]{2,1,0:T(8,128)(2,1)}), bf16[16,24,896]{2,1,0:T(8,128)(2,1)S(1)}, u32[]{:S(2)}, u32[]{:S(2)}) %all-to-all-start.1) | async-done | bytes 688160 | tf_op jit(solution)/shard_map/all_to_all | solution.py:162
  81.4 3.7 %all-to-all-start = ((bf16[16,40,896]{2,1,0:T(8,128)(2,1)}), bf16[16,40,896]{2,1,0:T(8,128)(2,1)S(1)}, u32[]{:S(2)}, u32[]{:S(2)}) async-start(bf16[16,40,896]{2,1,0:T(8,128)(2,1)} %bitcast.3), calls=%async_computation | async-start | bytes 2293760 | tf_op jit(solution)/shard_map/all_to_all | solution.py:162
  85.1 0.7 dynamic-slice_bitcast_fusion.order_ref
  85.8 16.9 %all-to-all-done.first_ref = bf16[16,40,896]{2,1,0:T(8,128)(2,1)S(1)} async-done(((bf16[16,40,896]{2,1,0:T(8,128)(2,1)}), bf16[16,40,896]{2,1,0:T(8,128)(2,1)S(1)}, u32[]{:S(2)}, u32[]{:S(2)}) %all-to-all-start) | async-done | bytes 1146912 | tf_op jit(solution)/shard_map/all_to_all | solution.py:162
  102.7 1.4 %plane_sums.1 = bf16[8,8,896]{2,1,0:T(8,128)(2,1)} custom-call(s32[8]{0:T(128)S(1)} %dynamic-slice_bitcast_fusion.order_ref, bf16[16,40,896]{2,1,0:T(8,128)(2,1)S(1)} %all-to-all-done.first_ref, bf16[16,24,896]{2,1,0:T(8,128)(2,1)S(1)} %all-to-all-done.1.second_ref), custom_call_target="tpu_custom_call" | custom-call | flops 917504 | bytes 1949696 | tf_op jit(solution)/shard_map/plane_sums/pallas_call | solution.py:134
  104.1 12.1 %all-to-all-start.2 = ((bf16[8,8,896]{2,1,0:T(8,128)(2,1)}), bf16[8,8,896]{2,1,0:T(8,128)(2,1)S(1)}, u32[]{:S(2)}, u32[]{:S(2)}) async-start(bf16[8,8,896]{2,1,0:T(8,128)(2,1)} %plane_sums.1), calls=%async_computation.2 | async-start | bytes 229376 | tf_op jit(solution)/shard_map/all_to_all | solution.py:183
  116.2 0.0 copy-start
  116.2 2.0 %copy-done = bf16[2048,896]{1,0:T(8,128)(2,1)S(1)} copy-done((bf16[2048,896]{1,0:T(8,128)(2,1)S(1)}, bf16[2048,896]{1,0:T(8,128)(2,1)}, u32[]{:S(2)}) %copy-start) | copy-done | bytes 3670040
  118.2 0.0 copy-start.3
  118.2 1.4 %copy-done.3 = bf16[384,2048]{1,0:T(8,128)(2,1)S(1)} copy-done((bf16[384,2048]{1,0:T(8,128)(2,1)S(1)}, bf16[384,2048]{1,0:T(8,128)(2,1)}, u32[]{:S(2)}) %copy-start.3) | copy-done | bytes 1572888
  119.6 5.8 %hidden_grads.1 = bf16[384,896]{1,0:T(8,128)(2,1)} custom-call(s32[8]{0:T(128)S(1)} %dynamic-slice_bitcast_fusion.order_ref, bf16[384,2048]{1,0:T(8,128)(2,1)S(1)} %copy-done.3, bf16[2048,896]{1,0:T(8,128)(2,1)S(1)} %copy-done), custom_call_target="tpu_custom_call" | custom-call | flops 1409286144 | bytes 8000000 | tf_op jit(solution)/shard_map/hidden_grads/pallas_call | solution.py:43
  125.4 7.5 %all-to-all-done.2 = bf16[8,8,896]{2,1,0:T(8,128)(2,1)S(1)} async-done(((bf16[8,8,896]{2,1,0:T(8,128)(2,1)}), bf16[8,8,896]{2,1,0:T(8,128)(2,1)S(1)}, u32[]{:S(2)}, u32[]{:S(2)}) %all-to-all-start.2) | async-done | bytes 114720 | tf_op jit(solution)/shard_map/all_to_all | solution.py:183
  133.0 0.6 fusion
  (9 shorter events, 0.2 us)
Async XLA Ops:
  2.4 14.7 %collective-permute-start = (bf16[384,256]{1,0:T(8,128)(2,1)S(1)}, bf16[384,256]{1,0:T(8,128)(2,1)S(1)}, u32[]{:S(2)}, u32[]{:S(2)}) collective-permute-start(bf16[384,256]{1,0:T(8,128)(2,1)S(1)} %get-tuple-element.3), channel_id=1, source_target_pairs={{0,2},{2,4},{4,6},{6,7},{7,5},{5,3},{3,1},{1,0},{8,10},{10,12},{12... | collective-permute-start | bytes 589832 | tf_op jit(solution)/shard_map/ppermute | solution.py:167
  9.8 11.8 %collective-permute-start.1 = (bf16[384,256]{1,0:T(8,128)(2,1)S(1)}, bf16[384,256]{1,0:T(8,128)(2,1)S(1)}, u32[]{:S(2)}, u32[]{:S(2)}) collective-permute-start(bf16[384,256]{1,0:T(8,128)(2,1)S(1)} %get-tuple-element.3), channel_id=1, source_target_pairs={{2,0},{4,2},{6,4},{7,6},{5,7},{3,5},{1,3},{0,1},{10,8},{12,10},{14... | collective-permute-start | bytes 589832 | tf_op jit(solution)/shard_map/ppermute | solution.py:168
  11.7 44.4 %collective-permute-start.8 = (bf16[384,896]{1,0:T(8,128)(2,1)}, bf16[384,896]{1,0:T(8,128)(2,1)S(1)}, u32[]{:S(2)}, u32[]{:S(2)}) collective-permute-start(bf16[384,896]{1,0:T(8,128)(2,1)} %hid_ref.3), channel_id=1, source_target_pairs={{0,8},{8,0},{1,9},{9,1},{2,10},{10,2},{3,11},{11,3},{4,12},{12,4},... | collective-permute-start | bytes 2064392 | tf_op jit(solution)/shard_map/ppermute | solution.py:158
  17.1 8.5 %collective-permute-start.2 = (bf16[384,256]{1,0:T(8,128)(2,1)S(1)}, bf16[384,256]{1,0:T(8,128)(2,1)S(1)}, u32[]{:S(2)}, u32[]{:S(2)}) collective-permute-start(bf16[384,256]{1,0:T(8,128)(2,1)S(1)} %collective-permute-done), channel_id=1, source_target_pairs={{0,2},{2,4},{4,6},{6,7},{7,5},{5,3},{3,1},{1,0},{8,10},{10,12},{12... | collective-permute-start | bytes 589832 | tf_op jit(solution)/shard_map/ppermute | solution.py:167
  21.5 9.7 %collective-permute-start.3 = (bf16[384,256]{1,0:T(8,128)(2,1)S(1)}, bf16[384,256]{1,0:T(8,128)(2,1)S(1)}, u32[]{:S(2)}, u32[]{:S(2)}) collective-permute-start(bf16[384,256]{1,0:T(8,128)(2,1)S(1)} %collective-permute-done.1), channel_id=1, source_target_pairs={{2,0},{4,2},{6,4},{7,6},{5,7},{3,5},{1,3},{0,1},{10,8},{12,10},{14... | collective-permute-start | bytes 589832 | tf_op jit(solution)/shard_map/ppermute | solution.py:168
  24.0 32.1 %copy-start.1 = (bf16[384,896]{1,0:T(8,128)(2,1)S(1)}, bf16[384,896]{1,0:T(8,128)(2,1)}, u32[]{:S(2)}) copy-start(bf16[384,896]{1,0:T(8,128)(2,1)} %hid_ref.3) | copy-start | bytes 2064388
  25.6 12.8 %collective-permute-start.4 = (bf16[384,256]{1,0:T(8,128)(2,1)S(1)}, bf16[384,256]{1,0:T(8,128)(2,1)S(1)}, u32[]{:S(2)}, u32[]{:S(2)}) collective-permute-start(bf16[384,256]{1,0:T(8,128)(2,1)S(1)} %collective-permute-done.2), channel_id=1, source_target_pairs={{0,2},{2,4},{4,6},{6,7},{7,5},{5,3},{3,1},{1,0},{8,10},{10,12},{12... | collective-permute-start | bytes 589832 | tf_op jit(solution)/shard_map/ppermute | solution.py:167
  31.2 13.9 %collective-permute-start.5 = (bf16[384,256]{1,0:T(8,128)(2,1)S(1)}, bf16[384,256]{1,0:T(8,128)(2,1)S(1)}, u32[]{:S(2)}, u32[]{:S(2)}) collective-permute-start(bf16[384,256]{1,0:T(8,128)(2,1)S(1)} %collective-permute-done.3), channel_id=1, source_target_pairs={{2,0},{4,2},{6,4},{7,6},{5,7},{3,5},{1,3},{0,1},{10,8},{12,10},{14... | collective-permute-start | bytes 589832 | tf_op jit(solution)/shard_map/ppermute | solution.py:168
  38.4 12.1 %collective-permute-start.6 = (bf16[384,256]{1,0:T(8,128)(2,1)S(1)}, bf16[384,256]{1,0:T(8,128)(2,1)S(1)}, u32[]{:S(2)}, u32[]{:S(2)}) collective-permute-start(bf16[384,256]{1,0:T(8,128)(2,1)S(1)} %collective-permute-done.4), channel_id=1, source_target_pairs={{0,2},{2,4},{4,6},{6,7},{7,5},{5,3},{3,1},{1,0},{8,10},{10,12},{12... | collective-permute-start | bytes 589832 | tf_op jit(solution)/shard_map/ppermute | solution.py:170
  50.5 1.2 copy-start.2
  51.7 4.4 %collective-permute-start.9 = (bf16[384,768]{1,0:T(8,128)(2,1)S(1)}, bf16[384,768]{1,0:T(8,128)(2,1)}, u32[]{:S(2)}, u32[]{:S(2)}) collective-permute-start(bf16[384,768]{1,0:T(8,128)(2,1)S(1)} %get-tuple-element.4.mine_ref), channel_id=1, source_target_pairs={{0,8},{8,0},{1,9},{9,1},{2,10},{10,2},{3,11},{11,3},{4,12},{12,4},... | collective-permute-start | bytes 1769480 | tf_op jit(solution)/shard_map/ppermute | solution.py:158
  53.6 14.3 %collective-permute-start.7 = (bf16[384,1280]{1,0:T(8,128)(2,1)S(1)}, bf16[384,1280]{1,0:T(8,128)(2,1)}, u32[]{:S(2)}, u32[]{:S(2)}) collective-permute-start(bf16[384,1280]{1,0:T(8,128)(2,1)S(1)} %get-tuple-element.10.mine_ref), channel_id=1, source_target_pairs={{0,8},{8,0},{1,9},{9,1},{2,10},{10,2},{3,11},{11,3},{4,12},{12,4},... | collective-permute-start | bytes 2949128 | tf_op jit(solution)/shard_map/ppermute | solution.py:158
  59.3 22.0 %all-to-all-start.1 = ((bf16[16,24,896]{2,1,0:T(8,128)(2,1)}), bf16[16,24,896]{2,1,0:T(8,128)(2,1)S(1)}, u32[]{:S(2)}, u32[]{:S(2)}) async-start(bf16[16,24,896]{2,1,0:T(8,128)(2,1)} %bitcast.4), calls=%async_computation.1 | async-start | bytes 1376256 | tf_op jit(solution)/shard_map/all_to_all | solution.py:162
  81.4 21.3 %all-to-all-start = ((bf16[16,40,896]{2,1,0:T(8,128)(2,1)}), bf16[16,40,896]{2,1,0:T(8,128)(2,1)S(1)}, u32[]{:S(2)}, u32[]{:S(2)}) async-start(bf16[16,40,896]{2,1,0:T(8,128)(2,1)} %bitcast.3), calls=%async_computation | async-start | bytes 2293760 | tf_op jit(solution)/shard_map/all_to_all | solution.py:162
  104.1 28.9 %all-to-all-start.2 = ((bf16[8,8,896]{2,1,0:T(8,128)(2,1)}), bf16[8,8,896]{2,1,0:T(8,128)(2,1)S(1)}, u32[]{:S(2)}, u32[]{:S(2)}) async-start(bf16[8,8,896]{2,1,0:T(8,128)(2,1)} %plane_sums.1), calls=%async_computation.2 | async-start | bytes 229376 | tf_op jit(solution)/shard_map/all_to_all | solution.py:183
  116.2 2.0 %copy-start = (bf16[2048,896]{1,0:T(8,128)(2,1)S(1)}, bf16[2048,896]{1,0:T(8,128)(2,1)}, u32[]{:S(2)}) copy-start(bf16[2048,896]{1,0:T(8,128)(2,1)} %w_ref.1) | copy-start | bytes 11010052
  118.2 1.4 %copy-start.3 = (bf16[384,2048]{1,0:T(8,128)(2,1)S(1)}, bf16[384,2048]{1,0:T(8,128)(2,1)}, u32[]{:S(2)}) copy-start(bf16[384,2048]{1,0:T(8,128)(2,1)} %copy-done.2) | copy-start | bytes 4718596

commit v3 on v1

v3 whole, which is shorter than its diff:
```python
import functools

import jax
import jax.numpy as jnp
import numpy as np
from jax import lax
from jax.experimental import pallas as pl
from jax.experimental.pallas import tpu as pltpu
from jax.sharding import Mesh, PartitionSpec as P


GRP = ("y", "zh", "x", "core")
RING = (0, 2, 4, 6, 7, 5, 3, 1)
CW = [(RING[i], RING[(i + 1) % 8]) for i in range(8)]
CCW = [(b, a) for a, b in CW]
SHIFTS = (0, -1, 1, -2, 2, -3, 3, 4)
ORDER = np.array(
    [[RING[(RING.index(n) + s) % 8] for s in SHIFTS] for n in range(8)], np.int32
)


def smem():
    return pl.BlockSpec(memory_space=pltpu.SMEM)


def vmem():
    return pl.BlockSpec(memory_space=pltpu.VMEM)


def anywhere():
    return pl.BlockSpec(memory_space=pl.ANY)


def kernel_call(kernel, scalars, arrays, out_shape, scratch, flops, moved, limit):
    several = isinstance(out_shape, (list, tuple))
    return pl.pallas_call(
        kernel,
        in_specs=[smem() for _ in scalars] + [vmem() for _ in arrays],
        out_specs=[vmem() for _ in out_shape] if several else vmem(),
        out_shape=out_shape,
        scratch_shapes=scratch,
        compiler_params=pltpu.CompilerParams(vmem_limit_bytes=limit << 20),
        cost_estimate=pl.CostEstimate(flops=flops, bytes_accessed=moved, transcendentals=0),
    )(*scalars, *arrays)


def scale_kernel(core_ref, count_ref, gate_ref, grad_ref, own_ref, send_ref):
    line = lax.broadcasted_iota(jnp.int32, (256, 256), 0)
    column = lax.broadcasted_iota(jnp.int32, (256, 256), 1)
    half = lax.div(line, 128)
    side = half + core_ref[0] - 2 * half * core_ref[0]
    wanted = lax.div(lax.rem(line, 128), 32) * 64 + side * 32 + lax.rem(line, 32)
    pick = jnp.where(column == wanted, 1.0, 0.0).astype(jnp.bfloat16)
    turned = lax.dot_general(
        pick, grad_ref[...], (((1,), (1,)), ((), ())), preferred_element_type=jnp.float32
    )
    slot = lax.broadcasted_iota(jnp.int32, turned.shape, 1)
    scaled = jnp.where(slot < count_ref[0], turned * gate_ref[...], 0.0).astype(jnp.bfloat16)
    own_ref[...] = scaled[:128]
    send_ref[...] = scaled[128:]


def scale(core, counts, gate, grad):
    rows = grad.shape[0]
    half = jax.ShapeDtypeStruct((128, rows), jnp.bfloat16)
    return kernel_call(
        scale_kernel, (core, counts), (gate.reshape(1, rows), grad), [half, half], [],
        2 * 256 * 256 * rows, 4 * rows * 256, 8,
    )


def term_kernel(k, order_ref, piece_ref, hid_ref, theirs_ref, *refs):
    term_ref, sent_ref, product_ref, sems = refs[-4:]
    back = pltpu.make_async_copy(
        piece_ref.at[pl.ds(128, 128)], sent_ref.at[pl.ds(k * 128, 128)], sems.at[4]
    )
    back.start()
    units = hid_ref.shape[1]
    own, other = piece_ref[:128, :], piece_ref[128:, :]
    for low in range(0, units, 256):
        high = min(low + 256, units)
        product = jnp.dot(own, hid_ref[:, low:high], preferred_element_type=jnp.float32) + jnp.dot(
            other, theirs_ref[:, low:high], preferred_element_type=jnp.float32
        )
        product_ref[:, low:high] = product.astype(product_ref.dtype)
    owner = order_ref[k]
    copies = []
    for x in range(4):
        block = (lax.div(owner, 2) * 4 + x) * 2 + lax.rem(owner, 2)
        at = pl.multiple_of(block * 32, 32)
        copies.append(
            pltpu.make_async_copy(
                product_ref.at[pl.ds(x * 32, 32)], term_ref.at[pl.ds(at, 32)], sems.at[x]
            )
        )
        copies[-1].start()
    for copy in copies:
        copy.wait()
    back.wait()


def add_term(k, order, piece, hidden, hidden_theirs, state):
    rows, units = hidden.shape
    return pl.pallas_call(
        functools.partial(term_kernel, k),
        in_specs=[smem(), vmem(), vmem(), vmem()] + [anywhere() for _ in state],
        out_specs=[anywhere(), anywhere()],
        out_shape=[
            jax.ShapeDtypeStruct((1024, units), jnp.bfloat16),
            jax.ShapeDtypeStruct((1024, rows), jnp.bfloat16),
        ],
        input_output_aliases={4: 0, 5: 1} if state else {},
        scratch_shapes=[
            pltpu.VMEM((128, units), jnp.bfloat16),
            pltpu.SemaphoreType.DMA((5,)),
        ],
        compiler_params=pltpu.CompilerParams(vmem_limit_bytes=8 << 20),
        cost_estimate=pl.CostEstimate(
            flops=128 * 4 * rows * units,
            bytes_accessed=2 * (2 * rows * units + 128 * (units + 3 * rows)),
            transcendentals=0,
        ),
        name="add_term",
    )(order, piece, hidden, hidden_theirs, *state)


def hidden_kernel(order_ref, core_ref, *refs):
    pieces, (theirs_ref, w_ref, out_ref, full_ref) = refs[:8], refs[8:]
    core = core_ref[0]
    for k, piece_ref in enumerate(pieces):
        base = order_ref[k] * 256
        for x in range(4):
            own = pl.multiple_of(base + x * 64 + core * 32, 32)
            other = pl.multiple_of(base + x * 64 + 32 - core * 32, 32)
            at = k * 128 + x * 32
            full_ref[pl.ds(own, 32), :] = piece_ref[x * 32 : x * 32 + 32, :]
            full_ref[pl.ds(other, 32), :] = theirs_ref[at : at + 32, :]
    full = full_ref[...]
    units = out_ref.shape[1]
    for low in range(0, units, 256):
        high = min(low + 256, units)
        out_ref[:, low:high] = lax.dot_general(
            full, w_ref[:, low:high], (((0,), (0,)), ((), ())), preferred_element_type=jnp.float32
        ).astype(out_ref.dtype)


def hidden_grads(order, core, pieces, theirs, w_down):
    model, units = w_down.shape
    rows = theirs.shape[1]
    return kernel_call(
        hidden_kernel, (order, core), (*pieces, theirs, w_down),
        jax.ShapeDtypeStruct((rows, units), jnp.bfloat16),
        [pltpu.VMEM((model, rows), jnp.bfloat16)],
        2 * rows * model * units, 2 * (2 * rows * model + model * units + rows * units),
        24,
    )


def plane_kernel(zh_ref, in_ref, keep_ref, send_ref):
    zh = zh_ref[0]
    mine = pl.multiple_of(zh * 32, 32)
    theirs = pl.multiple_of(32 - zh * 32, 32)
    keep = in_ref[0, pl.ds(mine, 32), :].astype(jnp.float32)
    send = in_ref[0, pl.ds(theirs, 32), :].astype(jnp.float32)
    for chip in range(1, 16):
        keep += in_ref[chip, pl.ds(mine, 32), :].astype(jnp.float32)
        send += in_ref[chip, pl.ds(theirs, 32), :].astype(jnp.float32)
    keep_ref[...] = keep
    send_ref[...] = send.astype(send_ref.dtype)


def plane_sums(zh, parts):
    units = parts.shape[2]
    return kernel_call(
        plane_kernel, (zh,), (parts,),
        [
            jax.ShapeDtypeStruct((32, units), jnp.float32),
            jax.ShapeDtypeStruct((32, units), jnp.bfloat16),
        ],
        [], 16 * 64 * units, 2 * 18 * 64 * units, 8,
    )


def body(grad_out, gate_prob, hidden, w_down, slot_counts):
    _, units = hidden.shape
    order = lax.dynamic_index_in_dim(
        jnp.asarray(ORDER), lax.axis_index("node"), 0, keepdims=False
    )
    core = lax.axis_index("core").reshape(1)
    zh = lax.axis_index("zh").reshape(1)

    def swap(value):
        return lax.ppermute(value, "core", [(0, 1), (1, 0)])

    own, send = scale(core, slot_counts, gate_prob, grad_out)
    theirs = swap(send)
    shard = jnp.concatenate([own, theirs], axis=0)
    hidden_theirs = swap(hidden)

    pieces = [shard]
    forward = backward = shard
    for _ in range(1, 4):
        forward = lax.ppermute(forward, "node", CW)
        backward = lax.ppermute(backward, "node", CCW)
        pieces += [forward, backward]
    pieces.append(lax.ppermute(forward, "node", CW))

    state = ()
    for k, piece in enumerate(pieces):
        state = add_term(k, order, piece, hidden, hidden_theirs, state)
    term, sent = state
    parts = lax.all_to_all(term.reshape(16, 64, units), ("y", "x"), 0, 0, tiled=True)
    theirs = swap(sent)
    grad_hidden = hidden_grads(order, core, pieces, theirs, w_down)
    keep, cross = plane_sums(zh, parts)
    far = lax.ppermute(cross, "zh", [(0, 1), (1, 0)])
    return grad_hidden, (keep + far.astype(jnp.float32)).astype(jnp.bfloat16)


def solution(mesh):
    fine = Mesh(mesh.devices.reshape(4, 2, 4, 2, 8), GRP + ("node",))
    return jax.shard_map(
        body,
        mesh=fine,
        in_specs=(P(GRP, "node"), P(GRP), P(GRP, "node"), P(None, "node"), P(GRP)),
        out_specs=(P(GRP, "node"), P(GRP, "node")),
        check_vma=False,
    )
```

time: 131 us -> 121 us (0.924)
  the two profiles are of different devices: /device:TPU:32 before, /device:TPU:64 now
where the time goes in v3:
time: 121 us
  starting transfers between devices  55.2 us (46%)
  waiting for transfers between devices  38.6 us (32%)
  Pallas kernels  19.1 us (16%)
  local copies, waits for them, and re-layouts  5.53 us (5%)
  between operations  1.69 us (1%)
    all_to_all x1, waiting for transfers between devices, body(): lax.all_to_all(term.reshape(16, 64, units), ('y', 'x'), 0, 0, tiled=True)  23.8 us
    all_to_all x1, starting transfers between devices, body(): lax.all_to_all(term.reshape(16, 64, units), ('y', 'x'), 0, 0, tiled=True)  17.8 us
    ppermute x3, starting transfers between devices, body(): forward = lax.ppermute(forward, 'node', CW)  17 us
    pallas_call x8, Pallas kernels, add_term(): pl.pallas_call(functools.partial(term_kernel, k), in_specs=[smem(), vmem(...  14.6 us
    ppermute x1, waiting for transfers between devices, body(): far = lax.ppermute(cross, 'zh', [(0, 1), (1, 0)])  6.75 us
    ppermute x3, starting transfers between devices, body(): backward = lax.ppermute(backward, 'node', CCW)  6.69 us
    ppermute x3, starting transfers between devices, swap(): return lax.ppermute(value, 'core', [(0, 1), (1, 0)])  5.9 us
    ppermute x1, starting transfers between devices, body(): pieces.append(lax.ppermute(forward, 'node', CW))  5.74 us
  transfers between devices with their start and end apart: 12, of which 7 were waited for; matrix products, arithmetic and copies ran while one was open for 1% of the time, Pallas kernels for 14%

profile of v3, /device:TPU:64, one launch (start us, length us, event | category | flops | bytes accessed | tf_op | source)
XLA Modules:
  0.0 120.7 jit_solution(8638807771310635871)
XLA Ops:
  1.3 0.7 reshape.17.gate_ref
  2.0 0.9 copy-done.17
  2.9 0.3 shard_map.77
  3.2 1.9 %collective-permute-start = (bf16[128,384]{1,0:T(8,128)(2,1)S(1)}, bf16[128,384]{1,0:T(8,128)(2,1)S(1)}, u32[]{:S(2)}, u32[]{:S(2)}) collective-permute-start(bf16[128,384]{1,0:T(8,128)(2,1)S(1)} %get-tuple-element.23), channel_id=1, source_target_pairs={{0,8},{8,0},{1,9},{9,1},{2,10},{10,2},{3,11},{11,3},{4,12},{12,4},... | collective-permute-start | bytes 294920 | tf_op jit(solution)/shard_map/ppermute | solution.py:193
  5.1 1.2 %collective-permute-done = bf16[128,384]{1,0:T(8,128)(2,1)S(1)} collective-permute-done((bf16[128,384]{1,0:T(8,128)(2,1)S(1)}, bf16[128,384]{1,0:T(8,128)(2,1)S(1)}, u32[]{:S(2)}, u32[]{:S(2)}) %collective-permute-start) | collective-permute-done | bytes 98336 | tf_op jit(solution)/shard_map/ppermute | solution.py:193
  6.4 6.4 %collective-permute-start.1 = (bf16[256,384]{1,0:T(8,128)(2,1)S(1)}, bf16[256,384]{1,0:T(8,128)(2,1)S(1)}, u32[]{:S(2)}, u32[]{:S(2)}) collective-permute-start(bf16[256,384]{1,0:T(8,128)(2,1)S(1)} %constant_dynamic-update-slice_fusion.piece_ref.refs_0_), channel_id=1, source_target_pairs={{0,2},{2,4},{4,6},{6,7},{7,5},{5,3},{3,1},{1,0},{8,10},{10,12},{12... | collective-permute-start | bytes 589832 | tf_op jit(solution)/shard_map/ppermute | solution.py:203
  12.8 1.9 %collective-permute-start.8 = (bf16[384,896]{1,0:T(8,128)(2,1)}, bf16[384,896]{1,0:T(8,128)(2,1)S(1)}, u32[]{:S(2)}, u32[]{:S(2)}) collective-permute-start(bf16[384,896]{1,0:T(8,128)(2,1)} %hid_ref.15), channel_id=1, source_target_pairs={{0,8},{8,0},{1,9},{9,1},{2,10},{10,2},{3,11},{11,3},{4,12},{12,4},... | collective-permute-start | bytes 2064392 | tf_op jit(solution)/shard_map/ppermute | solution.py:193
  14.7 2.6 %collective-permute-start.2 = (bf16[256,384]{1,0:T(8,128)(2,1)S(1)}, bf16[256,384]{1,0:T(8,128)(2,1)S(1)}, u32[]{:S(2)}, u32[]{:S(2)}) collective-permute-start(bf16[256,384]{1,0:T(8,128)(2,1)S(1)} %constant_dynamic-update-slice_fusion.piece_ref.refs_0_), channel_id=1, source_target_pairs={{2,0},{4,2},{6,4},{7,6},{5,7},{3,5},{1,3},{0,1},{10,8},{12,10},{14... | collective-permute-start | bytes 589832 | tf_op jit(solution)/shard_map/ppermute | solution.py:204
  17.3 1.2 collective-permute-done.1.piece_ref.refs_1_
  18.5 5.2 %collective-permute-start.3 = (bf16[256,384]{1,0:T(8,128)(2,1)S(1)}, bf16[256,384]{1,0:T(8,128)(2,1)S(1)}, u32[]{:S(2)}, u32[]{:S(2)}) collective-permute-start(bf16[256,384]{1,0:T(8,128)(2,1)S(1)} %collective-permute-done.1.piece_ref.refs_1_), channel_id=1, source_target_pairs={{0,2},{2,4},{4,6},{6,7},{7,5},{5,3},{3,1},{1,0},{8,10},{10,12},{12... | collective-permute-start | bytes 589832 | tf_op jit(solution)/shard_map/ppermute | solution.py:203
  23.7 2.4 %collective-permute-done.2.piece_ref.refs_2_ = bf16[256,384]{1,0:T(8,128)(2,1)S(1)} collective-permute-done((bf16[256,384]{1,0:T(8,128)(2,1)S(1)}, bf16[256,384]{1,0:T(8,128)(2,1)S(1)}, u32[]{:S(2)}, u32[]{:S(2)}) %collective-permute-start.2) | collective-permute-done | bytes 196640 | tf_op jit(solution)/shard_map/ppermute | solution.py:204
  26.1 1.9 %collective-permute-start.4 = (bf16[256,384]{1,0:T(8,128)(2,1)S(1)}, bf16[256,384]{1,0:T(8,128)(2,1)S(1)}, u32[]{:S(2)}, u32[]{:S(2)}) collective-permute-start(bf16[256,384]{1,0:T(8,128)(2,1)S(1)} %collective-permute-done.2.piece_ref.refs_2_), channel_id=1, source_target_pairs={{2,0},{4,2},{6,4},{7,6},{5,7},{3,5},{1,3},{0,1},{10,8},{12,10},{14... | collective-permute-start | bytes 589832 | tf_op jit(solution)/shard_map/ppermute | solution.py:204
  28.0 0.7 collective-permute-done.3.piece_ref.refs_3_
  28.7 5.3 %collective-permute-start.5 = (bf16[256,384]{1,0:T(8,128)(2,1)S(1)}, bf16[256,384]{1,0:T(8,128)(2,1)S(1)}, u32[]{:S(2)}, u32[]{:S(2)}) collective-permute-start(bf16[256,384]{1,0:T(8,128)(2,1)S(1)} %collective-permute-done.3.piece_ref.refs_3_), channel_id=1, source_target_pairs={{0,2},{2,4},{4,6},{6,7},{7,5},{5,3},{3,1},{1,0},{8,10},{10,12},{12... | collective-permute-start | bytes 589832 | tf_op jit(solution)/shard_map/ppermute | solution.py:203
  34.1 2.5 %collective-permute-done.4.piece_ref.refs_4_ = bf16[256,384]{1,0:T(8,128)(2,1)S(1)} collective-permute-done((bf16[256,384]{1,0:T(8,128)(2,1)S(1)}, bf16[256,384]{1,0:T(8,128)(2,1)S(1)}, u32[]{:S(2)}, u32[]{:S(2)}) %collective-permute-start.4) | collective-permute-done | bytes 196640 | tf_op jit(solution)/shard_map/ppermute | solution.py:204
  36.6 2.2 %collective-permute-start.6 = (bf16[256,384]{1,0:T(8,128)(2,1)S(1)}, bf16[256,384]{1,0:T(8,128)(2,1)S(1)}, u32[]{:S(2)}, u32[]{:S(2)}) collective-permute-start(bf16[256,384]{1,0:T(8,128)(2,1)S(1)} %collective-permute-done.4.piece_ref.refs_4_), channel_id=1, source_target_pairs={{2,0},{4,2},{6,4},{7,6},{5,7},{3,5},{1,3},{0,1},{10,8},{12,10},{14... | collective-permute-start | bytes 589832 | tf_op jit(solution)/shard_map/ppermute | solution.py:204
  38.8 0.0 collective-permute-done.5.piece_ref.refs_5_
  38.8 0.0 copy-start.11
  38.8 5.7 %collective-permute-start.7 = (bf16[256,384]{1,0:T(8,128)(2,1)S(1)}, bf16[256,384]{1,0:T(8,128)(2,1)S(1)}, u32[]{:S(2)}, u32[]{:S(2)}) collective-permute-start(bf16[256,384]{1,0:T(8,128)(2,1)S(1)} %collective-permute-done.5.piece_ref.refs_5_), channel_id=1, source_target_pairs={{0,2},{2,4},{4,6},{6,7},{7,5},{5,3},{3,1},{1,0},{8,10},{10,12},{12... | collective-permute-start | bytes 589832 | tf_op jit(solution)/shard_map/ppermute | solution.py:206
  44.6 0.7 dynamic-slice_bitcast_fusion.order_ref
  45.3 0.0 collective-permute-done.8.theirs_ref
  45.3 1.1 copy-done
  46.4 1.8 %add_term.8 = (bf16[1024,896]{1,0:T(8,128)(2,1)}, bf16[1024,384]{1,0:T(8,128)(2,1)S(1)}) custom-call(s32[8]{0:T(128)S(1)} %dynamic-slice_bitcast_fusion.order_ref, bf16[256,384]{1,0:T(8,128)(2,1)S(1)} %constant_dynamic-update-slice_fusion.piece_ref.refs_0_, bf16[384,896]{1,0:T(8,128)(2,1)S(1)} %copy-done, bf16[384,896]{1,0:T(8,128)(2,1)S(1)} %collective-permute-done.8.theirs_ref), custom_call_target="tpu_custom_call" | custom-call | flops 176160768 | bytes 1900544 | tf_op jit(solution)/shard_map/add_term/pallas_call | solution.py:104
  48.2 0.0 copy-done.1
  48.2 1.8 %add_term.9 = (bf16[1024,896]{1,0:T(8,128)(2,1)}, bf16[1024,384]{1,0:T(8,128)(2,1)S(1)}) custom-call(s32[8]{0:T(128)S(1)} %dynamic-slice_bitcast_fusion.order_ref, bf16[256,384]{1,0:T(8,128)(2,1)S(1)} %collective-permute-done.1.piece_ref.refs_1_, bf16[384,896]{1,0:T(8,128)(2,1)S(1)} %copy-done.1, ...), custom_call_target="tpu_custom_call", output_to_operand_aliasing={{0}: (4, {}), {1}: (5, {})} | custom-call | flops 176160768 | bytes 1900544 | tf_op jit(solution)/shard_map/add_term/pallas_call | solution.py:104
  50.1 0.0 copy-done.3
  50.1 1.8 %add_term.10 = (bf16[1024,896]{1,0:T(8,128)(2,1)}, bf16[1024,384]{1,0:T(8,128)(2,1)S(1)}) custom-call(s32[8]{0:T(128)S(1)} %dynamic-slice_bitcast_fusion.order_ref, bf16[256,384]{1,0:T(8,128)(2,1)S(1)} %collective-permute-done.2.piece_ref.refs_2_, bf16[384,896]{1,0:T(8,128)(2,1)S(1)} %copy-done.1, ...), custom_call_target="tpu_custom_call", output_to_operand_aliasing={{0}: (4, {}), {1}: (5, {})} | custom-call | flops 176160768 | bytes 1900544 | tf_op jit(solution)/shard_map/add_term/pallas_call | solution.py:104
  51.9 1.8 %add_term.11 = (bf16[1024,896]{1,0:T(8,128)(2,1)}, bf16[1024,384]{1,0:T(8,128)(2,1)S(1)}) custom-call(s32[8]{0:T(128)S(1)} %dynamic-slice_bitcast_fusion.order_ref, bf16[256,384]{1,0:T(8,128)(2,1)S(1)} %collective-permute-done.3.piece_ref.refs_3_, bf16[384,896]{1,0:T(8,128)(2,1)S(1)} %copy-done.1, ...), custom_call_target="tpu_custom_call", output_to_operand_aliasing={{0}: (4, {}), {1}: (5, {})} | custom-call | flops 176160768 | bytes 1900544 | tf_op jit(solution)/shard_map/add_term/pallas_call | solution.py:104
  53.8 1.8 %add_term.12 = (bf16[1024,896]{1,0:T(8,128)(2,1)}, bf16[1024,384]{1,0:T(8,128)(2,1)S(1)}) custom-call(s32[8]{0:T(128)S(1)} %dynamic-slice_bitcast_fusion.order_ref, bf16[256,384]{1,0:T(8,128)(2,1)S(1)} %collective-permute-done.4.piece_ref.refs_4_, bf16[384,896]{1,0:T(8,128)(2,1)S(1)} %copy-done.1, ...), custom_call_target="tpu_custom_call", output_to_operand_aliasing={{0}: (4, {}), {1}: (5, {})} | custom-call | flops 176160768 | bytes 1900544 | tf_op jit(solution)/shard_map/add_term/pallas_call | solution.py:104
  55.6 0.0 copy-done.11
  55.6 1.8 %add_term.13 = (bf16[1024,896]{1,0:T(8,128)(2,1)}, bf16[1024,384]{1,0:T(8,128)(2,1)S(1)}) custom-call(s32[8]{0:T(128)S(1)} %dynamic-slice_bitcast_fusion.order_ref, bf16[256,384]{1,0:T(8,128)(2,1)S(1)} %collective-permute-done.5.piece_ref.refs_5_, bf16[384,896]{1,0:T(8,128)(2,1)S(1)} %copy-done.1, ...), custom_call_target="tpu_custom_call", output_to_operand_aliasing={{0}: (4, {}), {1}: (5, {})} | custom-call | flops 176160768 | bytes 1900544 | tf_op jit(solution)/shard_map/add_term/pallas_call | solution.py:104
  57.5 0.0 collective-permute-done.6.piece_ref.refs_6_
  57.5 1.8 %add_term.14 = (bf16[1024,896]{1,0:T(8,128)(2,1)}, bf16[1024,384]{1,0:T(8,128)(2,1)S(1)}) custom-call(s32[8]{0:T(128)S(1)} %dynamic-slice_bitcast_fusion.order_ref, bf16[256,384]{1,0:T(8,128)(2,1)S(1)} %collective-permute-done.6.piece_ref.refs_6_, bf16[384,896]{1,0:T(8,128)(2,1)S(1)} %copy-done.1, ...), custom_call_target="tpu_custom_call", output_to_operand_aliasing={{0}: (4, {}), {1}: (5, {})} | custom-call | flops 176160768 | bytes 1900544 | tf_op jit(solution)/shard_map/add_term/pallas_call | solution.py:104
  59.3 0.0 collective-permute-done.7.piece_ref.refs_7_
  59.3 1.8 %add_term.15 = (bf16[1024,896]{1,0:T(8,128)(2,1)}, bf16[1024,384]{1,0:T(8,128)(2,1)S(1)}) custom-call(s32[8]{0:T(128)S(1)} %dynamic-slice_bitcast_fusion.order_ref, bf16[256,384]{1,0:T(8,128)(2,1)S(1)} %collective-permute-done.7.piece_ref.refs_7_, bf16[384,896]{1,0:T(8,128)(2,1)S(1)} %copy-done.1, ...), custom_call_target="tpu_custom_call", output_to_operand_aliasing={{0}: (4, {}), {1}: (5, {})} | custom-call | flops 176160768 | bytes 1900544 | tf_op jit(solution)/shard_map/add_term/pallas_call | solution.py:104
  61.2 0.0 copy-done.15
  61.2 17.8 %all-to-all-start = ((bf16[16,64,896]{2,1,0:T(8,128)(2,1)}), bf16[16,64,896]{2,1,0:T(8,128)(2,1)S(1)}, u32[]{:S(2)}, u32[]{:S(2)}) async-start(bf16[16,64,896]{2,1,0:T(8,128)(2,1)} %bitcast.3), calls=%async_computation | async-start | bytes 3670016 | tf_op jit(solution)/shard_map/all_to_all | solution.py:212
  79.0 0.0 copy-start.4
  79.1 2.1 %collective-permute-start.9 = (bf16[1024,384]{1,0:T(8,128)(2,1)S(1)}, bf16[1024,384]{1,0:T(8,128)(2,1)}, u32[]{:S(2)}, u32[]{:S(2)}) collective-permute-start(bf16[1024,384]{1,0:T(8,128)(2,1)S(1)} %get-tuple-element.38), channel_id=1, source_target_pairs={{0,8},{8,0},{1,9},{9,1},{2,10},{10,2},{3,11},{11,3},{4,12},{12,4},... | collective-permute-start | bytes 2359304 | tf_op jit(solution)/shard_map/ppermute | solution.py:193
  81.1 23.8 %all-to-all-done.in_ref = bf16[16,64,896]{2,1,0:T(8,128)(2,1)S(1)} async-done(((bf16[16,64,896]{2,1,0:T(8,128)(2,1)}), bf16[16,64,896]{2,1,0:T(8,128)(2,1)S(1)}, u32[]{:S(2)}, u32[]{:S(2)}) %all-to-all-start) | async-done | bytes 1835040 | tf_op jit(solution)/shard_map/all_to_all | solution.py:212
  104.9 0.2 shard_map.79
  105.2 2.1 %collective-permute-start.10 = (bf16[32,896]{1,0:T(8,128)(2,1)S(1)}, bf16[32,896]{1,0:T(8,128)(2,1)S(1)}, u32[]{:S(2)}, u32[]{:S(2)}) collective-permute-start(bf16[32,896]{1,0:T(8,128)(2,1)S(1)} %get-tuple-element.41), channel_id=1, source_target_pairs={{0,64},{64,0},{1,65},{65,1},{2,66},{66,2},{3,67},{67,3},{4,68},{68... | collective-permute-start | bytes 172040 | tf_op jit(solution)/shard_map/ppermute | solution.py:216
  107.2 0.0 collective-permute-done.9.refs_8_
  107.3 0.0 copy-start.2
  107.3 2.0 %copy-done.2 = bf16[2048,896]{1,0:T(8,128)(2,1)S(1)} copy-done((bf16[2048,896]{1,0:T(8,128)(2,1)S(1)}, bf16[2048,896]{1,0:T(8,128)(2,1)}, u32[]{:S(2)}) %copy-start.2) | copy-done | bytes 3670040
  109.4 4.0 %shard_map.78 = bf16[384,896]{1,0:T(8,128)(2,1)} custom-call(s32[8]{0:T(128)S(1)} %dynamic-slice_bitcast_fusion.order_ref, s32[1]{0:T(128)} %bitcast.1.core_ref, bf16[256,384]{1,0:T(8,128)(2,1)S(1)} %constant_dynamic-update-slice_fusion.piece_ref.refs_0_, bf16[256,384]{1,0:T(8,128)(2,1)S(1)} %copy-done.4, bf16[256,384]{1,0:T(8,128)(2,1)S(1)} %copy-done.6, ...), custom_call_target="tpu_custom_call" | custom-call | flops 1409286144 | bytes 7503872 | tf_op jit(solution)/shard_map/pallas_call | solution.py:36
  113.3 6.7 %collective-permute-done.10 = bf16[32,896]{1,0:T(8,128)(2,1)S(1)} collective-permute-done((bf16[32,896]{1,0:T(8,128)(2,1)S(1)}, bf16[32,896]{1,0:T(8,128)(2,1)S(1)}, u32[]{:S(2)}, u32[]{:S(2)}) %collective-permute-start.10) | collective-permute-done | bytes 57376 | tf_op jit(solution)/shard_map/ppermute | solution.py:216
  120.1 0.6 add_convert_fusion
  (28 shorter events, 0.1 us)
Async XLA Ops:
  2.0 0.9 copy-start.17
  3.2 3.2 %collective-permute-start = (bf16[128,384]{1,0:T(8,128)(2,1)S(1)}, bf16[128,384]{1,0:T(8,128)(2,1)S(1)}, u32[]{:S(2)}, u32[]{:S(2)}) collective-permute-start(bf16[128,384]{1,0:T(8,128)(2,1)S(1)} %get-tuple-element.23), channel_id=1, source_target_pairs={{0,8},{8,0},{1,9},{9,1},{2,10},{10,2},{3,11},{11,3},{4,12},{12,4},... | collective-permute-start | bytes 294920 | tf_op jit(solution)/shard_map/ppermute | solution.py:193
  6.4 12.1 %collective-permute-start.1 = (bf16[256,384]{1,0:T(8,128)(2,1)S(1)}, bf16[256,384]{1,0:T(8,128)(2,1)S(1)}, u32[]{:S(2)}, u32[]{:S(2)}) collective-permute-start(bf16[256,384]{1,0:T(8,128)(2,1)S(1)} %constant_dynamic-update-slice_fusion.piece_ref.refs_0_), channel_id=1, source_target_pairs={{0,2},{2,4},{4,6},{6,7},{7,5},{5,3},{3,1},{1,0},{8,10},{10,12},{12... | collective-permute-start | bytes 589832 | tf_op jit(solution)/shard_map/ppermute | solution.py:203
  12.8 32.5 %collective-permute-start.8 = (bf16[384,896]{1,0:T(8,128)(2,1)}, bf16[384,896]{1,0:T(8,128)(2,1)S(1)}, u32[]{:S(2)}, u32[]{:S(2)}) collective-permute-start(bf16[384,896]{1,0:T(8,128)(2,1)} %hid_ref.15), channel_id=1, source_target_pairs={{0,8},{8,0},{1,9},{9,1},{2,10},{10,2},{3,11},{11,3},{4,12},{12,4},... | collective-permute-start | bytes 2064392 | tf_op jit(solution)/shard_map/ppermute | solution.py:193
  14.7 11.4 %collective-permute-start.2 = (bf16[256,384]{1,0:T(8,128)(2,1)S(1)}, bf16[256,384]{1,0:T(8,128)(2,1)S(1)}, u32[]{:S(2)}, u32[]{:S(2)}) collective-permute-start(bf16[256,384]{1,0:T(8,128)(2,1)S(1)} %constant_dynamic-update-slice_fusion.piece_ref.refs_0_), channel_id=1, source_target_pairs={{2,0},{4,2},{6,4},{7,6},{5,7},{3,5},{1,3},{0,1},{10,8},{12,10},{14... | collective-permute-start | bytes 589832 | tf_op jit(solution)/shard_map/ppermute | solution.py:204
  18.5 31.6 %copy-start.3 = (bf16[256,384]{1,0:T(8,128)(2,1)}, bf16[256,384]{1,0:T(8,128)(2,1)S(1)}, u32[]{:S(2)}) copy-start(bf16[256,384]{1,0:T(8,128)(2,1)S(1)} %collective-permute-done.1.piece_ref.refs_1_) | copy-start | bytes 589828
  18.5 10.2 %collective-permute-start.3 = (bf16[256,384]{1,0:T(8,128)(2,1)S(1)}, bf16[256,384]{1,0:T(8,128)(2,1)S(1)}, u32[]{:S(2)}, u32[]{:S(2)}) collective-permute-start(bf16[256,384]{1,0:T(8,128)(2,1)S(1)} %collective-permute-done.1.piece_ref.refs_1_), channel_id=1, source_target_pairs={{0,2},{2,4},{4,6},{6,7},{7,5},{5,3},{3,1},{1,0},{8,10},{10,12},{12... | collective-permute-start | bytes 589832 | tf_op jit(solution)/shard_map/ppermute | solution.py:203
  26.1 24.0 %copy-start.5 = (bf16[256,384]{1,0:T(8,128)(2,1)}, bf16[256,384]{1,0:T(8,128)(2,1)S(1)}, u32[]{:S(2)}) copy-start(bf16[256,384]{1,0:T(8,128)(2,1)S(1)} %collective-permute-done.2.piece_ref.refs_2_) | copy-start | bytes 589828
  26.1 10.5 %collective-permute-start.4 = (bf16[256,384]{1,0:T(8,128)(2,1)S(1)}, bf16[256,384]{1,0:T(8,128)(2,1)S(1)}, u32[]{:S(2)}, u32[]{:S(2)}) collective-permute-start(bf16[256,384]{1,0:T(8,128)(2,1)S(1)} %collective-permute-done.2.piece_ref.refs_2_), channel_id=1, source_target_pairs={{2,0},{4,2},{6,4},{7,6},{5,7},{3,5},{1,3},{0,1},{10,8},{12,10},{14... | collective-permute-start | bytes 589832 | tf_op jit(solution)/shard_map/ppermute | solution.py:204
  28.7 23.2 %copy-start.7 = (bf16[256,384]{1,0:T(8,128)(2,1)}, bf16[256,384]{1,0:T(8,128)(2,1)S(1)}, u32[]{:S(2)}) copy-start(bf16[256,384]{1,0:T(8,128)(2,1)S(1)} %collective-permute-done.3.piece_ref.refs_3_) | copy-start | bytes 589828
  28.7 10.1 %collective-permute-start.5 = (bf16[256,384]{1,0:T(8,128)(2,1)S(1)}, bf16[256,384]{1,0:T(8,128)(2,1)S(1)}, u32[]{:S(2)}, u32[]{:S(2)}) collective-permute-start(bf16[256,384]{1,0:T(8,128)(2,1)S(1)} %collective-permute-done.3.piece_ref.refs_3_), channel_id=1, source_target_pairs={{0,2},{2,4},{4,6},{6,7},{7,5},{5,3},{3,1},{1,0},{8,10},{10,12},{12... | collective-permute-start | bytes 589832 | tf_op jit(solution)/shard_map/ppermute | solution.py:203
  36.6 17.2 %copy-start.9 = (bf16[256,384]{1,0:T(8,128)(2,1)}, bf16[256,384]{1,0:T(8,128)(2,1)S(1)}, u32[]{:S(2)}) copy-start(bf16[256,384]{1,0:T(8,128)(2,1)S(1)} %collective-permute-done.4.piece_ref.refs_4_) | copy-start | bytes 589828
  36.6 20.9 %collective-permute-start.6 = (bf16[256,384]{1,0:T(8,128)(2,1)S(1)}, bf16[256,384]{1,0:T(8,128)(2,1)S(1)}, u32[]{:S(2)}, u32[]{:S(2)}) collective-permute-start(bf16[256,384]{1,0:T(8,128)(2,1)S(1)} %collective-permute-done.4.piece_ref.refs_4_), channel_id=1, source_target_pairs={{2,0},{4,2},{6,4},{7,6},{5,7},{3,5},{1,3},{0,1},{10,8},{12,10},{14... | collective-permute-start | bytes 589832 | tf_op jit(solution)/shard_map/ppermute | solution.py:204
  38.8 16.8 %copy-start.11 = (bf16[256,384]{1,0:T(8,128)(2,1)}, bf16[256,384]{1,0:T(8,128)(2,1)S(1)}, u32[]{:S(2)}) copy-start(bf16[256,384]{1,0:T(8,128)(2,1)S(1)} %collective-permute-done.5.piece_ref.refs_5_) | copy-start | bytes 589828
  38.8 20.5 %collective-permute-start.7 = (bf16[256,384]{1,0:T(8,128)(2,1)S(1)}, bf16[256,384]{1,0:T(8,128)(2,1)S(1)}, u32[]{:S(2)}, u32[]{:S(2)}) collective-permute-start(bf16[256,384]{1,0:T(8,128)(2,1)S(1)} %collective-permute-done.5.piece_ref.refs_5_), channel_id=1, source_target_pairs={{0,2},{2,4},{4,6},{6,7},{7,5},{5,3},{3,1},{1,0},{8,10},{10,12},{12... | collective-permute-start | bytes 589832 | tf_op jit(solution)/shard_map/ppermute | solution.py:206
  45.3 1.1 copy-start
  46.4 1.9 %copy-start.1 = (bf16[384,896]{1,0:T(8,128)(2,1)S(1)}, bf16[384,896]{1,0:T(8,128)(2,1)}, u32[]{:S(2)}) copy-start(bf16[384,896]{1,0:T(8,128)(2,1)} %hid_ref.15) | copy-start | bytes 2064388
  57.5 1.8 %copy-start.13 = (bf16[256,384]{1,0:T(8,128)(2,1)}, bf16[256,384]{1,0:T(8,128)(2,1)S(1)}, u32[]{:S(2)}) copy-start(bf16[256,384]{1,0:T(8,128)(2,1)S(1)} %collective-permute-done.6.piece_ref.refs_6_) | copy-start | bytes 589828
  59.3 1.9 %copy-start.15 = (bf16[256,384]{1,0:T(8,128)(2,1)}, bf16[256,384]{1,0:T(8,128)(2,1)S(1)}, u32[]{:S(2)}) copy-start(bf16[256,384]{1,0:T(8,128)(2,1)S(1)} %collective-permute-done.7.piece_ref.refs_7_) | copy-start | bytes 589828
  61.2 43.7 %all-to-all-start = ((bf16[16,64,896]{2,1,0:T(8,128)(2,1)}), bf16[16,64,896]{2,1,0:T(8,128)(2,1)S(1)}, u32[]{:S(2)}, u32[]{:S(2)}) async-start(bf16[16,64,896]{2,1,0:T(8,128)(2,1)} %bitcast.3), calls=%async_computation | async-start | bytes 3670016 | tf_op jit(solution)/shard_map/all_to_all | solution.py:212
  79.0 28.2 %copy-start.4 = (bf16[256,384]{1,0:T(8,128)(2,1)S(1)}, bf16[256,384]{1,0:T(8,128)(2,1)}, u32[]{:S(2)}) copy-start(bf16[256,384]{1,0:T(8,128)(2,1)} %copy-done.3) | copy-start | bytes 589828
  79.1 28.2 %copy-start.6 = (bf16[256,384]{1,0:T(8,128)(2,1)S(1)}, bf16[256,384]{1,0:T(8,128)(2,1)}, u32[]{:S(2)}) copy-start(bf16[256,384]{1,0:T(8,128)(2,1)} %copy-done.5) | copy-start | bytes 589828
  79.1 28.2 %copy-start.8 = (bf16[256,384]{1,0:T(8,128)(2,1)S(1)}, bf16[256,384]{1,0:T(8,128)(2,1)}, u32[]{:S(2)}) copy-start(bf16[256,384]{1,0:T(8,128)(2,1)} %copy-done.7) | copy-start | bytes 589828
  79.1 28.2 %collective-permute-start.9 = (bf16[1024,384]{1,0:T(8,128)(2,1)S(1)}, bf16[1024,384]{1,0:T(8,128)(2,1)}, u32[]{:S(2)}, u32[]{:S(2)}) collective-permute-start(bf16[1024,384]{1,0:T(8,128)(2,1)S(1)} %get-tuple-element.38), channel_id=1, source_target_pairs={{0,8},{8,0},{1,9},{9,1},{2,10},{10,2},{3,11},{11,3},{4,12},{12,4},... | collective-permute-start | bytes 2359304 | tf_op jit(solution)/shard_map/ppermute | solution.py:193
  104.9 2.4 %copy-start.10 = (bf16[256,384]{1,0:T(8,128)(2,1)S(1)}, bf16[256,384]{1,0:T(8,128)(2,1)}, u32[]{:S(2)}) copy-start(bf16[256,384]{1,0:T(8,128)(2,1)} %copy-done.9) | copy-start | bytes 589828
  104.9 2.4 %copy-start.12 = (bf16[256,384]{1,0:T(8,128)(2,1)S(1)}, bf16[256,384]{1,0:T(8,128)(2,1)}, u32[]{:S(2)}) copy-start(bf16[256,384]{1,0:T(8,128)(2,1)} %copy-done.11) | copy-start | bytes 589828
  104.9 2.4 %copy-start.14 = (bf16[256,384]{1,0:T(8,128)(2,1)S(1)}, bf16[256,384]{1,0:T(8,128)(2,1)}, u32[]{:S(2)}) copy-start(bf16[256,384]{1,0:T(8,128)(2,1)} %copy-done.13) | copy-start | bytes 589828
  104.9 2.4 %copy-start.16 = (bf16[256,384]{1,0:T(8,128)(2,1)S(1)}, bf16[256,384]{1,0:T(8,128)(2,1)}, u32[]{:S(2)}) copy-start(bf16[256,384]{1,0:T(8,128)(2,1)} %copy-done.15) | copy-start | bytes 589828
  105.2 14.9 %collective-permute-start.10 = (bf16[32,896]{1,0:T(8,128)(2,1)S(1)}, bf16[32,896]{1,0:T(8,128)(2,1)S(1)}, u32[]{:S(2)}, u32[]{:S(2)}) collective-permute-start(bf16[32,896]{1,0:T(8,128)(2,1)S(1)} %get-tuple-element.41), channel_id=1, source_target_pairs={{0,64},{64,0},{1,65},{65,1},{2,66},{66,2},{3,67},{67,3},{4,68},{68... | collective-permute-start | bytes 172040 | tf_op jit(solution)/shard_map/ppermute | solution.py:216
  107.3 2.0 %copy-start.2 = (bf16[2048,896]{1,0:T(8,128)(2,1)S(1)}, bf16[2048,896]{1,0:T(8,128)(2,1)}, u32[]{:S(2)}) copy-start(bf16[2048,896]{1,0:T(8,128)(2,1)} %refs_9_.1) | copy-start | bytes 11010052

commit v4 on v3

--- a/solution.py
+++ b/solution.py
@@ -44,28 +44,42 @@
     )(*scalars, *arrays)
 
 
-def scale_kernel(core_ref, count_ref, gate_ref, grad_ref, own_ref, send_ref):
+def scale_kernel(count_ref, gate_ref, grad_ref, own_ref, send_ref):
     line = lax.broadcasted_iota(jnp.int32, (256, 256), 0)
     column = lax.broadcasted_iota(jnp.int32, (256, 256), 1)
     half = lax.div(line, 128)
-    side = half + core_ref[0] - 2 * half * core_ref[0]
+    core = lax.axis_index("core")
+    side = half + core - 2 * half * core
     wanted = lax.div(lax.rem(line, 128), 32) * 64 + side * 32 + lax.rem(line, 32)
     pick = jnp.where(column == wanted, 1.0, 0.0).astype(jnp.bfloat16)
     turned = lax.dot_general(
         pick, grad_ref[...], (((1,), (1,)), ((), ())), preferred_element_type=jnp.float32
     )
     slot = lax.broadcasted_iota(jnp.int32, turned.shape, 1)
-    scaled = jnp.where(slot < count_ref[0], turned * gate_ref[...], 0.0).astype(jnp.bfloat16)
+    scaled = jnp.where(slot < count_ref[0], turned * gate_ref[...][None, :], 0.0).astype(jnp.bfloat16)
     own_ref[...] = scaled[:128]
     send_ref[...] = scaled[128:]
 
 
-def scale(core, counts, gate, grad):
+def scale(counts, gate, grad):
     rows = grad.shape[0]
     half = jax.ShapeDtypeStruct((128, rows), jnp.bfloat16)
     return kernel_call(
-        scale_kernel, (core, counts), (gate.reshape(1, rows), grad), [half, half], [],
+        scale_kernel, (counts,), (gate, grad), [half, half], [],
         2 * 256 * 256 * rows, 4 * rows * 256, 8,
+    )
+
+
+def join_kernel(own_ref, theirs_ref, out_ref):
+    out_ref[:128, :] = own_ref[...]
+    out_ref[128:, :] = theirs_ref[...]
+
+
+def join(own, theirs):
+    rows = own.shape[1]
+    return kernel_call(
+        join_kernel, (), (own, theirs), jax.ShapeDtypeStruct((256, rows), jnp.bfloat16), [],
+        0, 4 * 256 * rows, 8,
     )
 
 
@@ -192,9 +206,9 @@
     def swap(value):
         return lax.ppermute(value, "core", [(0, 1), (1, 0)])
 
-    own, send = scale(core, slot_counts, gate_prob, grad_out)
+    own, send = scale(slot_counts, gate_prob, grad_out)
     theirs = swap(send)
-    shard = jnp.concatenate([own, theirs], axis=0)
+    shard = join(own, theirs)
     hidden_theirs = swap(hidden)
 
     pieces = [shard]

time: 121 us -> 121 us (level)
    unnamed x37 -> x38, local copies, waits for them, and re-layouts: 4.13 us -> 4.79 us
    pallas_call x3 -> x4, Pallas kernels: 4.49 us -> 4.51 us  [kernel_call(): pl.pallas_call(kernel, in_specs=[smem() for _ in scalars] + [vmem() for _...]
where the time goes in v4:
time: 121 us
  starting transfers between devices  55.2 us (46%)
  waiting for transfers between devices  38.6 us (32%)
  Pallas kernels  19.1 us (16%)
  local copies, waits for them, and re-layouts  5.49 us (5%)
  between operations  1.69 us (1%)
    all_to_all x1, waiting for transfers between devices, body(): lax.all_to_all(term.reshape(16, 64, units), ('y', 'x'), 0, 0, tiled=True)  23.7 us
    all_to_all x1, starting transfers between devices, body(): lax.all_to_all(term.reshape(16, 64, units), ('y', 'x'), 0, 0, tiled=True)  17.8 us
    ppermute x3, starting transfers between devices, body(): forward = lax.ppermute(forward, 'node', CW)  17 us
    pallas_call x8, Pallas kernels, add_term(): pl.pallas_call(functools.partial(term_kernel, k), in_specs=[smem(), vmem(...  14.6 us
    ppermute x1, waiting for transfers between devices, body(): far = lax.ppermute(cross, 'zh', [(0, 1), (1, 0)])  6.75 us
    ppermute x3, starting transfers between devices, body(): backward = lax.ppermute(backward, 'node', CCW)  6.69 us
    ppermute x3, starting transfers between devices, swap(): return lax.ppermute(value, 'core', [(0, 1), (1, 0)])  5.9 us
    ppermute x1, starting transfers between devices, body(): pieces.append(lax.ppermute(forward, 'node', CW))  5.74 us
  transfers between devices with their start and end apart: 12, of which 7 were waited for; matrix products, arithmetic and copies ran while one was open for 1% of the time, Pallas kernels for 14%

profile of v4, /device:TPU:64, one launch (start us, length us, event | category | flops | bytes accessed | tf_op | source)
XLA Modules:
  0.0 120.7 jit_solution(973518473598903735)
XLA Ops:
  1.3 0.0 copy-start.17
  1.3 0.9 copy-done.17
  2.2 0.7 copy-done.18
  2.9 0.3 shard_map.77
  3.2 1.9 %collective-permute-start = (bf16[128,384]{1,0:T(8,128)(2,1)S(1)}, bf16[128,384]{1,0:T(8,128)(2,1)S(1)}, u32[]{:S(2)}, u32[]{:S(2)}) collective-permute-start(bf16[128,384]{1,0:T(8,128)(2,1)S(1)} %get-tuple-element.23), channel_id=1, source_target_pairs={{0,8},{8,0},{1,9},{9,1},{2,10},{10,2},{3,11},{11,3},{4,12},{12,4},... | collective-permute-start | bytes 294920 | tf_op jit(solution)/shard_map/ppermute | solution.py:207
  5.1 1.3 %collective-permute-done.theirs_ref = bf16[128,384]{1,0:T(8,128)(2,1)S(1)} collective-permute-done((bf16[128,384]{1,0:T(8,128)(2,1)S(1)}, bf16[128,384]{1,0:T(8,128)(2,1)S(1)}, u32[]{:S(2)}, u32[]{:S(2)}) %collective-permute-start) | collective-permute-done | bytes 98336 | tf_op jit(solution)/shard_map/ppermute | solution.py:207
  6.4 6.4 %collective-permute-start.1 = (bf16[256,384]{1,0:T(8,128)(2,1)S(1)}, bf16[256,384]{1,0:T(8,128)(2,1)S(1)}, u32[]{:S(2)}, u32[]{:S(2)}) collective-permute-start(bf16[256,384]{1,0:T(8,128)(2,1)S(1)} %shard_map.78.piece_ref.refs_0_), channel_id=1, source_target_pairs={{0,2},{2,4},{4,6},{6,7},{7,5},{5,3},{3,1},{1,0},{8,10},{10,12},{12... | collective-permute-start | bytes 589832 | tf_op jit(solution)/shard_map/ppermute | solution.py:217
  12.8 1.9 %collective-permute-start.8 = (bf16[384,896]{1,0:T(8,128)(2,1)}, bf16[384,896]{1,0:T(8,128)(2,1)S(1)}, u32[]{:S(2)}, u32[]{:S(2)}) collective-permute-start(bf16[384,896]{1,0:T(8,128)(2,1)} %hid_ref.15), channel_id=1, source_target_pairs={{0,8},{8,0},{1,9},{9,1},{2,10},{10,2},{3,11},{11,3},{4,12},{12,4},... | collective-permute-start | bytes 2064392 | tf_op jit(solution)/shard_map/ppermute | solution.py:207
  14.7 2.6 %collective-permute-start.2 = (bf16[256,384]{1,0:T(8,128)(2,1)S(1)}, bf16[256,384]{1,0:T(8,128)(2,1)S(1)}, u32[]{:S(2)}, u32[]{:S(2)}) collective-permute-start(bf16[256,384]{1,0:T(8,128)(2,1)S(1)} %shard_map.78.piece_ref.refs_0_), channel_id=1, source_target_pairs={{2,0},{4,2},{6,4},{7,6},{5,7},{3,5},{1,3},{0,1},{10,8},{12,10},{14... | collective-permute-start | bytes 589832 | tf_op jit(solution)/shard_map/ppermute | solution.py:218
  17.3 1.2 collective-permute-done.1.piece_ref.refs_1_
  18.5 5.2 %collective-permute-start.3 = (bf16[256,384]{1,0:T(8,128)(2,1)S(1)}, bf16[256,384]{1,0:T(8,128)(2,1)S(1)}, u32[]{:S(2)}, u32[]{:S(2)}) collective-permute-start(bf16[256,384]{1,0:T(8,128)(2,1)S(1)} %collective-permute-done.1.piece_ref.refs_1_), channel_id=1, source_target_pairs={{0,2},{2,4},{4,6},{6,7},{7,5},{5,3},{3,1},{1,0},{8,10},{10,12},{12... | collective-permute-start | bytes 589832 | tf_op jit(solution)/shard_map/ppermute | solution.py:217
  23.7 2.4 %collective-permute-done.2.piece_ref.refs_2_ = bf16[256,384]{1,0:T(8,128)(2,1)S(1)} collective-permute-done((bf16[256,384]{1,0:T(8,128)(2,1)S(1)}, bf16[256,384]{1,0:T(8,128)(2,1)S(1)}, u32[]{:S(2)}, u32[]{:S(2)}) %collective-permute-start.2) | collective-permute-done | bytes 196640 | tf_op jit(solution)/shard_map/ppermute | solution.py:218
  26.1 1.9 %collective-permute-start.4 = (bf16[256,384]{1,0:T(8,128)(2,1)S(1)}, bf16[256,384]{1,0:T(8,128)(2,1)S(1)}, u32[]{:S(2)}, u32[]{:S(2)}) collective-permute-start(bf16[256,384]{1,0:T(8,128)(2,1)S(1)} %collective-permute-done.2.piece_ref.refs_2_), channel_id=1, source_target_pairs={{2,0},{4,2},{6,4},{7,6},{5,7},{3,5},{1,3},{0,1},{10,8},{12,10},{14... | collective-permute-start | bytes 589832 | tf_op jit(solution)/shard_map/ppermute | solution.py:218
  28.0 0.7 collective-permute-done.3.piece_ref.refs_3_
  28.7 5.3 %collective-permute-start.5 = (bf16[256,384]{1,0:T(8,128)(2,1)S(1)}, bf16[256,384]{1,0:T(8,128)(2,1)S(1)}, u32[]{:S(2)}, u32[]{:S(2)}) collective-permute-start(bf16[256,384]{1,0:T(8,128)(2,1)S(1)} %collective-permute-done.3.piece_ref.refs_3_), channel_id=1, source_target_pairs={{0,2},{2,4},{4,6},{6,7},{7,5},{5,3},{3,1},{1,0},{8,10},{10,12},{12... | collective-permute-start | bytes 589832 | tf_op jit(solution)/shard_map/ppermute | solution.py:217
  34.1 2.5 %collective-permute-done.4.piece_ref.refs_4_ = bf16[256,384]{1,0:T(8,128)(2,1)S(1)} collective-permute-done((bf16[256,384]{1,0:T(8,128)(2,1)S(1)}, bf16[256,384]{1,0:T(8,128)(2,1)S(1)}, u32[]{:S(2)}, u32[]{:S(2)}) %collective-permute-start.4) | collective-permute-done | bytes 196640 | tf_op jit(solution)/shard_map/ppermute | solution.py:218
  36.6 2.2 %collective-permute-start.6 = (bf16[256,384]{1,0:T(8,128)(2,1)S(1)}, bf16[256,384]{1,0:T(8,128)(2,1)S(1)}, u32[]{:S(2)}, u32[]{:S(2)}) collective-permute-start(bf16[256,384]{1,0:T(8,128)(2,1)S(1)} %collective-permute-done.4.piece_ref.refs_4_), channel_id=1, source_target_pairs={{2,0},{4,2},{6,4},{7,6},{5,7},{3,5},{1,3},{0,1},{10,8},{12,10},{14... | collective-permute-start | bytes 589832 | tf_op jit(solution)/shard_map/ppermute | solution.py:218
  38.8 0.0 collective-permute-done.5.piece_ref.refs_5_
  38.8 0.0 copy-start.11
  38.8 5.7 %collective-permute-start.7 = (bf16[256,384]{1,0:T(8,128)(2,1)S(1)}, bf16[256,384]{1,0:T(8,128)(2,1)S(1)}, u32[]{:S(2)}, u32[]{:S(2)}) collective-permute-start(bf16[256,384]{1,0:T(8,128)(2,1)S(1)} %collective-permute-done.5.piece_ref.refs_5_), channel_id=1, source_target_pairs={{0,2},{2,4},{4,6},{6,7},{7,5},{5,3},{3,1},{1,0},{8,10},{10,12},{12... | collective-permute-start | bytes 589832 | tf_op jit(solution)/shard_map/ppermute | solution.py:220
  44.6 0.7 dynamic-slice_bitcast_fusion.order_ref
  45.3 0.0 collective-permute-done.8.theirs_ref
  45.3 1.1 copy-done
  46.4 1.8 %add_term.8 = (bf16[1024,896]{1,0:T(8,128)(2,1)}, bf16[1024,384]{1,0:T(8,128)(2,1)S(1)}) custom-call(s32[8]{0:T(128)S(1)} %dynamic-slice_bitcast_fusion.order_ref, bf16[256,384]{1,0:T(8,128)(2,1)S(1)} %shard_map.78.piece_ref.refs_0_, bf16[384,896]{1,0:T(8,128)(2,1)S(1)} %copy-done, bf16[384,896]{1,0:T(8,128)(2,1)S(1)} %collective-permute-done.8.theirs_ref), custom_call_target="tpu_custom_call" | custom-call | flops 176160768 | bytes 1900544 | tf_op jit(solution)/shard_map/add_term/pallas_call | solution.py:118
  48.2 0.0 copy-done.1
  48.2 1.8 %add_term.9 = (bf16[1024,896]{1,0:T(8,128)(2,1)}, bf16[1024,384]{1,0:T(8,128)(2,1)S(1)}) custom-call(s32[8]{0:T(128)S(1)} %dynamic-slice_bitcast_fusion.order_ref, bf16[256,384]{1,0:T(8,128)(2,1)S(1)} %collective-permute-done.1.piece_ref.refs_1_, bf16[384,896]{1,0:T(8,128)(2,1)S(1)} %copy-done.1, ...), custom_call_target="tpu_custom_call", output_to_operand_aliasing={{0}: (4, {}), {1}: (5, {})} | custom-call | flops 176160768 | bytes 1900544 | tf_op jit(solution)/shard_map/add_term/pallas_call | solution.py:118
  50.1 0.0 copy-done.3
  50.1 1.8 %add_term.10 = (bf16[1024,896]{1,0:T(8,128)(2,1)}, bf16[1024,384]{1,0:T(8,128)(2,1)S(1)}) custom-call(s32[8]{0:T(128)S(1)} %dynamic-slice_bitcast_fusion.order_ref, bf16[256,384]{1,0:T(8,128)(2,1)S(1)} %collective-permute-done.2.piece_ref.refs_2_, bf16[384,896]{1,0:T(8,128)(2,1)S(1)} %copy-done.1, ...), custom_call_target="tpu_custom_call", output_to_operand_aliasing={{0}: (4, {}), {1}: (5, {})} | custom-call | flops 176160768 | bytes 1900544 | tf_op jit(solution)/shard_map/add_term/pallas_call | solution.py:118
  51.9 0.0 copy-done.7
  51.9 1.8 %add_term.11 = (bf16[1024,896]{1,0:T(8,128)(2,1)}, bf16[1024,384]{1,0:T(8,128)(2,1)S(1)}) custom-call(s32[8]{0:T(128)S(1)} %dynamic-slice_bitcast_fusion.order_ref, bf16[256,384]{1,0:T(8,128)(2,1)S(1)} %collective-permute-done.3.piece_ref.refs_3_, bf16[384,896]{1,0:T(8,128)(2,1)S(1)} %copy-done.1, ...), custom_call_target="tpu_custom_call", output_to_operand_aliasing={{0}: (4, {}), {1}: (5, {})} | custom-call | flops 176160768 | bytes 1900544 | tf_op jit(solution)/shard_map/add_term/pallas_call | solution.py:118
  53.8 1.8 %add_term.12 = (bf16[1024,896]{1,0:T(8,128)(2,1)}, bf16[1024,384]{1,0:T(8,128)(2,1)S(1)}) custom-call(s32[8]{0:T(128)S(1)} %dynamic-slice_bitcast_fusion.order_ref, bf16[256,384]{1,0:T(8,128)(2,1)S(1)} %collective-permute-done.4.piece_ref.refs_4_, bf16[384,896]{1,0:T(8,128)(2,1)S(1)} %copy-done.1, ...), custom_call_target="tpu_custom_call", output_to_operand_aliasing={{0}: (4, {}), {1}: (5, {})} | custom-call | flops 176160768 | bytes 1900544 | tf_op jit(solution)/shard_map/add_term/pallas_call | solution.py:118
  55.6 1.8 %add_term.13 = (bf16[1024,896]{1,0:T(8,128)(2,1)}, bf16[1024,384]{1,0:T(8,128)(2,1)S(1)}) custom-call(s32[8]{0:T(128)S(1)} %dynamic-slice_bitcast_fusion.order_ref, bf16[256,384]{1,0:T(8,128)(2,1)S(1)} %collective-permute-done.5.piece_ref.refs_5_, bf16[384,896]{1,0:T(8,128)(2,1)S(1)} %copy-done.1, ...), custom_call_target="tpu_custom_call", output_to_operand_aliasing={{0}: (4, {}), {1}: (5, {})} | custom-call | flops 176160768 | bytes 1900544 | tf_op jit(solution)/shard_map/add_term/pallas_call | solution.py:118
  57.5 0.0 collective-permute-done.6.piece_ref.refs_6_
  57.5 1.8 %add_term.14 = (bf16[1024,896]{1,0:T(8,128)(2,1)}, bf16[1024,384]{1,0:T(8,128)(2,1)S(1)}) custom-call(s32[8]{0:T(128)S(1)} %dynamic-slice_bitcast_fusion.order_ref, bf16[256,384]{1,0:T(8,128)(2,1)S(1)} %collective-permute-done.6.piece_ref.refs_6_, bf16[384,896]{1,0:T(8,128)(2,1)S(1)} %copy-done.1, ...), custom_call_target="tpu_custom_call", output_to_operand_aliasing={{0}: (4, {}), {1}: (5, {})} | custom-call | flops 176160768 | bytes 1900544 | tf_op jit(solution)/shard_map/add_term/pallas_call | solution.py:118
  59.3 0.0 collective-permute-done.7.piece_ref.refs_7_
  59.3 1.8 %add_term.15 = (bf16[1024,896]{1,0:T(8,128)(2,1)}, bf16[1024,384]{1,0:T(8,128)(2,1)S(1)}) custom-call(s32[8]{0:T(128)S(1)} %dynamic-slice_bitcast_fusion.order_ref, bf16[256,384]{1,0:T(8,128)(2,1)S(1)} %collective-permute-done.7.piece_ref.refs_7_, bf16[384,896]{1,0:T(8,128)(2,1)S(1)} %copy-done.1, ...), custom_call_target="tpu_custom_call", output_to_operand_aliasing={{0}: (4, {}), {1}: (5, {})} | custom-call | flops 176160768 | bytes 1900544 | tf_op jit(solution)/shard_map/add_term/pallas_call | solution.py:118
  61.2 17.8 %all-to-all-start = ((bf16[16,64,896]{2,1,0:T(8,128)(2,1)}), bf16[16,64,896]{2,1,0:T(8,128)(2,1)S(1)}, u32[]{:S(2)}, u32[]{:S(2)}) async-start(bf16[16,64,896]{2,1,0:T(8,128)(2,1)} %bitcast.3), calls=%async_computation | async-start | bytes 3670016 | tf_op jit(solution)/shard_map/all_to_all | solution.py:226
  79.0 0.0 copy-start.4
  79.1 2.1 %collective-permute-start.9 = (bf16[1024,384]{1,0:T(8,128)(2,1)S(1)}, bf16[1024,384]{1,0:T(8,128)(2,1)}, u32[]{:S(2)}, u32[]{:S(2)}) collective-permute-start(bf16[1024,384]{1,0:T(8,128)(2,1)S(1)} %get-tuple-element.38), channel_id=1, source_target_pairs={{0,8},{8,0},{1,9},{9,1},{2,10},{10,2},{3,11},{11,3},{4,12},{12,4},... | collective-permute-start | bytes 2359304 | tf_op jit(solution)/shard_map/ppermute | solution.py:207
  81.1 23.7 %all-to-all-done.in_ref = bf16[16,64,896]{2,1,0:T(8,128)(2,1)S(1)} async-done(((bf16[16,64,896]{2,1,0:T(8,128)(2,1)}), bf16[16,64,896]{2,1,0:T(8,128)(2,1)S(1)}, u32[]{:S(2)}, u32[]{:S(2)}) %all-to-all-start) | async-done | bytes 1835040 | tf_op jit(solution)/shard_map/all_to_all | solution.py:226
  104.9 0.2 shard_map.80
  105.1 2.1 %collective-permute-start.10 = (bf16[32,896]{1,0:T(8,128)(2,1)S(1)}, bf16[32,896]{1,0:T(8,128)(2,1)S(1)}, u32[]{:S(2)}, u32[]{:S(2)}) collective-permute-start(bf16[32,896]{1,0:T(8,128)(2,1)S(1)} %get-tuple-element.41), channel_id=1, source_target_pairs={{0,64},{64,0},{1,65},{65,1},{2,66},{66,2},{3,67},{67,3},{4,68},{68... | collective-permute-start | bytes 172040 | tf_op jit(solution)/shard_map/ppermute | solution.py:230
  107.2 0.0 collective-permute-done.9.refs_8_
  107.3 0.0 copy-start.2
  107.3 2.0 %copy-done.2 = bf16[2048,896]{1,0:T(8,128)(2,1)S(1)} copy-done((bf16[2048,896]{1,0:T(8,128)(2,1)S(1)}, bf16[2048,896]{1,0:T(8,128)(2,1)}, u32[]{:S(2)}) %copy-start.2) | copy-done | bytes 3670040
  109.3 4.0 %shard_map.79 = bf16[384,896]{1,0:T(8,128)(2,1)} custom-call(s32[8]{0:T(128)S(1)} %dynamic-slice_bitcast_fusion.order_ref, s32[1]{0:T(128)} %bitcast.1.core_ref, bf16[256,384]{1,0:T(8,128)(2,1)S(1)} %shard_map.78.piece_ref.refs_0_, bf16[256,384]{1,0:T(8,128)(2,1)S(1)} %copy-done.4, bf16[256,384]{1,0:T(8,128)(2,1)S(1)} %copy-done.6, ...), custom_call_target="tpu_custom_call" | custom-call | flops 1409286144 | bytes 7503872 | tf_op jit(solution)/shard_map/pallas_call | solution.py:36
  113.3 6.7 %collective-permute-done.10 = bf16[32,896]{1,0:T(8,128)(2,1)S(1)} collective-permute-done((bf16[32,896]{1,0:T(8,128)(2,1)S(1)}, bf16[32,896]{1,0:T(8,128)(2,1)S(1)}, u32[]{:S(2)}, u32[]{:S(2)}) %collective-permute-start.10) | collective-permute-done | bytes 57376 | tf_op jit(solution)/shard_map/ppermute | solution.py:230
  120.1 0.6 add_convert_fusion
  (28 shorter events, 0.1 us)
Async XLA Ops:
  1.3 0.9 copy-start.17
  2.2 0.7 copy-start.18
  3.2 3.2 %collective-permute-start = (bf16[128,384]{1,0:T(8,128)(2,1)S(1)}, bf16[128,384]{1,0:T(8,128)(2,1)S(1)}, u32[]{:S(2)}, u32[]{:S(2)}) collective-permute-start(bf16[128,384]{1,0:T(8,128)(2,1)S(1)} %get-tuple-element.23), channel_id=1, source_target_pairs={{0,8},{8,0},{1,9},{9,1},{2,10},{10,2},{3,11},{11,3},{4,12},{12,4},... | collective-permute-start | bytes 294920 | tf_op jit(solution)/shard_map/ppermute | solution.py:207
  6.4 12.1 %collective-permute-start.1 = (bf16[256,384]{1,0:T(8,128)(2,1)S(1)}, bf16[256,384]{1,0:T(8,128)(2,1)S(1)}, u32[]{:S(2)}, u32[]{:S(2)}) collective-permute-start(bf16[256,384]{1,0:T(8,128)(2,1)S(1)} %shard_map.78.piece_ref.refs_0_), channel_id=1, source_target_pairs={{0,2},{2,4},{4,6},{6,7},{7,5},{5,3},{3,1},{1,0},{8,10},{10,12},{12... | collective-permute-start | bytes 589832 | tf_op jit(solution)/shard_map/ppermute | solution.py:217
  12.8 32.5 %collective-permute-start.8 = (bf16[384,896]{1,0:T(8,128)(2,1)}, bf16[384,896]{1,0:T(8,128)(2,1)S(1)}, u32[]{:S(2)}, u32[]{:S(2)}) collective-permute-start(bf16[384,896]{1,0:T(8,128)(2,1)} %hid_ref.15), channel_id=1, source_target_pairs={{0,8},{8,0},{1,9},{9,1},{2,10},{10,2},{3,11},{11,3},{4,12},{12,4},... | collective-permute-start | bytes 2064392 | tf_op jit(solution)/shard_map/ppermute | solution.py:207
  14.7 11.4 %collective-permute-start.2 = (bf16[256,384]{1,0:T(8,128)(2,1)S(1)}, bf16[256,384]{1,0:T(8,128)(2,1)S(1)}, u32[]{:S(2)}, u32[]{:S(2)}) collective-permute-start(bf16[256,384]{1,0:T(8,128)(2,1)S(1)} %shard_map.78.piece_ref.refs_0_), channel_id=1, source_target_pairs={{2,0},{4,2},{6,4},{7,6},{5,7},{3,5},{1,3},{0,1},{10,8},{12,10},{14... | collective-permute-start | bytes 589832 | tf_op jit(solution)/shard_map/ppermute | solution.py:218
  18.5 31.6 %copy-start.3 = (bf16[256,384]{1,0:T(8,128)(2,1)}, bf16[256,384]{1,0:T(8,128)(2,1)S(1)}, u32[]{:S(2)}) copy-start(bf16[256,384]{1,0:T(8,128)(2,1)S(1)} %collective-permute-done.1.piece_ref.refs_1_) | copy-start | bytes 589828
  18.5 10.2 %collective-permute-start.3 = (bf16[256,384]{1,0:T(8,128)(2,1)S(1)}, bf16[256,384]{1,0:T(8,128)(2,1)S(1)}, u32[]{:S(2)}, u32[]{:S(2)}) collective-permute-start(bf16[256,384]{1,0:T(8,128)(2,1)S(1)} %collective-permute-done.1.piece_ref.refs_1_), channel_id=1, source_target_pairs={{0,2},{2,4},{4,6},{6,7},{7,5},{5,3},{3,1},{1,0},{8,10},{10,12},{12... | collective-permute-start | bytes 589832 | tf_op jit(solution)/shard_map/ppermute | solution.py:217
  26.1 24.0 %copy-start.5 = (bf16[256,384]{1,0:T(8,128)(2,1)}, bf16[256,384]{1,0:T(8,128)(2,1)S(1)}, u32[]{:S(2)}) copy-start(bf16[256,384]{1,0:T(8,128)(2,1)S(1)} %collective-permute-done.2.piece_ref.refs_2_) | copy-start | bytes 589828
  26.1 10.5 %collective-permute-start.4 = (bf16[256,384]{1,0:T(8,128)(2,1)S(1)}, bf16[256,384]{1,0:T(8,128)(2,1)S(1)}, u32[]{:S(2)}, u32[]{:S(2)}) collective-permute-start(bf16[256,384]{1,0:T(8,128)(2,1)S(1)} %collective-permute-done.2.piece_ref.refs_2_), channel_id=1, source_target_pairs={{2,0},{4,2},{6,4},{7,6},{5,7},{3,5},{1,3},{0,1},{10,8},{12,10},{14... | collective-permute-start | bytes 589832 | tf_op jit(solution)/shard_map/ppermute | solution.py:218
  28.7 23.2 %copy-start.7 = (bf16[256,384]{1,0:T(8,128)(2,1)}, bf16[256,384]{1,0:T(8,128)(2,1)S(1)}, u32[]{:S(2)}) copy-start(bf16[256,384]{1,0:T(8,128)(2,1)S(1)} %collective-permute-done.3.piece_ref.refs_3_) | copy-start | bytes 589828
  28.7 10.1 %collective-permute-start.5 = (bf16[256,384]{1,0:T(8,128)(2,1)S(1)}, bf16[256,384]{1,0:T(8,128)(2,1)S(1)}, u32[]{:S(2)}, u32[]{:S(2)}) collective-permute-start(bf16[256,384]{1,0:T(8,128)(2,1)S(1)} %collective-permute-done.3.piece_ref.refs_3_), channel_id=1, source_target_pairs={{0,2},{2,4},{4,6},{6,7},{7,5},{5,3},{3,1},{1,0},{8,10},{10,12},{12... | collective-permute-start | bytes 589832 | tf_op jit(solution)/shard_map/ppermute | solution.py:217
  36.6 17.2 %copy-start.9 = (bf16[256,384]{1,0:T(8,128)(2,1)}, bf16[256,384]{1,0:T(8,128)(2,1)S(1)}, u32[]{:S(2)}) copy-start(bf16[256,384]{1,0:T(8,128)(2,1)S(1)} %collective-permute-done.4.piece_ref.refs_4_) | copy-start | bytes 589828
  36.6 20.9 %collective-permute-start.6 = (bf16[256,384]{1,0:T(8,128)(2,1)S(1)}, bf16[256,384]{1,0:T(8,128)(2,1)S(1)}, u32[]{:S(2)}, u32[]{:S(2)}) collective-permute-start(bf16[256,384]{1,0:T(8,128)(2,1)S(1)} %collective-permute-done.4.piece_ref.refs_4_), channel_id=1, source_target_pairs={{2,0},{4,2},{6,4},{7,6},{5,7},{3,5},{1,3},{0,1},{10,8},{12,10},{14... | collective-permute-start | bytes 589832 | tf_op jit(solution)/shard_map/ppermute | solution.py:218
  38.8 16.8 %copy-start.11 = (bf16[256,384]{1,0:T(8,128)(2,1)}, bf16[256,384]{1,0:T(8,128)(2,1)S(1)}, u32[]{:S(2)}) copy-start(bf16[256,384]{1,0:T(8,128)(2,1)S(1)} %collective-permute-done.5.piece_ref.refs_5_) | copy-start | bytes 589828
  38.8 20.5 %collective-permute-start.7 = (bf16[256,384]{1,0:T(8,128)(2,1)S(1)}, bf16[256,384]{1,0:T(8,128)(2,1)S(1)}, u32[]{:S(2)}, u32[]{:S(2)}) collective-permute-start(bf16[256,384]{1,0:T(8,128)(2,1)S(1)} %collective-permute-done.5.piece_ref.refs_5_), channel_id=1, source_target_pairs={{0,2},{2,4},{4,6},{6,7},{7,5},{5,3},{3,1},{1,0},{8,10},{10,12},{12... | collective-permute-start | bytes 589832 | tf_op jit(solution)/shard_map/ppermute | solution.py:220
  45.3 1.1 copy-start
  46.4 1.8 %copy-start.1 = (bf16[384,896]{1,0:T(8,128)(2,1)S(1)}, bf16[384,896]{1,0:T(8,128)(2,1)}, u32[]{:S(2)}) copy-start(bf16[384,896]{1,0:T(8,128)(2,1)} %hid_ref.15) | copy-start | bytes 2064388
  57.5 1.8 %copy-start.13 = (bf16[256,384]{1,0:T(8,128)(2,1)}, bf16[256,384]{1,0:T(8,128)(2,1)S(1)}, u32[]{:S(2)}) copy-start(bf16[256,384]{1,0:T(8,128)(2,1)S(1)} %collective-permute-done.6.piece_ref.refs_6_) | copy-start | bytes 589828
  59.3 1.9 %copy-start.15 = (bf16[256,384]{1,0:T(8,128)(2,1)}, bf16[256,384]{1,0:T(8,128)(2,1)S(1)}, u32[]{:S(2)}) copy-start(bf16[256,384]{1,0:T(8,128)(2,1)S(1)} %collective-permute-done.7.piece_ref.refs_7_) | copy-start | bytes 589828
  61.2 43.7 %all-to-all-start = ((bf16[16,64,896]{2,1,0:T(8,128)(2,1)}), bf16[16,64,896]{2,1,0:T(8,128)(2,1)S(1)}, u32[]{:S(2)}, u32[]{:S(2)}) async-start(bf16[16,64,896]{2,1,0:T(8,128)(2,1)} %bitcast.3), calls=%async_computation | async-start | bytes 3670016 | tf_op jit(solution)/shard_map/all_to_all | solution.py:226
  79.0 28.2 %copy-start.4 = (bf16[256,384]{1,0:T(8,128)(2,1)S(1)}, bf16[256,384]{1,0:T(8,128)(2,1)}, u32[]{:S(2)}) copy-start(bf16[256,384]{1,0:T(8,128)(2,1)} %copy-done.3) | copy-start | bytes 589828
  79.1 28.2 %copy-start.6 = (bf16[256,384]{1,0:T(8,128)(2,1)S(1)}, bf16[256,384]{1,0:T(8,128)(2,1)}, u32[]{:S(2)}) copy-start(bf16[256,384]{1,0:T(8,128)(2,1)} %copy-done.5) | copy-start | bytes 589828
  79.1 28.2 %copy-start.8 = (bf16[256,384]{1,0:T(8,128)(2,1)S(1)}, bf16[256,384]{1,0:T(8,128)(2,1)}, u32[]{:S(2)}) copy-start(bf16[256,384]{1,0:T(8,128)(2,1)} %copy-done.7) | copy-start | bytes 589828
  79.1 28.1 %collective-permute-start.9 = (bf16[1024,384]{1,0:T(8,128)(2,1)S(1)}, bf16[1024,384]{1,0:T(8,128)(2,1)}, u32[]{:S(2)}, u32[]{:S(2)}) collective-permute-start(bf16[1024,384]{1,0:T(8,128)(2,1)S(1)} %get-tuple-element.38), channel_id=1, source_target_pairs={{0,8},{8,0},{1,9},{9,1},{2,10},{10,2},{3,11},{11,3},{4,12},{12,4},... | collective-permute-start | bytes 2359304 | tf_op jit(solution)/shard_map/ppermute | solution.py:207
  104.9 2.4 %copy-start.10 = (bf16[256,384]{1,0:T(8,128)(2,1)S(1)}, bf16[256,384]{1,0:T(8,128)(2,1)}, u32[]{:S(2)}) copy-start(bf16[256,384]{1,0:T(8,128)(2,1)} %copy-done.9) | copy-start | bytes 589828
  104.9 2.4 %copy-start.12 = (bf16[256,384]{1,0:T(8,128)(2,1)S(1)}, bf16[256,384]{1,0:T(8,128)(2,1)}, u32[]{:S(2)}) copy-start(bf16[256,384]{1,0:T(8,128)(2,1)} %copy-done.11) | copy-start | bytes 589828
  104.9 2.4 %copy-start.14 = (bf16[256,384]{1,0:T(8,128)(2,1)S(1)}, bf16[256,384]{1,0:T(8,128)(2,1)}, u32[]{:S(2)}) copy-start(bf16[256,384]{1,0:T(8,128)(2,1)} %copy-done.13) | copy-start | bytes 589828
  104.9 2.4 %copy-start.16 = (bf16[256,384]{1,0:T(8,128)(2,1)S(1)}, bf16[256,384]{1,0:T(8,128)(2,1)}, u32[]{:S(2)}) copy-start(bf16[256,384]{1,0:T(8,128)(2,1)} %copy-done.15) | copy-start | bytes 589828
  105.1 14.9 %collective-permute-start.10 = (bf16[32,896]{1,0:T(8,128)(2,1)S(1)}, bf16[32,896]{1,0:T(8,128)(2,1)S(1)}, u32[]{:S(2)}, u32[]{:S(2)}) collective-permute-start(bf16[32,896]{1,0:T(8,128)(2,1)S(1)} %get-tuple-element.41), channel_id=1, source_target_pairs={{0,64},{64,0},{1,65},{65,1},{2,66},{66,2},{3,67},{67,3},{4,68},{68... | collective-permute-start | bytes 172040 | tf_op jit(solution)/shard_map/ppermute | solution.py:230
  107.3 2.0 %copy-start.2 = (bf16[2048,896]{1,0:T(8,128)(2,1)S(1)}, bf16[2048,896]{1,0:T(8,128)(2,1)}, u32[]{:S(2)}) copy-start(bf16[2048,896]{1,0:T(8,128)(2,1)} %refs_9_.1) | copy-start | bytes 11010052

commit v5 on v4

--- a/solution.py
+++ b/solution.py
@@ -11,9 +11,9 @@
 
 GRP = ("y", "zh", "x", "core")
 RING = (0, 2, 4, 6, 7, 5, 3, 1)
-CW = [(RING[i], RING[(i + 1) % 8]) for i in range(8)]
+CW = [(RING[(i + 1) % 8], RING[i]) for i in range(8)]
 CCW = [(b, a) for a, b in CW]
-SHIFTS = (0, -1, 1, -2, 2, -3, 3, 4)
+SHIFTS = (0, 1, -1, 2, -2, 3, -3, 4)
 ORDER = np.array(
     [[RING[(RING.index(n) + s) % 8] for s in SHIFTS] for n in range(8)], np.int32
 )
@@ -100,7 +100,7 @@
     owner = order_ref[k]
     copies = []
     for x in range(4):
-        block = (lax.div(owner, 2) * 4 + x) * 2 + lax.rem(owner, 2)
+        block = (x * 4 + lax.div(owner, 2)) * 2 + lax.rem(owner, 2)
         at = pl.multiple_of(block * 32, 32)
         copies.append(
             pltpu.make_async_copy(
@@ -223,7 +223,7 @@
     for k, piece in enumerate(pieces):
         state = add_term(k, order, piece, hidden, hidden_theirs, state)
     term, sent = state
-    parts = lax.all_to_all(term.reshape(16, 64, units), ("y", "x"), 0, 0, tiled=True)
+    parts = lax.all_to_all(term.reshape(16, 64, units), ("x", "y"), 0, 0, tiled=True)
     theirs = swap(sent)
     grad_hidden = hidden_grads(order, core, pieces, theirs, w_down)
     keep, cross = plane_sums(zh, parts)

time: 121 us -> 112 us (0.926)
  starting transfers between devices: 55.2 us -> 46.1 us
    all_to_all x1, starting transfers between devices: 17.8 us -> 7.71 us  [body(): lax.all_to_all(term.reshape(16, 64, units), ('x', 'y'), 0, 0, tiled=True)]
    ppermute x1, starting transfers between devices: 2.05 us -> 7.66 us  [body(): far = lax.ppermute(cross, 'zh', [(0, 1), (1, 0)])]
    ppermute x1, waiting for transfers between devices: 6.75 us -> 1.2 us  [body(): far = lax.ppermute(cross, 'zh', [(0, 1), (1, 0)])]
    ppermute x3, waiting for transfers between devices: 1.91 us -> 6.59 us  [body(): forward = lax.ppermute(forward, 'node', CW)]
    ppermute x1, starting transfers between devices: 5.74 us -> 1.91 us  [body(): pieces.append(lax.ppermute(forward, 'node', CW))]
    ppermute x3, starting transfers between devices: 17 us -> 14 us  [body(): forward = lax.ppermute(forward, 'node', CW)]
    ppermute x3, starting transfers between devices: 6.69 us -> 9 us  [body(): backward = lax.ppermute(backward, 'node', CCW)]
  transfers between devices with their start and end apart: 12 -> 12, of which waited for: 7 -> 8; matrix products, arithmetic and copies ran while one was open for 1% -> 1% of each run, Pallas kernels for 14% -> 15%
where the time goes in v5:
time: 112 us; the launch traced here: 111 us
  starting transfers between devices  46.1 us (41%)
  waiting for transfers between devices  38.3 us (34%)
  Pallas kernels  19.1 us (17%)
  local copies, waits for them, and re-layouts  5.49 us (5%)
  between operations  1.67 us (1%)
    all_to_all x1, waiting for transfers between devices, body(): lax.all_to_all(term.reshape(16, 64, units), ('x', 'y'), 0, 0, tiled=True)  24.7 us
    pallas_call x8, Pallas kernels, add_term(): pl.pallas_call(functools.partial(term_kernel, k), in_specs=[smem(), vmem(...  14.6 us
    ppermute x3, starting transfers between devices, body(): forward = lax.ppermute(forward, 'node', CW)  14 us
    ppermute x3, starting transfers between devices, body(): backward = lax.ppermute(backward, 'node', CCW)  9 us
    all_to_all x1, starting transfers between devices, body(): lax.all_to_all(term.reshape(16, 64, units), ('x', 'y'), 0, 0, tiled=True)  7.71 us
    ppermute x1, starting transfers between devices, body(): far = lax.ppermute(cross, 'zh', [(0, 1), (1, 0)])  7.66 us
    ppermute x3, waiting for transfers between devices, body(): forward = lax.ppermute(forward, 'node', CW)  6.59 us
    ppermute x3, starting transfers between devices, swap(): return lax.ppermute(value, 'core', [(0, 1), (1, 0)])  5.9 us
  transfers between devices with their start and end apart: 12, of which 8 were waited for; matrix products, arithmetic and copies ran while one was open for 1% of the time, Pallas kernels for 15%

profile of v5, /device:TPU:64, one launch (start us, length us, event | category | flops | bytes accessed | tf_op | source)
XLA Modules:
  0.0 111.4 jit_solution(14517513107244274283)
XLA Ops:
  1.3 0.0 copy-start.17
  1.3 0.9 copy-done.17
  2.2 0.7 copy-done.18
  2.9 0.3 shard_map.77
  3.2 1.9 %collective-permute-start = (bf16[128,384]{1,0:T(8,128)(2,1)S(1)}, bf16[128,384]{1,0:T(8,128)(2,1)S(1)}, u32[]{:S(2)}, u32[]{:S(2)}) collective-permute-start(bf16[128,384]{1,0:T(8,128)(2,1)S(1)} %get-tuple-element.23), channel_id=1, source_target_pairs={{0,8},{8,0},{1,9},{9,1},{2,10},{10,2},{3,11},{11,3},{4,12},{12,4},... | collective-permute-start | bytes 294920 | tf_op jit(solution)/shard_map/ppermute | solution.py:207
  5.1 1.3 %collective-permute-done.theirs_ref = bf16[128,384]{1,0:T(8,128)(2,1)S(1)} collective-permute-done((bf16[128,384]{1,0:T(8,128)(2,1)S(1)}, bf16[128,384]{1,0:T(8,128)(2,1)S(1)}, u32[]{:S(2)}, u32[]{:S(2)}) %collective-permute-start) | collective-permute-done | bytes 98336 | tf_op jit(solution)/shard_map/ppermute | solution.py:207
  6.4 6.9 %collective-permute-start.1 = (bf16[256,384]{1,0:T(8,128)(2,1)S(1)}, bf16[256,384]{1,0:T(8,128)(2,1)S(1)}, u32[]{:S(2)}, u32[]{:S(2)}) collective-permute-start(bf16[256,384]{1,0:T(8,128)(2,1)S(1)} %shard_map.78.piece_ref.refs_0_), channel_id=1, source_target_pairs={{2,0},{4,2},{6,4},{7,6},{5,7},{3,5},{1,3},{0,1},{10,8},{12,10},{14... | collective-permute-start | bytes 589832 | tf_op jit(solution)/shard_map/ppermute | solution.py:217
  13.3 1.9 %collective-permute-start.8 = (bf16[384,896]{1,0:T(8,128)(2,1)}, bf16[384,896]{1,0:T(8,128)(2,1)S(1)}, u32[]{:S(2)}, u32[]{:S(2)}) collective-permute-start(bf16[384,896]{1,0:T(8,128)(2,1)} %hid_ref.15), channel_id=1, source_target_pairs={{0,8},{8,0},{1,9},{9,1},{2,10},{10,2},{3,11},{11,3},{4,12},{12,4},... | collective-permute-start | bytes 2064392 | tf_op jit(solution)/shard_map/ppermute | solution.py:207
  15.2 1.9 %collective-permute-start.2 = (bf16[256,384]{1,0:T(8,128)(2,1)S(1)}, bf16[256,384]{1,0:T(8,128)(2,1)S(1)}, u32[]{:S(2)}, u32[]{:S(2)}) collective-permute-start(bf16[256,384]{1,0:T(8,128)(2,1)S(1)} %shard_map.78.piece_ref.refs_0_), channel_id=1, source_target_pairs={{0,2},{2,4},{4,6},{6,7},{7,5},{5,3},{3,1},{1,0},{8,10},{10,12},{12... | collective-permute-start | bytes 589832 | tf_op jit(solution)/shard_map/ppermute | solution.py:218
  17.1 0.8 collective-permute-done.1.piece_ref.refs_1_
  18.0 5.1 %collective-permute-start.3 = (bf16[256,384]{1,0:T(8,128)(2,1)S(1)}, bf16[256,384]{1,0:T(8,128)(2,1)S(1)}, u32[]{:S(2)}, u32[]{:S(2)}) collective-permute-start(bf16[256,384]{1,0:T(8,128)(2,1)S(1)} %collective-permute-done.1.piece_ref.refs_1_), channel_id=1, source_target_pairs={{2,0},{4,2},{6,4},{7,6},{5,7},{3,5},{1,3},{0,1},{10,8},{12,10},{14... | collective-permute-start | bytes 589832 | tf_op jit(solution)/shard_map/ppermute | solution.py:217
  23.1 2.7 %collective-permute-done.2.piece_ref.refs_2_ = bf16[256,384]{1,0:T(8,128)(2,1)S(1)} collective-permute-done((bf16[256,384]{1,0:T(8,128)(2,1)S(1)}, bf16[256,384]{1,0:T(8,128)(2,1)S(1)}, u32[]{:S(2)}, u32[]{:S(2)}) %collective-permute-start.2) | collective-permute-done | bytes 196640 | tf_op jit(solution)/shard_map/ppermute | solution.py:218
  25.8 2.9 %collective-permute-start.4 = (bf16[256,384]{1,0:T(8,128)(2,1)S(1)}, bf16[256,384]{1,0:T(8,128)(2,1)S(1)}, u32[]{:S(2)}, u32[]{:S(2)}) collective-permute-start(bf16[256,384]{1,0:T(8,128)(2,1)S(1)} %collective-permute-done.2.piece_ref.refs_2_), channel_id=1, source_target_pairs={{0,2},{2,4},{4,6},{6,7},{7,5},{5,3},{3,1},{1,0},{8,10},{10,12},{12... | collective-permute-start | bytes 589832 | tf_op jit(solution)/shard_map/ppermute | solution.py:218
  28.7 2.9 %collective-permute-done.3.piece_ref.refs_3_ = bf16[256,384]{1,0:T(8,128)(2,1)S(1)} collective-permute-done((bf16[256,384]{1,0:T(8,128)(2,1)S(1)}, bf16[256,384]{1,0:T(8,128)(2,1)S(1)}, u32[]{:S(2)}, u32[]{:S(2)}) %collective-permute-start.3) | collective-permute-done | bytes 196640 | tf_op jit(solution)/shard_map/ppermute | solution.py:217
  31.7 1.9 %collective-permute-start.5 = (bf16[256,384]{1,0:T(8,128)(2,1)S(1)}, bf16[256,384]{1,0:T(8,128)(2,1)S(1)}, u32[]{:S(2)}, u32[]{:S(2)}) collective-permute-start(bf16[256,384]{1,0:T(8,128)(2,1)S(1)} %collective-permute-done.3.piece_ref.refs_3_), channel_id=1, source_target_pairs={{2,0},{4,2},{6,4},{7,6},{5,7},{3,5},{1,3},{0,1},{10,8},{12,10},{14... | collective-permute-start | bytes 589832 | tf_op jit(solution)/shard_map/ppermute | solution.py:217
  33.6 1.9 %collective-permute-done.4.piece_ref.refs_4_ = bf16[256,384]{1,0:T(8,128)(2,1)S(1)} collective-permute-done((bf16[256,384]{1,0:T(8,128)(2,1)S(1)}, bf16[256,384]{1,0:T(8,128)(2,1)S(1)}, u32[]{:S(2)}, u32[]{:S(2)}) %collective-permute-start.4) | collective-permute-done | bytes 196640 | tf_op jit(solution)/shard_map/ppermute | solution.py:218
  35.5 4.2 %collective-permute-start.6 = (bf16[256,384]{1,0:T(8,128)(2,1)S(1)}, bf16[256,384]{1,0:T(8,128)(2,1)S(1)}, u32[]{:S(2)}, u32[]{:S(2)}) collective-permute-start(bf16[256,384]{1,0:T(8,128)(2,1)S(1)} %collective-permute-done.4.piece_ref.refs_4_), channel_id=1, source_target_pairs={{0,2},{2,4},{4,6},{6,7},{7,5},{5,3},{3,1},{1,0},{8,10},{10,12},{12... | collective-permute-start | bytes 589832 | tf_op jit(solution)/shard_map/ppermute | solution.py:218
  39.7 2.8 %collective-permute-done.5.piece_ref.refs_5_ = bf16[256,384]{1,0:T(8,128)(2,1)S(1)} collective-permute-done((bf16[256,384]{1,0:T(8,128)(2,1)S(1)}, bf16[256,384]{1,0:T(8,128)(2,1)S(1)}, u32[]{:S(2)}, u32[]{:S(2)}) %collective-permute-start.5) | collective-permute-done | bytes 196640 | tf_op jit(solution)/shard_map/ppermute | solution.py:217
  42.5 1.9 %collective-permute-start.7 = (bf16[256,384]{1,0:T(8,128)(2,1)S(1)}, bf16[256,384]{1,0:T(8,128)(2,1)S(1)}, u32[]{:S(2)}, u32[]{:S(2)}) collective-permute-start(bf16[256,384]{1,0:T(8,128)(2,1)S(1)} %collective-permute-done.5.piece_ref.refs_5_), channel_id=1, source_target_pairs={{2,0},{4,2},{6,4},{7,6},{5,7},{3,5},{1,3},{0,1},{10,8},{12,10},{14... | collective-permute-start | bytes 589832 | tf_op jit(solution)/shard_map/ppermute | solution.py:220
  44.4 0.7 dynamic-slice_bitcast_fusion.order_ref
  45.1 0.0 collective-permute-done.8.theirs_ref
  45.1 1.1 copy-done
  46.2 1.8 %add_term.8 = (bf16[1024,896]{1,0:T(8,128)(2,1)}, bf16[1024,384]{1,0:T(8,128)(2,1)S(1)}) custom-call(s32[8]{0:T(128)S(1)} %dynamic-slice_bitcast_fusion.order_ref, bf16[256,384]{1,0:T(8,128)(2,1)S(1)} %shard_map.78.piece_ref.refs_0_, bf16[384,896]{1,0:T(8,128)(2,1)S(1)} %copy-done, bf16[384,896]{1,0:T(8,128)(2,1)S(1)} %collective-permute-done.8.theirs_ref), custom_call_target="tpu_custom_call" | custom-call | flops 176160768 | bytes 1900544 | tf_op jit(solution)/shard_map/add_term/pallas_call | solution.py:118
  48.1 0.0 copy-done.1
  48.1 1.8 %add_term.9 = (bf16[1024,896]{1,0:T(8,128)(2,1)}, bf16[1024,384]{1,0:T(8,128)(2,1)S(1)}) custom-call(s32[8]{0:T(128)S(1)} %dynamic-slice_bitcast_fusion.order_ref, bf16[256,384]{1,0:T(8,128)(2,1)S(1)} %collective-permute-done.1.piece_ref.refs_1_, bf16[384,896]{1,0:T(8,128)(2,1)S(1)} %copy-done.1, ...), custom_call_target="tpu_custom_call", output_to_operand_aliasing={{0}: (4, {}), {1}: (5, {})} | custom-call | flops 176160768 | bytes 1900544 | tf_op jit(solution)/shard_map/add_term/pallas_call | solution.py:118
  49.9 1.8 %add_term.10 = (bf16[1024,896]{1,0:T(8,128)(2,1)}, bf16[1024,384]{1,0:T(8,128)(2,1)S(1)}) custom-call(s32[8]{0:T(128)S(1)} %dynamic-slice_bitcast_fusion.order_ref, bf16[256,384]{1,0:T(8,128)(2,1)S(1)} %collective-permute-done.2.piece_ref.refs_2_, bf16[384,896]{1,0:T(8,128)(2,1)S(1)} %copy-done.1, ...), custom_call_target="tpu_custom_call", output_to_operand_aliasing={{0}: (4, {}), {1}: (5, {})} | custom-call | flops 176160768 | bytes 1900544 | tf_op jit(solution)/shard_map/add_term/pallas_call | solution.py:118
  51.8 1.8 %add_term.11 = (bf16[1024,896]{1,0:T(8,128)(2,1)}, bf16[1024,384]{1,0:T(8,128)(2,1)S(1)}) custom-call(s32[8]{0:T(128)S(1)} %dynamic-slice_bitcast_fusion.order_ref, bf16[256,384]{1,0:T(8,128)(2,1)S(1)} %collective-permute-done.3.piece_ref.refs_3_, bf16[384,896]{1,0:T(8,128)(2,1)S(1)} %copy-done.1, ...), custom_call_target="tpu_custom_call", output_to_operand_aliasing={{0}: (4, {}), {1}: (5, {})} | custom-call | flops 176160768 | bytes 1900544 | tf_op jit(solution)/shard_map/add_term/pallas_call | solution.py:118
  53.6 1.8 %add_term.12 = (bf16[1024,896]{1,0:T(8,128)(2,1)}, bf16[1024,384]{1,0:T(8,128)(2,1)S(1)}) custom-call(s32[8]{0:T(128)S(1)} %dynamic-slice_bitcast_fusion.order_ref, bf16[256,384]{1,0:T(8,128)(2,1)S(1)} %collective-permute-done.4.piece_ref.refs_4_, bf16[384,896]{1,0:T(8,128)(2,1)S(1)} %copy-done.1, ...), custom_call_target="tpu_custom_call", output_to_operand_aliasing={{0}: (4, {}), {1}: (5, {})} | custom-call | flops 176160768 | bytes 1900544 | tf_op jit(solution)/shard_map/add_term/pallas_call | solution.py:118
  55.5 1.8 %add_term.13 = (bf16[1024,896]{1,0:T(8,128)(2,1)}, bf16[1024,384]{1,0:T(8,128)(2,1)S(1)}) custom-call(s32[8]{0:T(128)S(1)} %dynamic-slice_bitcast_fusion.order_ref, bf16[256,384]{1,0:T(8,128)(2,1)S(1)} %collective-permute-done.5.piece_ref.refs_5_, bf16[384,896]{1,0:T(8,128)(2,1)S(1)} %copy-done.1, ...), custom_call_target="tpu_custom_call", output_to_operand_aliasing={{0}: (4, {}), {1}: (5, {})} | custom-call | flops 176160768 | bytes 1900544 | tf_op jit(solution)/shard_map/add_term/pallas_call | solution.py:118
  57.3 0.0 collective-permute-done.6.piece_ref.refs_6_
  57.3 1.8 %add_term.14 = (bf16[1024,896]{1,0:T(8,128)(2,1)}, bf16[1024,384]{1,0:T(8,128)(2,1)S(1)}) custom-call(s32[8]{0:T(128)S(1)} %dynamic-slice_bitcast_fusion.order_ref, bf16[256,384]{1,0:T(8,128)(2,1)S(1)} %collective-permute-done.6.piece_ref.refs_6_, bf16[384,896]{1,0:T(8,128)(2,1)S(1)} %copy-done.1, ...), custom_call_target="tpu_custom_call", output_to_operand_aliasing={{0}: (4, {}), {1}: (5, {})} | custom-call | flops 176160768 | bytes 1900544 | tf_op jit(solution)/shard_map/add_term/pallas_call | solution.py:118
  59.2 0.0 collective-permute-done.7.piece_ref.refs_7_
  59.2 1.8 %add_term.15 = (bf16[1024,896]{1,0:T(8,128)(2,1)}, bf16[1024,384]{1,0:T(8,128)(2,1)S(1)}) custom-call(s32[8]{0:T(128)S(1)} %dynamic-slice_bitcast_fusion.order_ref, bf16[256,384]{1,0:T(8,128)(2,1)S(1)} %collective-permute-done.7.piece_ref.refs_7_, bf16[384,896]{1,0:T(8,128)(2,1)S(1)} %copy-done.1, ...), custom_call_target="tpu_custom_call", output_to_operand_aliasing={{0}: (4, {}), {1}: (5, {})} | custom-call | flops 176160768 | bytes 1900544 | tf_op jit(solution)/shard_map/add_term/pallas_call | solution.py:118
  61.0 0.0 copy-done.15
  61.0 7.7 %all-to-all-start = ((bf16[16,64,896]{2,1,0:T(8,128)(2,1)}), bf16[16,64,896]{2,1,0:T(8,128)(2,1)S(1)}, u32[]{:S(2)}, u32[]{:S(2)}) async-start(bf16[16,64,896]{2,1,0:T(8,128)(2,1)} %bitcast.3), calls=%async_computation | async-start | bytes 3670016 | tf_op jit(solution)/shard_map/all_to_all | solution.py:226
  68.8 0.0 copy-start.4
  68.8 0.0 copy-start.6
  68.8 0.0 copy-start.8
  68.8 2.1 %collective-permute-start.9 = (bf16[1024,384]{1,0:T(8,128)(2,1)S(1)}, bf16[1024,384]{1,0:T(8,128)(2,1)}, u32[]{:S(2)}, u32[]{:S(2)}) collective-permute-start(bf16[1024,384]{1,0:T(8,128)(2,1)S(1)} %get-tuple-element.38), channel_id=1, source_target_pairs={{0,8},{8,0},{1,9},{9,1},{2,10},{10,2},{3,11},{11,3},{4,12},{12,4},... | collective-permute-start | bytes 2359304 | tf_op jit(solution)/shard_map/ppermute | solution.py:207
  70.9 24.7 %all-to-all-done.in_ref = bf16[16,64,896]{2,1,0:T(8,128)(2,1)S(1)} async-done(((bf16[16,64,896]{2,1,0:T(8,128)(2,1)}), bf16[16,64,896]{2,1,0:T(8,128)(2,1)S(1)}, u32[]{:S(2)}, u32[]{:S(2)}) %all-to-all-start) | async-done | bytes 1835040 | tf_op jit(solution)/shard_map/all_to_all | solution.py:226
  95.6 0.2 shard_map.80
  95.8 7.7 %collective-permute-start.10 = (bf16[32,896]{1,0:T(8,128)(2,1)S(1)}, bf16[32,896]{1,0:T(8,128)(2,1)S(1)}, u32[]{:S(2)}, u32[]{:S(2)}) collective-permute-start(bf16[32,896]{1,0:T(8,128)(2,1)S(1)} %get-tuple-element.41), channel_id=1, source_target_pairs={{0,64},{64,0},{1,65},{65,1},{2,66},{66,2},{3,67},{67,3},{4,68},{68... | collective-permute-start | bytes 172040 | tf_op jit(solution)/shard_map/ppermute | solution.py:230
  103.5 0.0 collective-permute-done.9.refs_8_
  103.6 0.0 copy-start.2
  103.6 2.0 %copy-done.2 = bf16[2048,896]{1,0:T(8,128)(2,1)S(1)} copy-done((bf16[2048,896]{1,0:T(8,128)(2,1)S(1)}, bf16[2048,896]{1,0:T(8,128)(2,1)}, u32[]{:S(2)}) %copy-start.2) | copy-done | bytes 3670040
  105.6 4.0 %shard_map.79 = bf16[384,896]{1,0:T(8,128)(2,1)} custom-call(s32[8]{0:T(128)S(1)} %dynamic-slice_bitcast_fusion.order_ref, s32[1]{0:T(128)} %bitcast.1.core_ref, bf16[256,384]{1,0:T(8,128)(2,1)S(1)} %shard_map.78.piece_ref.refs_0_, bf16[256,384]{1,0:T(8,128)(2,1)S(1)} %copy-done.4, bf16[256,384]{1,0:T(8,128)(2,1)S(1)} %copy-done.6, ...), custom_call_target="tpu_custom_call" | custom-call | flops 1409286144 | bytes 7503872 | tf_op jit(solution)/shard_map/pallas_call | solution.py:36
  109.6 1.2 %collective-permute-done.10 = bf16[32,896]{1,0:T(8,128)(2,1)S(1)} collective-permute-done((bf16[32,896]{1,0:T(8,128)(2,1)S(1)}, bf16[32,896]{1,0:T(8,128)(2,1)S(1)}, u32[]{:S(2)}, u32[]{:S(2)}) %collective-permute-start.10) | collective-permute-done | bytes 57376 | tf_op jit(solution)/shard_map/ppermute | solution.py:230
  110.8 0.6 add_convert_fusion
  (28 shorter events, 0.1 us)
Async XLA Ops:
  1.3 0.9 copy-start.17
  2.2 0.7 copy-start.18
  3.2 3.2 %collective-permute-start = (bf16[128,384]{1,0:T(8,128)(2,1)S(1)}, bf16[128,384]{1,0:T(8,128)(2,1)S(1)}, u32[]{:S(2)}, u32[]{:S(2)}) collective-permute-start(bf16[128,384]{1,0:T(8,128)(2,1)S(1)} %get-tuple-element.23), channel_id=1, source_target_pairs={{0,8},{8,0},{1,9},{9,1},{2,10},{10,2},{3,11},{11,3},{4,12},{12,4},... | collective-permute-start | bytes 294920 | tf_op jit(solution)/shard_map/ppermute | solution.py:207
  6.4 11.6 %collective-permute-start.1 = (bf16[256,384]{1,0:T(8,128)(2,1)S(1)}, bf16[256,384]{1,0:T(8,128)(2,1)S(1)}, u32[]{:S(2)}, u32[]{:S(2)}) collective-permute-start(bf16[256,384]{1,0:T(8,128)(2,1)S(1)} %shard_map.78.piece_ref.refs_0_), channel_id=1, source_target_pairs={{2,0},{4,2},{6,4},{7,6},{5,7},{3,5},{1,3},{0,1},{10,8},{12,10},{14... | collective-permute-start | bytes 589832 | tf_op jit(solution)/shard_map/ppermute | solution.py:217
  13.3 31.8 %collective-permute-start.8 = (bf16[384,896]{1,0:T(8,128)(2,1)}, bf16[384,896]{1,0:T(8,128)(2,1)S(1)}, u32[]{:S(2)}, u32[]{:S(2)}) collective-permute-start(bf16[384,896]{1,0:T(8,128)(2,1)} %hid_ref.15), channel_id=1, source_target_pairs={{0,8},{8,0},{1,9},{9,1},{2,10},{10,2},{3,11},{11,3},{4,12},{12,4},... | collective-permute-start | bytes 2064392 | tf_op jit(solution)/shard_map/ppermute | solution.py:207
  15.2 10.6 %collective-permute-start.2 = (bf16[256,384]{1,0:T(8,128)(2,1)S(1)}, bf16[256,384]{1,0:T(8,128)(2,1)S(1)}, u32[]{:S(2)}, u32[]{:S(2)}) collective-permute-start(bf16[256,384]{1,0:T(8,128)(2,1)S(1)} %shard_map.78.piece_ref.refs_0_), channel_id=1, source_target_pairs={{0,2},{2,4},{4,6},{6,7},{7,5},{5,3},{3,1},{1,0},{8,10},{10,12},{12... | collective-permute-start | bytes 589832 | tf_op jit(solution)/shard_map/ppermute | solution.py:218
  18.0 31.9 %copy-start.3 = (bf16[256,384]{1,0:T(8,128)(2,1)}, bf16[256,384]{1,0:T(8,128)(2,1)S(1)}, u32[]{:S(2)}) copy-start(bf16[256,384]{1,0:T(8,128)(2,1)S(1)} %collective-permute-done.1.piece_ref.refs_1_) | copy-start | bytes 589828
  18.0 13.7 %collective-permute-start.3 = (bf16[256,384]{1,0:T(8,128)(2,1)S(1)}, bf16[256,384]{1,0:T(8,128)(2,1)S(1)}, u32[]{:S(2)}, u32[]{:S(2)}) collective-permute-start(bf16[256,384]{1,0:T(8,128)(2,1)S(1)} %collective-permute-done.1.piece_ref.refs_1_), channel_id=1, source_target_pairs={{2,0},{4,2},{6,4},{7,6},{5,7},{3,5},{1,3},{0,1},{10,8},{12,10},{14... | collective-permute-start | bytes 589832 | tf_op jit(solution)/shard_map/ppermute | solution.py:217
  25.8 24.1 %copy-start.5 = (bf16[256,384]{1,0:T(8,128)(2,1)}, bf16[256,384]{1,0:T(8,128)(2,1)S(1)}, u32[]{:S(2)}) copy-start(bf16[256,384]{1,0:T(8,128)(2,1)S(1)} %collective-permute-done.2.piece_ref.refs_2_) | copy-start | bytes 589828
  25.8 9.6 %collective-permute-start.4 = (bf16[256,384]{1,0:T(8,128)(2,1)S(1)}, bf16[256,384]{1,0:T(8,128)(2,1)S(1)}, u32[]{:S(2)}, u32[]{:S(2)}) collective-permute-start(bf16[256,384]{1,0:T(8,128)(2,1)S(1)} %collective-permute-done.2.piece_ref.refs_2_), channel_id=1, source_target_pairs={{0,2},{2,4},{4,6},{6,7},{7,5},{5,3},{3,1},{1,0},{8,10},{10,12},{12... | collective-permute-start | bytes 589832 | tf_op jit(solution)/shard_map/ppermute | solution.py:218
  31.7 20.1 %copy-start.7 = (bf16[256,384]{1,0:T(8,128)(2,1)}, bf16[256,384]{1,0:T(8,128)(2,1)S(1)}, u32[]{:S(2)}) copy-start(bf16[256,384]{1,0:T(8,128)(2,1)S(1)} %collective-permute-done.3.piece_ref.refs_3_) | copy-start | bytes 589828
  31.7 10.8 %collective-permute-start.5 = (bf16[256,384]{1,0:T(8,128)(2,1)S(1)}, bf16[256,384]{1,0:T(8,128)(2,1)S(1)}, u32[]{:S(2)}, u32[]{:S(2)}) collective-permute-start(bf16[256,384]{1,0:T(8,128)(2,1)S(1)} %collective-permute-done.3.piece_ref.refs_3_), channel_id=1, source_target_pairs={{2,0},{4,2},{6,4},{7,6},{5,7},{3,5},{1,3},{0,1},{10,8},{12,10},{14... | collective-permute-start | bytes 589832 | tf_op jit(solution)/shard_map/ppermute | solution.py:217
  35.5 18.1 %copy-start.9 = (bf16[256,384]{1,0:T(8,128)(2,1)}, bf16[256,384]{1,0:T(8,128)(2,1)S(1)}, u32[]{:S(2)}) copy-start(bf16[256,384]{1,0:T(8,128)(2,1)S(1)} %collective-permute-done.4.piece_ref.refs_4_) | copy-start | bytes 589828
  35.5 21.8 %collective-permute-start.6 = (bf16[256,384]{1,0:T(8,128)(2,1)S(1)}, bf16[256,384]{1,0:T(8,128)(2,1)S(1)}, u32[]{:S(2)}, u32[]{:S(2)}) collective-permute-start(bf16[256,384]{1,0:T(8,128)(2,1)S(1)} %collective-permute-done.4.piece_ref.refs_4_), channel_id=1, source_target_pairs={{0,2},{2,4},{4,6},{6,7},{7,5},{5,3},{3,1},{1,0},{8,10},{10,12},{12... | collective-permute-start | bytes 589832 | tf_op jit(solution)/shard_map/ppermute | solution.py:218
  42.5 13.0 %copy-start.11 = (bf16[256,384]{1,0:T(8,128)(2,1)}, bf16[256,384]{1,0:T(8,128)(2,1)S(1)}, u32[]{:S(2)}) copy-start(bf16[256,384]{1,0:T(8,128)(2,1)S(1)} %collective-permute-done.5.piece_ref.refs_5_) | copy-start | bytes 589828
  42.5 16.7 %collective-permute-start.7 = (bf16[256,384]{1,0:T(8,128)(2,1)S(1)}, bf16[256,384]{1,0:T(8,128)(2,1)S(1)}, u32[]{:S(2)}, u32[]{:S(2)}) collective-permute-start(bf16[256,384]{1,0:T(8,128)(2,1)S(1)} %collective-permute-done.5.piece_ref.refs_5_), channel_id=1, source_target_pairs={{2,0},{4,2},{6,4},{7,6},{5,7},{3,5},{1,3},{0,1},{10,8},{12,10},{14... | collective-permute-start | bytes 589832 | tf_op jit(solution)/shard_map/ppermute | solution.py:220
  45.1 1.1 copy-start
  46.2 1.8 %copy-start.1 = (bf16[384,896]{1,0:T(8,128)(2,1)S(1)}, bf16[384,896]{1,0:T(8,128)(2,1)}, u32[]{:S(2)}) copy-start(bf16[384,896]{1,0:T(8,128)(2,1)} %hid_ref.15) | copy-start | bytes 2064388
  57.3 1.8 %copy-start.13 = (bf16[256,384]{1,0:T(8,128)(2,1)}, bf16[256,384]{1,0:T(8,128)(2,1)S(1)}, u32[]{:S(2)}) copy-start(bf16[256,384]{1,0:T(8,128)(2,1)S(1)} %collective-permute-done.6.piece_ref.refs_6_) | copy-start | bytes 589828
  59.2 1.8 %copy-start.15 = (bf16[256,384]{1,0:T(8,128)(2,1)}, bf16[256,384]{1,0:T(8,128)(2,1)S(1)}, u32[]{:S(2)}) copy-start(bf16[256,384]{1,0:T(8,128)(2,1)S(1)} %collective-permute-done.7.piece_ref.refs_7_) | copy-start | bytes 589828
  61.0 34.5 %all-to-all-start = ((bf16[16,64,896]{2,1,0:T(8,128)(2,1)}), bf16[16,64,896]{2,1,0:T(8,128)(2,1)S(1)}, u32[]{:S(2)}, u32[]{:S(2)}) async-start(bf16[16,64,896]{2,1,0:T(8,128)(2,1)} %bitcast.3), calls=%async_computation | async-start | bytes 3670016 | tf_op jit(solution)/shard_map/all_to_all | solution.py:226
  68.8 34.7 %copy-start.4 = (bf16[256,384]{1,0:T(8,128)(2,1)S(1)}, bf16[256,384]{1,0:T(8,128)(2,1)}, u32[]{:S(2)}) copy-start(bf16[256,384]{1,0:T(8,128)(2,1)} %copy-done.3) | copy-start | bytes 589828
  68.8 34.7 %copy-start.6 = (bf16[256,384]{1,0:T(8,128)(2,1)S(1)}, bf16[256,384]{1,0:T(8,128)(2,1)}, u32[]{:S(2)}) copy-start(bf16[256,384]{1,0:T(8,128)(2,1)} %copy-done.5) | copy-start | bytes 589828
  68.8 34.7 %copy-start.8 = (bf16[256,384]{1,0:T(8,128)(2,1)S(1)}, bf16[256,384]{1,0:T(8,128)(2,1)}, u32[]{:S(2)}) copy-start(bf16[256,384]{1,0:T(8,128)(2,1)} %copy-done.7) | copy-start | bytes 589828
  68.8 34.7 %collective-permute-start.9 = (bf16[1024,384]{1,0:T(8,128)(2,1)S(1)}, bf16[1024,384]{1,0:T(8,128)(2,1)}, u32[]{:S(2)}, u32[]{:S(2)}) collective-permute-start(bf16[1024,384]{1,0:T(8,128)(2,1)S(1)} %get-tuple-element.38), channel_id=1, source_target_pairs={{0,8},{8,0},{1,9},{9,1},{2,10},{10,2},{3,11},{11,3},{4,12},{12,4},... | collective-permute-start | bytes 2359304 | tf_op jit(solution)/shard_map/ppermute | solution.py:207
  95.6 8.0 %copy-start.10 = (bf16[256,384]{1,0:T(8,128)(2,1)S(1)}, bf16[256,384]{1,0:T(8,128)(2,1)}, u32[]{:S(2)}) copy-start(bf16[256,384]{1,0:T(8,128)(2,1)} %copy-done.9) | copy-start | bytes 589828
  95.6 8.0 %copy-start.12 = (bf16[256,384]{1,0:T(8,128)(2,1)S(1)}, bf16[256,384]{1,0:T(8,128)(2,1)}, u32[]{:S(2)}) copy-start(bf16[256,384]{1,0:T(8,128)(2,1)} %copy-done.11) | copy-start | bytes 589828
  95.6 8.0 %copy-start.14 = (bf16[256,384]{1,0:T(8,128)(2,1)S(1)}, bf16[256,384]{1,0:T(8,128)(2,1)}, u32[]{:S(2)}) copy-start(bf16[256,384]{1,0:T(8,128)(2,1)} %copy-done.13) | copy-start | bytes 589828
  95.6 8.0 %copy-start.16 = (bf16[256,384]{1,0:T(8,128)(2,1)S(1)}, bf16[256,384]{1,0:T(8,128)(2,1)}, u32[]{:S(2)}) copy-start(bf16[256,384]{1,0:T(8,128)(2,1)} %copy-done.15) | copy-start | bytes 589828
  95.8 15.0 %collective-permute-start.10 = (bf16[32,896]{1,0:T(8,128)(2,1)S(1)}, bf16[32,896]{1,0:T(8,128)(2,1)S(1)}, u32[]{:S(2)}, u32[]{:S(2)}) collective-permute-start(bf16[32,896]{1,0:T(8,128)(2,1)S(1)} %get-tuple-element.41), channel_id=1, source_target_pairs={{0,64},{64,0},{1,65},{65,1},{2,66},{66,2},{3,67},{67,3},{4,68},{68... | collective-permute-start | bytes 172040 | tf_op jit(solution)/shard_map/ppermute | solution.py:230
  103.6 2.0 %copy-start.2 = (bf16[2048,896]{1,0:T(8,128)(2,1)S(1)}, bf16[2048,896]{1,0:T(8,128)(2,1)}, u32[]{:S(2)}) copy-start(bf16[2048,896]{1,0:T(8,128)(2,1)} %refs_9_.1) | copy-start | bytes 11010052

commit v6 on v5

--- a/solution.py
+++ b/solution.py
@@ -195,6 +195,17 @@
     )
 
 
+def finish_kernel(keep_ref, far_ref, out_ref):
+    out_ref[...] = (keep_ref[...] + far_ref[...].astype(jnp.float32)).astype(out_ref.dtype)
+
+
+def finish(keep, far):
+    return kernel_call(
+        finish_kernel, (), (keep, far), jax.ShapeDtypeStruct(far.shape, jnp.bfloat16), [],
+        keep.size, 8 * keep.size, 4,
+    )
+
+
 def body(grad_out, gate_prob, hidden, w_down, slot_counts):
     _, units = hidden.shape
     order = lax.dynamic_index_in_dim(
@@ -228,7 +239,7 @@
     grad_hidden = hidden_grads(order, core, pieces, theirs, w_down)
     keep, cross = plane_sums(zh, parts)
     far = lax.ppermute(cross, "zh", [(0, 1), (1, 0)])
-    return grad_hidden, (keep + far.astype(jnp.float32)).astype(jnp.bfloat16)
+    return grad_hidden, finish(keep, far)
 
 
 def solution(mesh):

time: 112 us -> 112 us (level)
    pallas_call x4 -> x5, Pallas kernels: 4.51 us -> 5.14 us  [kernel_call(): pl.pallas_call(kernel, in_specs=[smem() for _ in scalars] + [vmem() for _...]
where the time goes in v6:
time: 112 us; the launch traced here: 111 us
  starting transfers between devices  46.1 us (41%)
  waiting for transfers between devices  38.3 us (34%)
  Pallas kernels  19.8 us (18%)
  local copies, waits for them, and re-layouts  5.49 us (5%)
  between operations  1.67 us (1%)
    all_to_all x1, waiting for transfers between devices, body(): lax.all_to_all(term.reshape(16, 64, units), ('x', 'y'), 0, 0, tiled=True)  24.7 us
    pallas_call x8, Pallas kernels, add_term(): pl.pallas_call(functools.partial(term_kernel, k), in_specs=[smem(), vmem(...  14.6 us
    ppermute x3, starting transfers between devices, body(): forward = lax.ppermute(forward, 'node', CW)  14 us
    ppermute x3, starting transfers between devices, body(): backward = lax.ppermute(backward, 'node', CCW)  9 us
    all_to_all x1, starting transfers between devices, body(): lax.all_to_all(term.reshape(16, 64, units), ('x', 'y'), 0, 0, tiled=True)  7.71 us
    ppermute x1, starting transfers between devices, body(): far = lax.ppermute(cross, 'zh', [(0, 1), (1, 0)])  7.66 us
    ppermute x3, waiting for transfers between devices, body(): forward = lax.ppermute(forward, 'node', CW)  6.59 us
    ppermute x3, starting transfers between devices, swap(): return lax.ppermute(value, 'core', [(0, 1), (1, 0)])  5.9 us
  transfers between devices with their start and end apart: 12, of which 8 were waited for; matrix products, arithmetic and copies ran while one was open for 1% of the time, Pallas kernels for 15%

profile of v6, /device:TPU:64, one launch (start us, length us, event | category | flops | bytes accessed | tf_op | source)
XLA Modules:
  0.0 111.4 jit_solution(5075939802962738744)
XLA Ops:
  1.3 0.0 copy-start.17
  1.3 0.9 copy-done.17
  2.2 0.7 copy-done.18
  2.9 0.3 shard_map.77
  3.2 1.9 %collective-permute-start = (bf16[128,384]{1,0:T(8,128)(2,1)S(1)}, bf16[128,384]{1,0:T(8,128)(2,1)S(1)}, u32[]{:S(2)}, u32[]{:S(2)}) collective-permute-start(bf16[128,384]{1,0:T(8,128)(2,1)S(1)} %get-tuple-element.23), channel_id=1, source_target_pairs={{0,8},{8,0},{1,9},{9,1},{2,10},{10,2},{3,11},{11,3},{4,12},{12,4},... | collective-permute-start | bytes 294920 | tf_op jit(solution)/shard_map/ppermute | solution.py:218
  5.1 1.3 %collective-permute-done.theirs_ref = bf16[128,384]{1,0:T(8,128)(2,1)S(1)} collective-permute-done((bf16[128,384]{1,0:T(8,128)(2,1)S(1)}, bf16[128,384]{1,0:T(8,128)(2,1)S(1)}, u32[]{:S(2)}, u32[]{:S(2)}) %collective-permute-start) | collective-permute-done | bytes 98336 | tf_op jit(solution)/shard_map/ppermute | solution.py:218
  6.4 6.9 %collective-permute-start.1 = (bf16[256,384]{1,0:T(8,128)(2,1)S(1)}, bf16[256,384]{1,0:T(8,128)(2,1)S(1)}, u32[]{:S(2)}, u32[]{:S(2)}) collective-permute-start(bf16[256,384]{1,0:T(8,128)(2,1)S(1)} %shard_map.78.piece_ref.refs_0_), channel_id=1, source_target_pairs={{2,0},{4,2},{6,4},{7,6},{5,7},{3,5},{1,3},{0,1},{10,8},{12,10},{14... | collective-permute-start | bytes 589832 | tf_op jit(solution)/shard_map/ppermute | solution.py:228
  13.3 1.9 %collective-permute-start.8 = (bf16[384,896]{1,0:T(8,128)(2,1)}, bf16[384,896]{1,0:T(8,128)(2,1)S(1)}, u32[]{:S(2)}, u32[]{:S(2)}) collective-permute-start(bf16[384,896]{1,0:T(8,128)(2,1)} %hid_ref.15), channel_id=1, source_target_pairs={{0,8},{8,0},{1,9},{9,1},{2,10},{10,2},{3,11},{11,3},{4,12},{12,4},... | collective-permute-start | bytes 2064392 | tf_op jit(solution)/shard_map/ppermute | solution.py:218
  15.2 1.9 %collective-permute-start.2 = (bf16[256,384]{1,0:T(8,128)(2,1)S(1)}, bf16[256,384]{1,0:T(8,128)(2,1)S(1)}, u32[]{:S(2)}, u32[]{:S(2)}) collective-permute-start(bf16[256,384]{1,0:T(8,128)(2,1)S(1)} %shard_map.78.piece_ref.refs_0_), channel_id=1, source_target_pairs={{0,2},{2,4},{4,6},{6,7},{7,5},{5,3},{3,1},{1,0},{8,10},{10,12},{12... | collective-permute-start | bytes 589832 | tf_op jit(solution)/shard_map/ppermute | solution.py:229
  17.1 0.8 collective-permute-done.1.piece_ref.refs_1_
  18.0 5.1 %collective-permute-start.3 = (bf16[256,384]{1,0:T(8,128)(2,1)S(1)}, bf16[256,384]{1,0:T(8,128)(2,1)S(1)}, u32[]{:S(2)}, u32[]{:S(2)}) collective-permute-start(bf16[256,384]{1,0:T(8,128)(2,1)S(1)} %collective-permute-done.1.piece_ref.refs_1_), channel_id=1, source_target_pairs={{2,0},{4,2},{6,4},{7,6},{5,7},{3,5},{1,3},{0,1},{10,8},{12,10},{14... | collective-permute-start | bytes 589832 | tf_op jit(solution)/shard_map/ppermute | solution.py:228
  23.1 2.7 %collective-permute-done.2.piece_ref.refs_2_ = bf16[256,384]{1,0:T(8,128)(2,1)S(1)} collective-permute-done((bf16[256,384]{1,0:T(8,128)(2,1)S(1)}, bf16[256,384]{1,0:T(8,128)(2,1)S(1)}, u32[]{:S(2)}, u32[]{:S(2)}) %collective-permute-start.2) | collective-permute-done | bytes 196640 | tf_op jit(solution)/shard_map/ppermute | solution.py:229
  25.8 2.9 %collective-permute-start.4 = (bf16[256,384]{1,0:T(8,128)(2,1)S(1)}, bf16[256,384]{1,0:T(8,128)(2,1)S(1)}, u32[]{:S(2)}, u32[]{:S(2)}) collective-permute-start(bf16[256,384]{1,0:T(8,128)(2,1)S(1)} %collective-permute-done.2.piece_ref.refs_2_), channel_id=1, source_target_pairs={{0,2},{2,4},{4,6},{6,7},{7,5},{5,3},{3,1},{1,0},{8,10},{10,12},{12... | collective-permute-start | bytes 589832 | tf_op jit(solution)/shard_map/ppermute | solution.py:229
  28.7 2.9 %collective-permute-done.3.piece_ref.refs_3_ = bf16[256,384]{1,0:T(8,128)(2,1)S(1)} collective-permute-done((bf16[256,384]{1,0:T(8,128)(2,1)S(1)}, bf16[256,384]{1,0:T(8,128)(2,1)S(1)}, u32[]{:S(2)}, u32[]{:S(2)}) %collective-permute-start.3) | collective-permute-done | bytes 196640 | tf_op jit(solution)/shard_map/ppermute | solution.py:228
  31.7 1.9 %collective-permute-start.5 = (bf16[256,384]{1,0:T(8,128)(2,1)S(1)}, bf16[256,384]{1,0:T(8,128)(2,1)S(1)}, u32[]{:S(2)}, u32[]{:S(2)}) collective-permute-start(bf16[256,384]{1,0:T(8,128)(2,1)S(1)} %collective-permute-done.3.piece_ref.refs_3_), channel_id=1, source_target_pairs={{2,0},{4,2},{6,4},{7,6},{5,7},{3,5},{1,3},{0,1},{10,8},{12,10},{14... | collective-permute-start | bytes 589832 | tf_op jit(solution)/shard_map/ppermute | solution.py:228
  33.6 1.9 %collective-permute-done.4.piece_ref.refs_4_ = bf16[256,384]{1,0:T(8,128)(2,1)S(1)} collective-permute-done((bf16[256,384]{1,0:T(8,128)(2,1)S(1)}, bf16[256,384]{1,0:T(8,128)(2,1)S(1)}, u32[]{:S(2)}, u32[]{:S(2)}) %collective-permute-start.4) | collective-permute-done | bytes 196640 | tf_op jit(solution)/shard_map/ppermute | solution.py:229
  35.5 4.2 %collective-permute-start.6 = (bf16[256,384]{1,0:T(8,128)(2,1)S(1)}, bf16[256,384]{1,0:T(8,128)(2,1)S(1)}, u32[]{:S(2)}, u32[]{:S(2)}) collective-permute-start(bf16[256,384]{1,0:T(8,128)(2,1)S(1)} %collective-permute-done.4.piece_ref.refs_4_), channel_id=1, source_target_pairs={{0,2},{2,4},{4,6},{6,7},{7,5},{5,3},{3,1},{1,0},{8,10},{10,12},{12... | collective-permute-start | bytes 589832 | tf_op jit(solution)/shard_map/ppermute | solution.py:229
  39.7 2.8 %collective-permute-done.5.piece_ref.refs_5_ = bf16[256,384]{1,0:T(8,128)(2,1)S(1)} collective-permute-done((bf16[256,384]{1,0:T(8,128)(2,1)S(1)}, bf16[256,384]{1,0:T(8,128)(2,1)S(1)}, u32[]{:S(2)}, u32[]{:S(2)}) %collective-permute-start.5) | collective-permute-done | bytes 196640 | tf_op jit(solution)/shard_map/ppermute | solution.py:228
  42.5 1.9 %collective-permute-start.7 = (bf16[256,384]{1,0:T(8,128)(2,1)S(1)}, bf16[256,384]{1,0:T(8,128)(2,1)S(1)}, u32[]{:S(2)}, u32[]{:S(2)}) collective-permute-start(bf16[256,384]{1,0:T(8,128)(2,1)S(1)} %collective-permute-done.5.piece_ref.refs_5_), channel_id=1, source_target_pairs={{2,0},{4,2},{6,4},{7,6},{5,7},{3,5},{1,3},{0,1},{10,8},{12,10},{14... | collective-permute-start | bytes 589832 | tf_op jit(solution)/shard_map/ppermute | solution.py:231
  44.4 0.7 dynamic-slice_bitcast_fusion.order_ref
  45.1 0.0 collective-permute-done.8.theirs_ref
  45.1 1.1 copy-done
  46.2 1.8 %add_term.8 = (bf16[1024,896]{1,0:T(8,128)(2,1)}, bf16[1024,384]{1,0:T(8,128)(2,1)S(1)}) custom-call(s32[8]{0:T(128)S(1)} %dynamic-slice_bitcast_fusion.order_ref, bf16[256,384]{1,0:T(8,128)(2,1)S(1)} %shard_map.78.piece_ref.refs_0_, bf16[384,896]{1,0:T(8,128)(2,1)S(1)} %copy-done, bf16[384,896]{1,0:T(8,128)(2,1)S(1)} %collective-permute-done.8.theirs_ref), custom_call_target="tpu_custom_call" | custom-call | flops 176160768 | bytes 1900544 | tf_op jit(solution)/shard_map/add_term/pallas_call | solution.py:118
  48.1 0.0 copy-done.1
  48.1 1.8 %add_term.9 = (bf16[1024,896]{1,0:T(8,128)(2,1)}, bf16[1024,384]{1,0:T(8,128)(2,1)S(1)}) custom-call(s32[8]{0:T(128)S(1)} %dynamic-slice_bitcast_fusion.order_ref, bf16[256,384]{1,0:T(8,128)(2,1)S(1)} %collective-permute-done.1.piece_ref.refs_1_, bf16[384,896]{1,0:T(8,128)(2,1)S(1)} %copy-done.1, ...), custom_call_target="tpu_custom_call", output_to_operand_aliasing={{0}: (4, {}), {1}: (5, {})} | custom-call | flops 176160768 | bytes 1900544 | tf_op jit(solution)/shard_map/add_term/pallas_call | solution.py:118
  49.9 1.8 %add_term.10 = (bf16[1024,896]{1,0:T(8,128)(2,1)}, bf16[1024,384]{1,0:T(8,128)(2,1)S(1)}) custom-call(s32[8]{0:T(128)S(1)} %dynamic-slice_bitcast_fusion.order_ref, bf16[256,384]{1,0:T(8,128)(2,1)S(1)} %collective-permute-done.2.piece_ref.refs_2_, bf16[384,896]{1,0:T(8,128)(2,1)S(1)} %copy-done.1, ...), custom_call_target="tpu_custom_call", output_to_operand_aliasing={{0}: (4, {}), {1}: (5, {})} | custom-call | flops 176160768 | bytes 1900544 | tf_op jit(solution)/shard_map/add_term/pallas_call | solution.py:118
  51.8 1.8 %add_term.11 = (bf16[1024,896]{1,0:T(8,128)(2,1)}, bf16[1024,384]{1,0:T(8,128)(2,1)S(1)}) custom-call(s32[8]{0:T(128)S(1)} %dynamic-slice_bitcast_fusion.order_ref, bf16[256,384]{1,0:T(8,128)(2,1)S(1)} %collective-permute-done.3.piece_ref.refs_3_, bf16[384,896]{1,0:T(8,128)(2,1)S(1)} %copy-done.1, ...), custom_call_target="tpu_custom_call", output_to_operand_aliasing={{0}: (4, {}), {1}: (5, {})} | custom-call | flops 176160768 | bytes 1900544 | tf_op jit(solution)/shard_map/add_term/pallas_call | solution.py:118
  53.6 1.8 %add_term.12 = (bf16[1024,896]{1,0:T(8,128)(2,1)}, bf16[1024,384]{1,0:T(8,128)(2,1)S(1)}) custom-call(s32[8]{0:T(128)S(1)} %dynamic-slice_bitcast_fusion.order_ref, bf16[256,384]{1,0:T(8,128)(2,1)S(1)} %collective-permute-done.4.piece_ref.refs_4_, bf16[384,896]{1,0:T(8,128)(2,1)S(1)} %copy-done.1, ...), custom_call_target="tpu_custom_call", output_to_operand_aliasing={{0}: (4, {}), {1}: (5, {})} | custom-call | flops 176160768 | bytes 1900544 | tf_op jit(solution)/shard_map/add_term/pallas_call | solution.py:118
  55.5 1.8 %add_term.13 = (bf16[1024,896]{1,0:T(8,128)(2,1)}, bf16[1024,384]{1,0:T(8,128)(2,1)S(1)}) custom-call(s32[8]{0:T(128)S(1)} %dynamic-slice_bitcast_fusion.order_ref, bf16[256,384]{1,0:T(8,128)(2,1)S(1)} %collective-permute-done.5.piece_ref.refs_5_, bf16[384,896]{1,0:T(8,128)(2,1)S(1)} %copy-done.1, ...), custom_call_target="tpu_custom_call", output_to_operand_aliasing={{0}: (4, {}), {1}: (5, {})} | custom-call | flops 176160768 | bytes 1900544 | tf_op jit(solution)/shard_map/add_term/pallas_call | solution.py:118
  57.3 0.0 collective-permute-done.6.piece_ref.refs_6_
  57.3 1.8 %add_term.14 = (bf16[1024,896]{1,0:T(8,128)(2,1)}, bf16[1024,384]{1,0:T(8,128)(2,1)S(1)}) custom-call(s32[8]{0:T(128)S(1)} %dynamic-slice_bitcast_fusion.order_ref, bf16[256,384]{1,0:T(8,128)(2,1)S(1)} %collective-permute-done.6.piece_ref.refs_6_, bf16[384,896]{1,0:T(8,128)(2,1)S(1)} %copy-done.1, ...), custom_call_target="tpu_custom_call", output_to_operand_aliasing={{0}: (4, {}), {1}: (5, {})} | custom-call | flops 176160768 | bytes 1900544 | tf_op jit(solution)/shard_map/add_term/pallas_call | solution.py:118
  59.2 0.0 collective-permute-done.7.piece_ref.refs_7_
  59.2 1.8 %add_term.15 = (bf16[1024,896]{1,0:T(8,128)(2,1)}, bf16[1024,384]{1,0:T(8,128)(2,1)S(1)}) custom-call(s32[8]{0:T(128)S(1)} %dynamic-slice_bitcast_fusion.order_ref, bf16[256,384]{1,0:T(8,128)(2,1)S(1)} %collective-permute-done.7.piece_ref.refs_7_, bf16[384,896]{1,0:T(8,128)(2,1)S(1)} %copy-done.1, ...), custom_call_target="tpu_custom_call", output_to_operand_aliasing={{0}: (4, {}), {1}: (5, {})} | custom-call | flops 176160768 | bytes 1900544 | tf_op jit(solution)/shard_map/add_term/pallas_call | solution.py:118
  61.0 0.0 copy-done.15
  61.0 7.7 %all-to-all-start = ((bf16[16,64,896]{2,1,0:T(8,128)(2,1)}), bf16[16,64,896]{2,1,0:T(8,128)(2,1)S(1)}, u32[]{:S(2)}, u32[]{:S(2)}) async-start(bf16[16,64,896]{2,1,0:T(8,128)(2,1)} %bitcast.3), calls=%async_computation | async-start | bytes 3670016 | tf_op jit(solution)/shard_map/all_to_all | solution.py:237
  68.8 0.0 copy-start.4
  68.8 0.0 copy-start.6
  68.8 0.0 copy-start.8
  68.8 2.1 %collective-permute-start.9 = (bf16[1024,384]{1,0:T(8,128)(2,1)S(1)}, bf16[1024,384]{1,0:T(8,128)(2,1)}, u32[]{:S(2)}, u32[]{:S(2)}) collective-permute-start(bf16[1024,384]{1,0:T(8,128)(2,1)S(1)} %get-tuple-element.38), channel_id=1, source_target_pairs={{0,8},{8,0},{1,9},{9,1},{2,10},{10,2},{3,11},{11,3},{4,12},{12,4},... | collective-permute-start | bytes 2359304 | tf_op jit(solution)/shard_map/ppermute | solution.py:218
  70.9 24.7 %all-to-all-done.in_ref = bf16[16,64,896]{2,1,0:T(8,128)(2,1)S(1)} async-done(((bf16[16,64,896]{2,1,0:T(8,128)(2,1)}), bf16[16,64,896]{2,1,0:T(8,128)(2,1)S(1)}, u32[]{:S(2)}, u32[]{:S(2)}) %all-to-all-start) | async-done | bytes 1835040 | tf_op jit(solution)/shard_map/all_to_all | solution.py:237
  95.6 0.2 shard_map.80
  95.8 7.7 %collective-permute-start.10 = (bf16[32,896]{1,0:T(8,128)(2,1)S(1)}, bf16[32,896]{1,0:T(8,128)(2,1)S(1)}, u32[]{:S(2)}, u32[]{:S(2)}) collective-permute-start(bf16[32,896]{1,0:T(8,128)(2,1)S(1)} %get-tuple-element.41), channel_id=1, source_target_pairs={{0,64},{64,0},{1,65},{65,1},{2,66},{66,2},{3,67},{67,3},{4,68},{68... | collective-permute-start | bytes 172040 | tf_op jit(solution)/shard_map/ppermute | solution.py:241
  103.5 0.0 collective-permute-done.9.refs_8_
  103.6 0.0 copy-start.2
  103.6 2.0 %copy-done.2 = bf16[2048,896]{1,0:T(8,128)(2,1)S(1)} copy-done((bf16[2048,896]{1,0:T(8,128)(2,1)S(1)}, bf16[2048,896]{1,0:T(8,128)(2,1)}, u32[]{:S(2)}) %copy-start.2) | copy-done | bytes 3670040
  105.6 4.0 %shard_map.79 = bf16[384,896]{1,0:T(8,128)(2,1)} custom-call(s32[8]{0:T(128)S(1)} %dynamic-slice_bitcast_fusion.order_ref, s32[1]{0:T(128)} %bitcast.1.core_ref, bf16[256,384]{1,0:T(8,128)(2,1)S(1)} %shard_map.78.piece_ref.refs_0_, bf16[256,384]{1,0:T(8,128)(2,1)S(1)} %copy-done.4, bf16[256,384]{1,0:T(8,128)(2,1)S(1)} %copy-done.6, ...), custom_call_target="tpu_custom_call" | custom-call | flops 1409286144 | bytes 7503872 | tf_op jit(solution)/shard_map/pallas_call | solution.py:36
  109.6 1.2 %collective-permute-done.10.far_ref = bf16[32,896]{1,0:T(8,128)(2,1)S(1)} collective-permute-done((bf16[32,896]{1,0:T(8,128)(2,1)S(1)}, bf16[32,896]{1,0:T(8,128)(2,1)S(1)}, u32[]{:S(2)}, u32[]{:S(2)}) %collective-permute-start.10) | collective-permute-done | bytes 57376 | tf_op jit(solution)/shard_map/ppermute | solution.py:241
  110.8 0.6 shard_map.81
  (28 shorter events, 0.1 us)
Async XLA Ops:
  1.3 0.9 copy-start.17
  2.2 0.7 copy-start.18
  3.2 3.2 %collective-permute-start = (bf16[128,384]{1,0:T(8,128)(2,1)S(1)}, bf16[128,384]{1,0:T(8,128)(2,1)S(1)}, u32[]{:S(2)}, u32[]{:S(2)}) collective-permute-start(bf16[128,384]{1,0:T(8,128)(2,1)S(1)} %get-tuple-element.23), channel_id=1, source_target_pairs={{0,8},{8,0},{1,9},{9,1},{2,10},{10,2},{3,11},{11,3},{4,12},{12,4},... | collective-permute-start | bytes 294920 | tf_op jit(solution)/shard_map/ppermute | solution.py:218
  6.4 11.6 %collective-permute-start.1 = (bf16[256,384]{1,0:T(8,128)(2,1)S(1)}, bf16[256,384]{1,0:T(8,128)(2,1)S(1)}, u32[]{:S(2)}, u32[]{:S(2)}) collective-permute-start(bf16[256,384]{1,0:T(8,128)(2,1)S(1)} %shard_map.78.piece_ref.refs_0_), channel_id=1, source_target_pairs={{2,0},{4,2},{6,4},{7,6},{5,7},{3,5},{1,3},{0,1},{10,8},{12,10},{14... | collective-permute-start | bytes 589832 | tf_op jit(solution)/shard_map/ppermute | solution.py:228
  13.3 31.8 %collective-permute-start.8 = (bf16[384,896]{1,0:T(8,128)(2,1)}, bf16[384,896]{1,0:T(8,128)(2,1)S(1)}, u32[]{:S(2)}, u32[]{:S(2)}) collective-permute-start(bf16[384,896]{1,0:T(8,128)(2,1)} %hid_ref.15), channel_id=1, source_target_pairs={{0,8},{8,0},{1,9},{9,1},{2,10},{10,2},{3,11},{11,3},{4,12},{12,4},... | collective-permute-start | bytes 2064392 | tf_op jit(solution)/shard_map/ppermute | solution.py:218
  15.2 10.6 %collective-permute-start.2 = (bf16[256,384]{1,0:T(8,128)(2,1)S(1)}, bf16[256,384]{1,0:T(8,128)(2,1)S(1)}, u32[]{:S(2)}, u32[]{:S(2)}) collective-permute-start(bf16[256,384]{1,0:T(8,128)(2,1)S(1)} %shard_map.78.piece_ref.refs_0_), channel_id=1, source_target_pairs={{0,2},{2,4},{4,6},{6,7},{7,5},{5,3},{3,1},{1,0},{8,10},{10,12},{12... | collective-permute-start | bytes 589832 | tf_op jit(solution)/shard_map/ppermute | solution.py:229
  18.0 31.9 %copy-start.3 = (bf16[256,384]{1,0:T(8,128)(2,1)}, bf16[256,384]{1,0:T(8,128)(2,1)S(1)}, u32[]{:S(2)}) copy-start(bf16[256,384]{1,0:T(8,128)(2,1)S(1)} %collective-permute-done.1.piece_ref.refs_1_) | copy-start | bytes 589828
  18.0 13.7 %collective-permute-start.3 = (bf16[256,384]{1,0:T(8,128)(2,1)S(1)}, bf16[256,384]{1,0:T(8,128)(2,1)S(1)}, u32[]{:S(2)}, u32[]{:S(2)}) collective-permute-start(bf16[256,384]{1,0:T(8,128)(2,1)S(1)} %collective-permute-done.1.piece_ref.refs_1_), channel_id=1, source_target_pairs={{2,0},{4,2},{6,4},{7,6},{5,7},{3,5},{1,3},{0,1},{10,8},{12,10},{14... | collective-permute-start | bytes 589832 | tf_op jit(solution)/shard_map/ppermute | solution.py:228
  25.8 24.1 %copy-start.5 = (bf16[256,384]{1,0:T(8,128)(2,1)}, bf16[256,384]{1,0:T(8,128)(2,1)S(1)}, u32[]{:S(2)}) copy-start(bf16[256,384]{1,0:T(8,128)(2,1)S(1)} %collective-permute-done.2.piece_ref.refs_2_) | copy-start | bytes 589828
  25.8 9.6 %collective-permute-start.4 = (bf16[256,384]{1,0:T(8,128)(2,1)S(1)}, bf16[256,384]{1,0:T(8,128)(2,1)S(1)}, u32[]{:S(2)}, u32[]{:S(2)}) collective-permute-start(bf16[256,384]{1,0:T(8,128)(2,1)S(1)} %collective-permute-done.2.piece_ref.refs_2_), channel_id=1, source_target_pairs={{0,2},{2,4},{4,6},{6,7},{7,5},{5,3},{3,1},{1,0},{8,10},{10,12},{12... | collective-permute-start | bytes 589832 | tf_op jit(solution)/shard_map/ppermute | solution.py:229
  31.7 20.1 %copy-start.7 = (bf16[256,384]{1,0:T(8,128)(2,1)}, bf16[256,384]{1,0:T(8,128)(2,1)S(1)}, u32[]{:S(2)}) copy-start(bf16[256,384]{1,0:T(8,128)(2,1)S(1)} %collective-permute-done.3.piece_ref.refs_3_) | copy-start | bytes 589828
  31.7 10.8 %collective-permute-start.5 = (bf16[256,384]{1,0:T(8,128)(2,1)S(1)}, bf16[256,384]{1,0:T(8,128)(2,1)S(1)}, u32[]{:S(2)}, u32[]{:S(2)}) collective-permute-start(bf16[256,384]{1,0:T(8,128)(2,1)S(1)} %collective-permute-done.3.piece_ref.refs_3_), channel_id=1, source_target_pairs={{2,0},{4,2},{6,4},{7,6},{5,7},{3,5},{1,3},{0,1},{10,8},{12,10},{14... | collective-permute-start | bytes 589832 | tf_op jit(solution)/shard_map/ppermute | solution.py:228
  35.5 18.1 %copy-start.9 = (bf16[256,384]{1,0:T(8,128)(2,1)}, bf16[256,384]{1,0:T(8,128)(2,1)S(1)}, u32[]{:S(2)}) copy-start(bf16[256,384]{1,0:T(8,128)(2,1)S(1)} %collective-permute-done.4.piece_ref.refs_4_) | copy-start | bytes 589828
  35.5 21.8 %collective-permute-start.6 = (bf16[256,384]{1,0:T(8,128)(2,1)S(1)}, bf16[256,384]{1,0:T(8,128)(2,1)S(1)}, u32[]{:S(2)}, u32[]{:S(2)}) collective-permute-start(bf16[256,384]{1,0:T(8,128)(2,1)S(1)} %collective-permute-done.4.piece_ref.refs_4_), channel_id=1, source_target_pairs={{0,2},{2,4},{4,6},{6,7},{7,5},{5,3},{3,1},{1,0},{8,10},{10,12},{12... | collective-permute-start | bytes 589832 | tf_op jit(solution)/shard_map/ppermute | solution.py:229
  42.5 13.0 %copy-start.11 = (bf16[256,384]{1,0:T(8,128)(2,1)}, bf16[256,384]{1,0:T(8,128)(2,1)S(1)}, u32[]{:S(2)}) copy-start(bf16[256,384]{1,0:T(8,128)(2,1)S(1)} %collective-permute-done.5.piece_ref.refs_5_) | copy-start | bytes 589828
  42.5 16.7 %collective-permute-start.7 = (bf16[256,384]{1,0:T(8,128)(2,1)S(1)}, bf16[256,384]{1,0:T(8,128)(2,1)S(1)}, u32[]{:S(2)}, u32[]{:S(2)}) collective-permute-start(bf16[256,384]{1,0:T(8,128)(2,1)S(1)} %collective-permute-done.5.piece_ref.refs_5_), channel_id=1, source_target_pairs={{2,0},{4,2},{6,4},{7,6},{5,7},{3,5},{1,3},{0,1},{10,8},{12,10},{14... | collective-permute-start | bytes 589832 | tf_op jit(solution)/shard_map/ppermute | solution.py:231
  45.1 1.1 copy-start
  46.2 1.8 %copy-start.1 = (bf16[384,896]{1,0:T(8,128)(2,1)S(1)}, bf16[384,896]{1,0:T(8,128)(2,1)}, u32[]{:S(2)}) copy-start(bf16[384,896]{1,0:T(8,128)(2,1)} %hid_ref.15) | copy-start | bytes 2064388
  57.3 1.8 %copy-start.13 = (bf16[256,384]{1,0:T(8,128)(2,1)}, bf16[256,384]{1,0:T(8,128)(2,1)S(1)}, u32[]{:S(2)}) copy-start(bf16[256,384]{1,0:T(8,128)(2,1)S(1)} %collective-permute-done.6.piece_ref.refs_6_) | copy-start | bytes 589828
  59.2 1.8 %copy-start.15 = (bf16[256,384]{1,0:T(8,128)(2,1)}, bf16[256,384]{1,0:T(8,128)(2,1)S(1)}, u32[]{:S(2)}) copy-start(bf16[256,384]{1,0:T(8,128)(2,1)S(1)} %collective-permute-done.7.piece_ref.refs_7_) | copy-start | bytes 589828
  61.0 34.5 %all-to-all-start = ((bf16[16,64,896]{2,1,0:T(8,128)(2,1)}), bf16[16,64,896]{2,1,0:T(8,128)(2,1)S(1)}, u32[]{:S(2)}, u32[]{:S(2)}) async-start(bf16[16,64,896]{2,1,0:T(8,128)(2,1)} %bitcast.3), calls=%async_computation | async-start | bytes 3670016 | tf_op jit(solution)/shard_map/all_to_all | solution.py:237
  68.8 34.7 %copy-start.4 = (bf16[256,384]{1,0:T(8,128)(2,1)S(1)}, bf16[256,384]{1,0:T(8,128)(2,1)}, u32[]{:S(2)}) copy-start(bf16[256,384]{1,0:T(8,128)(2,1)} %copy-done.3) | copy-start | bytes 589828
  68.8 34.7 %copy-start.6 = (bf16[256,384]{1,0:T(8,128)(2,1)S(1)}, bf16[256,384]{1,0:T(8,128)(2,1)}, u32[]{:S(2)}) copy-start(bf16[256,384]{1,0:T(8,128)(2,1)} %copy-done.5) | copy-start | bytes 589828
  68.8 34.7 %copy-start.8 = (bf16[256,384]{1,0:T(8,128)(2,1)S(1)}, bf16[256,384]{1,0:T(8,128)(2,1)}, u32[]{:S(2)}) copy-start(bf16[256,384]{1,0:T(8,128)(2,1)} %copy-done.7) | copy-start | bytes 589828
  68.8 34.7 %collective-permute-start.9 = (bf16[1024,384]{1,0:T(8,128)(2,1)S(1)}, bf16[1024,384]{1,0:T(8,128)(2,1)}, u32[]{:S(2)}, u32[]{:S(2)}) collective-permute-start(bf16[1024,384]{1,0:T(8,128)(2,1)S(1)} %get-tuple-element.38), channel_id=1, source_target_pairs={{0,8},{8,0},{1,9},{9,1},{2,10},{10,2},{3,11},{11,3},{4,12},{12,4},... | collective-permute-start | bytes 2359304 | tf_op jit(solution)/shard_map/ppermute | solution.py:218
  95.6 8.0 %copy-start.10 = (bf16[256,384]{1,0:T(8,128)(2,1)S(1)}, bf16[256,384]{1,0:T(8,128)(2,1)}, u32[]{:S(2)}) copy-start(bf16[256,384]{1,0:T(8,128)(2,1)} %copy-done.9) | copy-start | bytes 589828
  95.6 8.0 %copy-start.12 = (bf16[256,384]{1,0:T(8,128)(2,1)S(1)}, bf16[256,384]{1,0:T(8,128)(2,1)}, u32[]{:S(2)}) copy-start(bf16[256,384]{1,0:T(8,128)(2,1)} %copy-done.11) | copy-start | bytes 589828
  95.6 8.0 %copy-start.14 = (bf16[256,384]{1,0:T(8,128)(2,1)S(1)}, bf16[256,384]{1,0:T(8,128)(2,1)}, u32[]{:S(2)}) copy-start(bf16[256,384]{1,0:T(8,128)(2,1)} %copy-done.13) | copy-start | bytes 589828
  95.6 8.0 %copy-start.16 = (bf16[256,384]{1,0:T(8,128)(2,1)S(1)}, bf16[256,384]{1,0:T(8,128)(2,1)}, u32[]{:S(2)}) copy-start(bf16[256,384]{1,0:T(8,128)(2,1)} %copy-done.15) | copy-start | bytes 589828
  95.8 15.0 %collective-permute-start.10 = (bf16[32,896]{1,0:T(8,128)(2,1)S(1)}, bf16[32,896]{1,0:T(8,128)(2,1)S(1)}, u32[]{:S(2)}, u32[]{:S(2)}) collective-permute-start(bf16[32,896]{1,0:T(8,128)(2,1)S(1)} %get-tuple-element.41), channel_id=1, source_target_pairs={{0,64},{64,0},{1,65},{65,1},{2,66},{66,2},{3,67},{67,3},{4,68},{68... | collective-permute-start | bytes 172040 | tf_op jit(solution)/shard_map/ppermute | solution.py:241
  103.6 2.0 %copy-start.2 = (bf16[2048,896]{1,0:T(8,128)(2,1)S(1)}, bf16[2048,896]{1,0:T(8,128)(2,1)}, u32[]{:S(2)}) copy-start(bf16[2048,896]{1,0:T(8,128)(2,1)} %refs_9_.1) | copy-start | bytes 11010052
